TPU v7x, 128 devices: a whole 4x4x4 slice. The times are simulated.
128 devices in a mesh: row: 8 (over z_hi, x), col: 16 (over z_lo, y, core).
Axes of the slice: x: 4, y: 4, z: 4 (z_hi: 2, z_lo: 2; z = z_hi * 2 + z_lo), core: 2. Of those that a mesh axis runs over, the one named last changes fastest.
Arguments:
- diag_blocks: float32 [2, 512, 512], replicated, may hold values from -1 to 5, as said below
- pivot_flags: int32 [2, 512], replicated, may hold values 0 or 1
- panels: bfloat16 [2, 32768, 512], P(None, ('row', 'col')), may hold values from -3 to 3
- structure: int32 [2, 32768], P(None, ('row', 'col')), may hold values 0 or 1
- ancestor_inverse: bfloat16 [32768, 32768], P('row', 'col'), may hold values from -0.046875 to 0.046875
Outputs:
- inverse_panel: bfloat16 [2, 32768, 512], P(None, ('row', 'col'))
- inverse_diagonal: float32 [2, 512, 512], replicated
Inputs may be any that keep to these rules, and one draw needn't show every extreme that they name: Each diag_blocks[k] is symmetric, and its off-diagonal part is small enough that every eigenvalue of each shifted block is at least 0.8, so every shifted block is positive definite.
All inputs are finite; a program needn't handle non-finite values. No bound on the sum of `structure` on one device may be relied on, other than what follows from the above.
Results may differ from a plain program's by a relative error of at most 0.0051.
Values may be sent and summed in bfloat16 or wider, within the bound.
No kernel may reach another device: no remote copies, remote signals or barrier semaphores. Data moves between devices by JAX's collectives and lax.ppermute only.
A program may use at most 192 MiB of HBM per device.

v0:
```python
import jax
import jax.numpy as jnp
from jax import lax
from jax.sharding import PartitionSpec as P

HIGHEST_PRECISION = lax.Precision.HIGHEST
PERTURBATION = 1.0


def from_root(value, axis, source):
    kept = jnp.where(lax.axis_index(axis) == source, value, 0).astype(value.dtype)
    return lax.psum(kept, axis)


def factor_inverse(diagonal_block, flag_row):
    node_width = diagonal_block.shape[0]
    identity = jnp.eye(node_width, dtype=jnp.float32)
    shifted = diagonal_block + PERTURBATION * identity * flag_row.astype(jnp.float32)[None, :]
    factor_lower = jnp.linalg.cholesky(shifted)
    lower_inverse = jax.scipy.linalg.solve_triangular(factor_lower, identity, lower=True)
    return jnp.dot(lower_inverse.T, lower_inverse, precision=HIGHEST_PRECISION)


def normalize_panel(panel_rows, member_row, inverse):
    masked = panel_rows.astype(jnp.float32) * member_row.astype(jnp.float32)[:, None]
    return jnp.dot(masked, inverse, precision=HIGHEST_PRECISION).astype(jnp.bfloat16)


def exact_contract(left_rows, right_rows):
    dims = (((0,), (0,)), ((), ()))
    return lax.dot_general(
        left_rows.astype(jnp.float32),
        right_rows,
        dims,
        precision=HIGHEST_PRECISION,
        preferred_element_type=jnp.float32,
    )


def local(diag_blocks, pivot_flags, panels, structure, ancestor_inverse):
    node_count = diag_blocks.shape[0]
    node_width = diag_blocks.shape[2]
    inverses = [
        factor_inverse(diag_blocks[supernode], pivot_flags[supernode])
        for supernode in range(node_count)
    ]
    normed = [
        normalize_panel(panels[supernode], structure[supernode], inverses[supernode])
        for supernode in range(node_count)
    ]
    groups = jnp.concatenate(normed, axis=1)
    col_ratio = lax.axis_size("col") // lax.axis_size("row")
    col_index = lax.axis_index("col")
    own_rows = ancestor_inverse.shape[0] // lax.axis_size("col")
    panel_terms = []
    diagonal_terms = []
    row_block = lax.all_gather(groups, "col", axis=0, tiled=True)
    block_rows = row_block.shape[0] // col_ratio
    column_part = lax.dynamic_slice_in_dim(
        row_block, col_index % col_ratio * block_rows, block_rows, 0
    )
    column_block = from_root(column_part, "row", col_index // col_ratio)
    group_size = groups.shape[1] // node_width

    def product(offset, row_count, column_block=column_block):
        return jnp.dot(ancestor_inverse, column_block, preferred_element_type=jnp.float32)

    summed = lax.psum_scatter(
        product(jnp.int32(0), own_rows * lax.axis_size("col")),
        "col",
        scatter_dimension=0,
        tiled=True,
    )
    for member in range(group_size):
        lower_col = member * node_width
        diagonal_terms.append(
            exact_contract(
                groups[:, lower_col : lower_col + node_width],
                summed[:, lower_col : lower_col + node_width],
            )
        )
    for member in range(group_size):
        lower_col = member * node_width
        panel_terms.append(summed[:, lower_col : lower_col + node_width])
    totals = lax.psum(jnp.stack(diagonal_terms), ("row", "col"))
    inverse_diagonal = jnp.stack(inverses) + totals
    inverse_panel = (-jnp.stack(panel_terms)).astype(jnp.bfloat16)
    return (inverse_panel, inverse_diagonal)


def solution(mesh):
    in_specs = (P(), P(), P(None, ("row", "col"), None), P(None, ("row", "col")), P("row", "col"))
    out_specs = (P(None, ("row", "col"), None), P())
    return jax.shard_map(local, mesh=mesh, in_specs=in_specs, out_specs=out_specs, check_vma=False)
```

profile of v0, /device:TPU:1, one launch (start us, length us, event | category | flops | bytes accessed | tf_op | source)
XLA Modules:
  0.0 775.9 jit_solution(5468474773533071747)
XLA Ops:
  7.3 0.8 slice_convert_fusion.3
  8.1 0.8 slice_convert_fusion.1
  8.9 2.7 fusion.90
  11.9 1.6 copy.13
  13.5 1.1 bitcast_add_fusion.1
  14.6 2.5 copy.10
  17.1 1.5 fusion.17
  18.6 1.0 copy-done.2
  19.6 11.7 %cholesky.358 = f32[128,128]{1,0:T(8,128)S(1)} custom-call(f32[128,128]{1,0:T(8,128)S(1)} %cholesky.439), custom_call_target="Cholesky" | custom-call | tf_op jit(solution)/shard_map/jit(cholesky)/cholesky | solution.py:19
  31.3 9.8 %custom-call.31 = f32[1,128,128]{1,2,0:T(8,128)S(1)} custom-call(f32[1,128,128]{2,1,0:T(8,128)S(1)} %get-tuple-element.65), custom_call_target="InvertDiagBlocksLowerTriangular" | custom-call | tf_op jit(solution)/shard_map/jit(cholesky)/cholesky | solution.py:19
  41.3 1.2 constant_dynamic-update-slice_fusion.3
  42.5 1.3 convolution_subtract_fusion.6
  43.8 11.7 %cholesky.377 = f32[128,128]{1,0:T(8,128)S(1)} custom-call(f32[128,128]{1,0:T(8,128)S(1)} %cholesky.443), custom_call_target="Cholesky" | custom-call | tf_op jit(solution)/shard_map/jit(cholesky)/cholesky | solution.py:19
  55.6 10.2 %custom-call.32 = f32[1,128,128]{1,2,0:T(8,128)S(1)} custom-call(f32[1,128,128]{2,1,0:T(8,128)S(1)} %get-tuple-element.62), custom_call_target="InvertDiagBlocksLowerTriangular" | custom-call | tf_op jit(solution)/shard_map/jit(cholesky)/cholesky | solution.py:19
  66.1 1.3 convolution_subtract_fusion.8
  67.4 11.7 %cholesky.398 = f32[128,128]{1,0:T(8,128)S(1)} custom-call(f32[128,128]{1,0:T(8,128)S(1)} %cholesky.448), custom_call_target="Cholesky" | custom-call | tf_op jit(solution)/shard_map/jit(cholesky)/cholesky | solution.py:19
  79.1 0.7 compare_reduce_fusion.1
  79.8 9.8 %custom-call.33 = f32[1,128,128]{1,2,0:T(8,128)S(1)} custom-call(f32[1,128,128]{2,1,0:T(8,128)S(1)} %get-tuple-element.59), custom_call_target="InvertDiagBlocksLowerTriangular" | custom-call | tf_op jit(solution)/shard_map/jit(cholesky)/cholesky | solution.py:19
  89.9 1.2 convolution_subtract_fusion.10
  91.1 11.9 %cholesky.415 = f32[128,128]{1,0:T(8,128)S(1)} custom-call(f32[128,128]{1,0:T(8,128)S(1)} %convolution_subtract_fusion.10), custom_call_target="Cholesky" | custom-call | tf_op jit(solution)/shard_map/jit(cholesky)/cholesky | solution.py:19
  106.8 1.1 select_select_fusion
  108.0 11.7 %while.5 = (s32[]{:T(128)}, f32[512,512]{1,0:T(8,128)}, s32[4,2]{0,1:T(2,128)S(1)}, f32[4,128,128]{2,1,0:T(8,128)S(1)}, s32[]{:T(128)}) while((s32[]{:T(128)}, f32[512,512]{1,0:T(8,128)}, s32[4,2]{0,1:T(2,128)S(1)}, f32[4,128,128]{2,1,0:T(8,128)S(1)}, s32[]{:T(128)}) %tuple.61), condition=%wide.while_cond.clone, body=%wide.while_body.clone.sunk | while | flops 2 | bytes 131189 | solution.py:20
  108.7 2.2 bitcast_dynamic-update-slice_fusion.5
  111.6 2.2 bitcast_dynamic-update-slice_fusion.5
  114.5 2.2 bitcast_dynamic-update-slice_fusion.5
  117.5 2.2 bitcast_dynamic-update-slice_fusion.5
  119.7 39.3 %custom-call.34 = f32[4,128,128]{1,2,0:T(8,128)S(1)} custom-call(f32[4,128,128]{2,1,0:T(8,128)S(1)} %get-tuple-element.19), custom_call_target="InvertDiagBlocksLowerTriangular" | custom-call | tf_op jit(solution)/shard_map/jit(_solve_triangular)/triangular_solve | solution.py:20
  159.4 1.4 convolution_subtract_fusion.1
  161.3 1.9 convolution_subtract_fusion
  163.7 2.4 convolution_subtract_fusion.4
  166.5 2.9 fusion.8
  169.6 1.3 copy.8
  170.9 1.5 fusion.18
  172.4 11.7 %cholesky.286 = f32[128,128]{1,0:T(8,128)S(1)} custom-call(f32[128,128]{1,0:T(8,128)S(1)} %cholesky.426), custom_call_target="Cholesky" | custom-call | tf_op jit(solution)/shard_map/jit(cholesky)/cholesky | solution.py:19
  184.1 10.0 %custom-call.27 = f32[1,128,128]{1,2,0:T(8,128)S(1)} custom-call(f32[1,128,128]{2,1,0:T(8,128)S(1)} %get-tuple-element.55), custom_call_target="InvertDiagBlocksLowerTriangular" | custom-call | tf_op jit(solution)/shard_map/jit(cholesky)/cholesky | solution.py:19
  194.9 11.7 %cholesky.305 = f32[128,128]{1,0:T(8,128)S(1)} custom-call(f32[128,128]{1,0:T(8,128)S(1)} %cholesky.430), custom_call_target="Cholesky" | custom-call | tf_op jit(solution)/shard_map/jit(cholesky)/cholesky | solution.py:19
  206.7 9.8 %custom-call.28 = f32[1,128,128]{1,2,0:T(8,128)S(1)} custom-call(f32[1,128,128]{2,1,0:T(8,128)S(1)} %get-tuple-element.52), custom_call_target="InvertDiagBlocksLowerTriangular" | custom-call | tf_op jit(solution)/shard_map/jit(cholesky)/cholesky | solution.py:19
  217.2 11.7 %cholesky.326 = f32[128,128]{1,0:T(8,128)S(1)} custom-call(f32[128,128]{1,0:T(8,128)S(1)} %cholesky.435), custom_call_target="Cholesky" | custom-call | tf_op jit(solution)/shard_map/jit(cholesky)/cholesky | solution.py:19
  228.9 0.7 compare_reduce_fusion.5
  229.7 10.2 %custom-call.29 = f32[1,128,128]{1,2,0:T(8,128)S(1)} custom-call(f32[1,128,128]{2,1,0:T(8,128)S(1)} %get-tuple-element.49), custom_call_target="InvertDiagBlocksLowerTriangular" | custom-call | tf_op jit(solution)/shard_map/jit(cholesky)/cholesky | solution.py:19
  240.4 11.7 %cholesky.343 = f32[128,128]{1,0:T(8,128)S(1)} custom-call(f32[128,128]{1,0:T(8,128)S(1)} %convolution_subtract_fusion.11), custom_call_target="Cholesky" | custom-call | tf_op jit(solution)/shard_map/jit(cholesky)/cholesky | solution.py:19
  256.9 10.6 %while.4 = (s32[]{:T(128)}, f32[512,512]{1,0:T(8,128)S(1)}, s32[4,2]{0,1:T(2,128)S(1)}, f32[4,128,128]{2,1,0:T(8,128)}, s32[]{:T(128)}) while((s32[]{:T(128)}, f32[512,512]{1,0:T(8,128)S(1)}, s32[4,2]{0,1:T(2,128)S(1)}, f32[4,128,128]{2,1,0:T(8,128)}, s32[]{:T(128)}) %tuple.75), condition=%wide.while_cond, body=%wide.while_body.sunk | while | flops 2 | bytes 132205 | solution.py:20
  257.6 2.0 bitcast_dynamic-update-slice_fusion.4
  260.2 2.0 bitcast_dynamic-update-slice_fusion.4
  262.9 2.0 bitcast_dynamic-update-slice_fusion.4
  265.5 2.0 bitcast_dynamic-update-slice_fusion.4
  267.5 40.4 %custom-call.30 = f32[4,128,128]{1,2,0:T(8,128)S(1)} custom-call(f32[4,128,128]{2,1,0:T(8,128)} %get-tuple-element.18), custom_call_target="InvertDiagBlocksLowerTriangular" | custom-call | tf_op jit(solution)/shard_map/jit(_solve_triangular)/triangular_solve | solution.py:20
  309.3 1.0 convolution_subtract_fusion.2
  310.8 1.5 convolution_subtract_fusion.5
  312.7 1.9 fusion
  314.6 1.1 convolution_convert_fusion
  315.7 1.1 convolution_convert_fusion.1
  316.8 0.9 pad_maximum_fusion.1
  317.8 55.8 %all-gather.2.cloned.1.call-done = bf16[4096,1024]{1,0:T(8,128)(2,1)} async-done(((bf16[256,1024]{1,0:T(8,128)(2,1)}), bf16[4096,1024]{1,0:T(8,128)(2,1)}) %all-gather.2.cloned.1.call-update) | async-done | bytes 8388624 | tf_op jit(solution)/shard_map/all_gather | solution.py:57
  373.6 5.4 dynamic-slice_select_fusion
  379.0 110.3 %all-reduce.4.cloned.1.call-done = bf16[2048,1024]{1,0:T(8,128)(2,1)} async-done(((bf16[2048,1024]{1,0:T(8,128)(2,1)}), bf16[2048,1024]{1,0:T(8,128)(2,1)}) %all-reduce.4.cloned.1.call-update) | async-done | bytes 4194320 | tf_op jit(solution)/shard_map/psum | solution.py:12
  489.3 23.8 %convolution_bitcast_fusion = f32[4096,1024]{0,1:T(8,128)} fusion(bf16[2048,1024]{1,0:T(8,128)(2,1)} %all-reduce.4.cloned.1.call-done, bf16[4096,2048]{1,0:T(8,128)(2,1)} %param.12), kind=kOutput, calls=%fused_computation.4 | convolution fusion | flops 17179869184 | bytes 37748736 | tf_op jit(solution)/shard_map/dot_general | solution.py:66
  513.2 95.7 %reduce-scatter.2.cloned.1.call-done = f32[256,1024]{0,1:T(8,128)} async-done(((f32[4096,1024]{0,1:T(8,128)}), f32[256,1024]{0,1:T(8,128)}) %reduce-scatter.2.cloned.1.call-update) | async-done | bytes 1048592 | tf_op jit(solution)/shard_map/reduce_scatter | solution.py:68
  608.9 1.7 convolution_bitcast_fusion.1
  610.7 1.8 convolution_bitcast_fusion.2
  612.5 1.5 pad_maximum_fusion
  614.2 1.0 copy.11
  615.2 150.5 %all-reduce.6.cloned.1.call-done = f32[2,512,512]{2,1,0:T(8,128)} async-done(((f32[2,512,512]{2,1,0:T(8,128)}), f32[2,512,512]{2,1,0:T(8,128)}) %all-reduce.6.cloned.1.call-update) | async-done | bytes 2097168 | tf_op jit(solution)/shard_map/psum | solution.py:85
  765.7 3.4 maximum_add_fusion
  (78 shorter events, 16.7 us)
Async XLA Ops:
  7.2 366.4 %all-gather.2.cloned.1.call-start = ((), (), s32[]{:S(2)}) async-start(), calls=%async_computation.1 | async-start | bytes 8912896 | tf_op jit(solution)/shard_map/all_gather | solution.py:57
  18.6 1.0 copy-start.2
  267.5 47.1 %copy-start.1 = (f32[512,512]{1,0:T(8,128)S(1)}, f32[512,512]{1,0:T(8,128)}, u32[]{:S(2)}) copy-start(f32[512,512]{1,0:T(8,128)} %fusion.8) | copy-start | bytes 3145732
  307.9 6.8 copy-start.3
  317.7 171.6 %all-reduce.4.cloned.1.call-start = ((), (), s32[]{:S(2)}) async-start(), calls=%async_computation.2 | async-start | bytes 8388608 | tf_op jit(solution)/shard_map/psum | solution.py:12
  379.0 230.0 %reduce-scatter.2.cloned.1.call-start = ((), (), s32[]{:S(2)}) async-start(), calls=%async_computation.3 | async-start | bytes 17825792 | tf_op jit(solution)/shard_map/reduce_scatter | solution.py:68
  513.2 252.6 %all-reduce.6.cloned.1.call-start = ((), (), s32[]{:S(2)}) async-start(), calls=%async_computation.4 | async-start | bytes 4194304 | tf_op jit(solution)/shard_map/psum | solution.py:85
  610.7 3.4 copy-start
Sparse Core Ops, SparseCore 0:
  317.8 55.6 all-gather.1
  379.1 110.1 all-reduce.3
  513.3 95.6 reduce-scatter.1
  614.2 151.4 all-reduce.5
where the time goes:
time: 785 us; the launch traced here: 776 us
  waiting for transfers between devices  412 us (52%)
  other arithmetic  256 us (33%)
  matrix products  54 us (7%)
  local copies, waits for them, and re-layouts  33.7 us (4%)
  between operations  19.6 us (2%)
    another operation x28, other arithmetic, factor_inverse(): factor_lower = jnp.linalg.cholesky(shifted)  158 us
    psum x1, waiting for transfers between devices, local(): totals = lax.psum(jnp.stack(diagonal_terms), ('row', 'col'))  150 us
    psum x1, waiting for transfers between devices, from_root(): return lax.psum(kept, axis)  110 us
    reduce_scatter x1, waiting for transfers between devices, local(): lax.psum_scatter(product(jnp.int32(0), own_rows * lax.axis_size('col')),...  95.7 us
    another operation x5, other arithmetic, factor_inverse(): jax.scipy.linalg.solve_triangular(factor_lower, identity, lower=True)  80.9 us
    all_gather x1, waiting for transfers between devices, local(): row_block = lax.all_gather(groups, 'col', axis=0, tiled=True)  55.8 us
    dot_general x1, matrix products, product(): jnp.dot(ancestor_inverse, column_block, preferred_element_type=jnp.float32)  23.8 us
    another operation x27, local copies, waits for them, and re-layouts, factor_inverse(): jax.scipy.linalg.solve_triangular(factor_lower, identity, lower=True)  22.9 us
  transfers between devices with their start and end apart: 4, of which 4 were waited for; matrix products, arithmetic and copies ran while one was open for 0% of the time, Pallas kernels for 0%

commit v1 on v0

v1 whole, which is shorter than its diff:
```python
import functools

import jax
import jax.numpy as jnp
import numpy as np
from jax import lax
from jax.experimental import pallas as pl
from jax.experimental.pallas import tpu as pltpu
from jax.sharding import Mesh, PartitionSpec as P

HIGHEST = lax.Precision.HIGHEST
PERTURBATION = 1.0
BLOCK = 128
STRIP = 8
GROUP = 2
ROW = ("z_hi", "x")
COL = ("z_lo", "y", "core")
AXES = ROW + COL
CHIPS = ("z_hi", "x", "z_lo", "y")
MESH_SHAPE = (2, 4, 2, 4, 2)


def after(value, *earlier):
    return lax.optimization_barrier((value, earlier))[0]


def lane_spread(tile, lane):
    index = jnp.full(tile.shape, lane, jnp.int32)
    return jnp.take_along_axis(tile, index, axis=1, mode="promise_in_bounds")


def small_inverses(nodes):
    row = lax.broadcasted_iota(jnp.int32, nodes[0][0].shape, 0)
    for i in range(len(nodes[0])):
        at = row == i
        pivot = [1.0 / cols[i][i : i + 1, :] for cols in nodes]
        left = [jnp.where(at, -1.0, cols[i]) for cols in nodes]
        nodes = [
            [
                -l * p if j == i else jnp.where(at, 0.0, cols[j]) - l * (cols[j][i : i + 1, :] * p)
                for j in range(len(cols))
            ]
            for cols, l, p in zip(nodes, left, pivot)
        ]
    return nodes


def invert_blocks(ref):
    count, n, _ = ref.shape
    nodes = range(count)
    lane = lax.broadcasted_iota(jnp.int32, (STRIP, n), 1)
    wide = lax.broadcasted_iota(jnp.int32, (n, n), 1)

    def step(strip, carry):
        base = pl.multiple_of(strip * STRIP, STRIP)
        inside = (wide >= base) & (wide < base + STRIP)
        whole = [ref[k] for k in nodes]
        rows = [ref[k, pl.ds(base, STRIP), :] for k in nodes]
        small = small_inverses(
            [[lane_spread(rows[k], base + j) for j in range(STRIP)] for k in nodes]
        )
        top = [small[k][0] * rows[k][0:1, :] for k in nodes]
        for j in range(1, STRIP):
            top = [top[k] + small[k][j] * rows[k][j : j + 1, :] for k in nodes]
        for j in range(STRIP):
            top = [jnp.where(lane == base + j, small[k][j], top[k]) for k in nodes]
        rest = [jnp.where(inside, 0.0, whole[k]) for k in nodes]
        for j in range(STRIP):
            rest = [
                rest[k] - lane_spread(whole[k], base + j) * top[k][j : j + 1, :] for k in nodes
            ]
        for k in nodes:
            ref[k] = rest[k]
            ref[k, pl.ds(base, STRIP), :] = top[k]
        return carry

    lax.fori_loop(0, n // STRIP, step, 0)


def inverse_kernel(block, in_ref, flag_ref, out_ref, block_ref, panel_ref):
    count, width, _ = in_ref.shape
    n = block_ref.shape[1]
    here = pl.ds(block * n, n)
    if block == 0:
        row = lax.broadcasted_iota(jnp.int32, (width, width), 0)
        col = lax.broadcasted_iota(jnp.int32, (width, width), 1)
        for k in range(count):
            shifts = PERTURBATION * flag_ref[k : k + 1, :].astype(jnp.float32)
            out_ref[k] = in_ref[k] + jnp.where(row == col, shifts, 0.0)
    else:
        out_ref[...] = in_ref[...]
    for k in range(count):
        block_ref[k] = out_ref[k, here, here]
    invert_blocks(block_ref)

    def update(k, carry):
        inner = block_ref[k]
        panel_ref[...] = jnp.dot(
            inner, out_ref[k, here, :], precision=HIGHEST, preferred_element_type=jnp.float32
        )
        panel_ref[:, here] = inner
        left = out_ref[k, :, here]
        out_ref[k, :, here] = jnp.zeros((width, n), jnp.float32)
        out_ref[k] = out_ref[k] - jnp.dot(
            left, panel_ref[...], precision=HIGHEST, preferred_element_type=jnp.float32
        )
        out_ref[k, here, :] = panel_ref[...]
        return carry

    lax.fori_loop(0, count, update, 0)


def eliminate(block, matrices, pivot_flags):
    count, width, _ = matrices.shape
    return pl.pallas_call(
        functools.partial(inverse_kernel, block),
        out_shape=jax.ShapeDtypeStruct(matrices.shape, jnp.float32),
        scratch_shapes=[
            pltpu.VMEM((count, BLOCK, BLOCK), jnp.float32),
            pltpu.VMEM((BLOCK, width), jnp.float32),
        ],
        compiler_params=pltpu.CompilerParams(vmem_limit_bytes=32 * 2**20),
        cost_estimate=pl.CostEstimate(
            flops=5 * 10**9, bytes_accessed=8 * matrices.size, transcendentals=0
        ),
        name="eliminate",
    )(matrices, pivot_flags)


def shift(value, **steps):
    return send(value, lambda **at: {name: at[name] + by for name, by in steps.items()})


def send(value, target):
    extents = [lax.axis_size(name) for name in AXES]
    moves = []
    for source in np.ndindex(*extents):
        at = {name: int(i) for name, i in zip(AXES, source)}
        at.update(target(**at))
        there = [at[name] % extent for name, extent in zip(AXES, extents)]
        moves.append(tuple(int(np.ravel_multi_index(i, extents)) for i in (source, there)))
    return lax.ppermute(value, AXES, moves)


def seed(strip, flip):
    return send(
        strip,
        lambda z_hi, x, z_lo, y, core: dict(
            z_hi=y // 2 ^ flip, x=y % 2 * 2 + core, z_lo=z_hi, y=x, core=z_lo
        ),
    )


def product_kernel(order_ref, place_ref, *refs):
    tiles, (*pieces, out_ref, columns_ref) = refs[:GROUP], refs[GROUP:]
    rows = pieces[0].shape[1]

    @pl.when(pl.program_id(0) == 0)
    def _():
        slot = 0
        for piece in pieces:
            for part in range(piece.shape[0]):
                start = pl.multiple_of(place_ref[slot] * rows, rows)
                columns_ref[pl.ds(start, rows), :] = piece[part]
                slot += 1

    tile = jnp.concatenate([ref[0] for ref in tiles], axis=0)
    out = jnp.dot(tile, columns_ref[...], preferred_element_type=jnp.float32)
    out_ref[...] = out.astype(out_ref.dtype).reshape(out_ref.shape)


def product(tile, pieces, order, place, dtype):
    blocks = order.shape[0]
    _, rows, depth = tile.shape
    width = pieces[0].shape[2]

    def tile_spec(member):
        return pl.BlockSpec(
            (1, rows, depth), lambda i, order, place: (order[GROUP * i + member], 0, 0)
        )

    return pl.pallas_call(
        product_kernel,
        out_shape=jax.ShapeDtypeStruct((blocks, rows, width), dtype),
        grid_spec=pltpu.PrefetchScalarGridSpec(
            num_scalar_prefetch=2,
            grid=(blocks // GROUP,),
            in_specs=[tile_spec(member) for member in range(GROUP)]
            + [pl.BlockSpec(p.shape, lambda i, order, place: (0, 0, 0)) for p in pieces],
            out_specs=pl.BlockSpec((GROUP, rows, width), lambda i, order, place: (i, 0, 0)),
            scratch_shapes=[pltpu.VMEM((depth, width), jnp.bfloat16)],
        ),
        compiler_params=pltpu.CompilerParams(vmem_limit_bytes=60 * 2**20),
        cost_estimate=pl.CostEstimate(
            flops=2 * blocks * rows * depth * width,
            bytes_accessed=2 * blocks * rows * depth + 2 * depth * width,
            transcendentals=0,
        ),
        name="product",
    )(order, place, *[tile] * GROUP, *pieces)


def total(term):
    core = lax.axis_index("core")
    half = term.shape[0] // 2
    chips = 64
    low, high = term[:half], term[half:]
    part = jnp.where(core == 0, low, high) + shift(jnp.where(core == 0, high, low), core=1)
    slices = lax.all_to_all(part.reshape(chips, half // chips, -1), CHIPS, 0, 0)
    summed = jnp.sum(slices, axis=0, keepdims=True).astype(jnp.bfloat16)
    spread = lax.all_to_all(jnp.broadcast_to(summed, slices.shape), CHIPS, 0, 0)
    own = spread.reshape(half, -1)
    other = shift(own, core=1)
    return jnp.concatenate([jnp.where(core == 0, own, other), jnp.where(core == 0, other, own)])


def invert(diag_blocks, pivot_flags, panels, structure, ancestor_inverse):
    nodes, own_rows, _ = panels.shape
    z_hi, x, z_lo, y, core = [lax.axis_index(name) for name in AXES]
    tile = ancestor_inverse.reshape(16, own_rows, ancestor_inverse.shape[1])
    masked = [
        jnp.where(structure[k][:, None] != 0, panels[k], 0).astype(jnp.bfloat16)
        for k in range(nodes)
    ]
    steps = [(d, e) for d in range(4) for e in range(2)]
    kept = jnp.stack([(z_lo ^ e) * 8 + (y + d) % 4 * 2 + core for d, e in steps]).astype(jnp.int32)

    seeds = [seed(masked[0], flip) for flip in range(2)]
    along = [masked[1]] + [shift(masked[1], x=d) for d in (1, 2, 3)]

    state = eliminate(0, diag_blocks, pivot_flags)
    state = eliminate(1, state, pivot_flags)

    pair = after(jnp.stack(seeds), state)
    first = [pair] + [shift(pair, x=d) for d in (1, 2, 3)]
    first_place = jnp.stack([(z_hi ^ e) * 4 + (x - d) % 4 for d, e in steps]).astype(jnp.int32)

    stacked = after(jnp.stack(along), state)
    turned = []
    for d in range(4):
        part = lax.dynamic_index_in_dim(stacked, (x - y - d) % 4, 0, keepdims=False)
        turned.append(shift(part, y=d) if d else part)

    state = eliminate(2, after(state, pair, stacked), pivot_flags)
    quad = after(jnp.stack(turned), state)
    second = []
    for flip in range(2):
        second.append(
            send(quad, lambda z_hi, x, z_lo, y, core: dict(z_hi=core ^ flip, z_lo=z_hi, core=z_lo))
        )
    second_place = jnp.stack(
        [(y - d) % 4 * 2 + (z_hi ^ flip) for flip in range(2) for d in range(4)]
    ).astype(jnp.int32)
    inverses = eliminate(3, after(state, quad), pivot_flags)

    pieces = [first, second]
    places = [first_place, second_place]
    order = after(kept, inverses)
    applied, terms = [], []
    for k in range(nodes):
        given = product(tile, pieces[k], order ^ 1, places[k], jnp.bfloat16)
        other = shift(given, core=1)
        mine = product(tile, pieces[k], order, places[k], jnp.float32)
        both = mine + other.astype(jnp.float32)
        leaving = [both[2 * d : 2 * d + 2].astype(jnp.bfloat16) for d in (1, 2, 3)]
        order = after(kept, *leaving)
        summed = both[0:2]
        for d, part in zip((1, 2, 3), leaving):
            arrived = shift(part, y=d)
            summed = summed + arrived.astype(jnp.float32)
        summed = summed[0] + shift(summed[1].astype(jnp.bfloat16), z_lo=1).astype(jnp.float32)
        applied.append(jnp.dot(summed, inverses[k], precision=HIGHEST))
        normed = jnp.dot(masked[k].astype(jnp.float32), inverses[k], precision=HIGHEST)
        terms.append(
            lax.dot_general(
                normed.astype(jnp.bfloat16).astype(jnp.float32),
                applied[k],
                (((0,), (0,)), ((), ())),
                precision=HIGHEST,
                preferred_element_type=jnp.float32,
            )
        )
        last = leaving
    totals = [total(after(terms[0], *last)), total(terms[1])]
    inverse_diagonal = jnp.stack(
        [inverses[k] + totals[k].astype(jnp.float32) for k in range(nodes)]
    )
    inverse_panel = (-jnp.stack(applied)).astype(jnp.bfloat16)
    return (inverse_panel, inverse_diagonal)


def solution(mesh):
    mesh = Mesh(mesh.devices.reshape(MESH_SHAPE), AXES)
    in_specs = (P(), P(), P(None, AXES, None), P(None, AXES), P(ROW, COL))
    out_specs = (P(None, AXES, None), P())
    return jax.shard_map(invert, mesh=mesh, in_specs=in_specs, out_specs=out_specs, check_vma=False)
```

time: 785 us -> 297 us (0.38)
  waiting for transfers between devices: 412 us -> 77.6 us
  other arithmetic: 256 us -> 27.1 us
  starting transfers between devices: 0.16 us -> 91.2 us
  Pallas kernels: 0 us -> 76.6 us
  matrix products: 54 us -> 5.81 us
  local copies, waits for them, and re-layouts: 33.7 us -> 15.2 us
  between operations: 19.6 us -> 1.25 us
    psum x2 -> x0, waiting for transfers between devices: 261 us -> none  [the longest x1 150 us: local(): totals = lax.psum(jnp.stack(diagonal_terms), ('row', 'col'))]
    another operation x34 -> x6, other arithmetic: 240 us -> 13.3 us  [the longest x28 158 us: factor_inverse(): factor_lower = jnp.linalg.cholesky(shifted)]
    reduce_scatter x1 -> x0, waiting for transfers between devices: 95.7 us -> none  [local(): lax.psum_scatter(product(jnp.int32(0), own_rows * lax.axis_size('col')),...]
    pallas_call x0 -> x8, Pallas kernels: none -> 76.6 us  [the longest x4 38.7 us: product(): pl.pallas_call(product_kernel, out_shape=jax.ShapeDtypeStruct((blocks, ro...]
    ppermute x0 -> x27, starting transfers between devices: none -> 68.3 us  [send(): return lax.ppermute(value, AXES, moves)]
    all_gather x1 -> x0, waiting for transfers between devices: 55.8 us -> none  [local(): row_block = lax.all_gather(groups, 'col', axis=0, tiled=True)]
    ppermute x0 -> x27, waiting for transfers between devices: none -> 47.5 us  [send(): return lax.ppermute(value, AXES, moves)]
    all_to_all x0 -> x4, waiting for transfers between devices: none -> 30.1 us  [the longest x2 17.4 us: total(): slices = lax.all_to_all(part.reshape(chips, half // chips, -1), CHIPS, 0, 0)]
  transfers between devices with their start and end apart: 4 -> 31, of which waited for: 4 -> 13; matrix products, arithmetic and copies ran while one was open for 0% -> 13% of each run, Pallas kernels for 0% -> 20%
where the time goes in v1:
time: 297 us; the launch traced here: 295 us
  starting transfers between devices  91.2 us (31%)
  waiting for transfers between devices  77.6 us (26%)
  Pallas kernels  76.6 us (26%)
  other arithmetic  27.1 us (9%)
  local copies, waits for them, and re-layouts  15.2 us (5%)
  matrix products  5.81 us (2%)
    ppermute x27, starting transfers between devices, send(): return lax.ppermute(value, AXES, moves)  68.3 us
    ppermute x27, waiting for transfers between devices, send(): return lax.ppermute(value, AXES, moves)  47.5 us
    pallas_call x4, Pallas kernels, product(): pl.pallas_call(product_kernel, out_shape=jax.ShapeDtypeStruct((blocks, ro...  38.7 us
    pallas_call x4, Pallas kernels, eliminate(): pl.pallas_call(functools.partial(inverse_kernel, block), out_shape=jax.Sh...  37.9 us
    all_to_all x2, waiting for transfers between devices, total(): slices = lax.all_to_all(part.reshape(chips, half // chips, -1), CHIPS, 0, 0)  17.4 us
    all_to_all x2, waiting for transfers between devices, total(): spread = lax.all_to_all(jnp.broadcast_to(summed, slices.shape), CHIPS, 0, 0)  12.6 us
    all_to_all x2, starting transfers between devices, total(): slices = lax.all_to_all(part.reshape(chips, half // chips, -1), CHIPS, 0, 0)  12.3 us
    all_to_all x2, starting transfers between devices, total(): spread = lax.all_to_all(jnp.broadcast_to(summed, slices.shape), CHIPS, 0, 0)  10.6 us
  transfers between devices with their start and end apart: 31, of which 13 were waited for; matrix products, arithmetic and copies ran while one was open for 13% of the time, Pallas kernels for 20%

profile of v1, /device:TPU:1, one launch (start us, length us, event | category | flops | bytes accessed | tf_op | source)
XLA Modules:
  0.0 294.8 jit_solution(18084882795618380320)
XLA Ops:
  1.4 1.2 bitcast_select_fusion
  2.6 6.0 %collective-permute-start.1 = (bf16[256,512]{1,0:T(8,128)(2,1)S(1)}, bf16[256,512]{1,0:T(8,128)(2,1)}, u32[]{:S(2)}, u32[]{:S(2)}) collective-permute-start(bf16[256,512]{1,0:T(8,128)(2,1)S(1)} %get-tuple-element.41), channel_id=1, source_target_pairs={{0,64},{1,80},{2,96},{3,112},{4,0},{5,16},{6,32},{7,48},{8,65},{9,... | collective-permute-start | bytes 786440 | tf_op jit(solution)/shard_map/ppermute | solution.py:142
  8.6 3.4 %collective-permute-start = (bf16[256,512]{1,0:T(8,128)(2,1)S(1)}, bf16[256,512]{1,0:T(8,128)(2,1)}, u32[]{:S(2)}, u32[]{:S(2)}) collective-permute-start(bf16[256,512]{1,0:T(8,128)(2,1)S(1)} %get-tuple-element.41), channel_id=1, source_target_pairs={{0,0},{1,16},{2,32},{3,48},{4,64},{5,80},{6,96},{7,112},{8,1},{9,1... | collective-permute-start | bytes 786440 | tf_op jit(solution)/shard_map/ppermute | solution.py:142
  12.0 3.4 %collective-permute-start.4 = (bf16[256,512]{1,0:T(8,128)(2,1)S(1)}, bf16[256,512]{1,0:T(8,128)(2,1)}, u32[]{:S(2)}, u32[]{:S(2)}) collective-permute-start(bf16[256,512]{1,0:T(8,128)(2,1)S(1)} %get-tuple-element.40), channel_id=1, source_target_pairs={{0,48},{1,49},{2,50},{3,51},{4,52},{5,53},{6,54},{7,55},{8,56},{9,... | collective-permute-start | bytes 786440 | tf_op jit(solution)/shard_map/ppermute | solution.py:142
  16.1 1.6 copy-done
  18.3 9.5 %eliminate.4.in_ref = f32[2,512,512]{2,1,0:T(8,128)S(1)} custom-call(f32[2,512,512]{2,1,0:T(8,128)S(1)} %copy-done, s32[2,512]{1,0:T(2,128)S(1)} %copy-done.1), custom_call_target="tpu_custom_call" | custom-call | flops 5000000000 | bytes 4194304 | tf_op jit(solution)/shard_map/eliminate/pallas_call | solution.py:115
  27.9 9.5 %eliminate.5.in_ref = f32[2,512,512]{2,1,0:T(8,128)S(1)} custom-call(f32[2,512,512]{2,1,0:T(8,128)S(1)} %eliminate.4.in_ref, s32[2,512]{1,0:T(2,128)S(1)} %copy-done.2), custom_call_target="tpu_custom_call" | custom-call | flops 5000000000 | bytes 4194304 | tf_op jit(solution)/shard_map/eliminate/pallas_call | solution.py:115
  38.5 1.1 pad_maximum_fusion.3.refs_2_
  39.6 2.1 collective-permute-start.10
  41.7 1.8 collective-permute-start.9
  43.4 1.2 pad_maximum_fusion.1
  44.8 4.1 %collective-permute-start.7 = (bf16[256,512]{1,0:T(8,128)(2,1)S(1)}, bf16[256,512]{1,0:T(8,128)(2,1)S(1)}, u32[]{:S(2)}, u32[]{:S(2)}) collective-permute-start(bf16[256,512]{1,0:T(8,128)(2,1)S(1)} %get-tuple-element.33), channel_id=1, source_target_pairs={{0,6},{1,7},{2,0},{3,1},{4,2},{5,3},{6,4},{7,5},{8,14},{9,15},{10,... | collective-permute-start | bytes 786440 | tf_op jit(solution)/shard_map/ppermute | solution.py:142
  49.6 9.5 %eliminate.6.in_ref = f32[2,512,512]{2,1,0:T(8,128)S(1)} custom-call(f32[2,512,512]{2,1,0:T(8,128)S(1)} %eliminate.5.in_ref, s32[2,512]{1,0:T(2,128)S(1)} %copy-done.2), custom_call_target="tpu_custom_call" | custom-call | flops 5000000000 | bytes 4194304 | tf_op jit(solution)/shard_map/eliminate/pallas_call | solution.py:115
  60.0 3.7 %collective-permute-done.5 = bf16[256,512]{1,0:T(8,128)(2,1)S(1)} collective-permute-done((bf16[256,512]{1,0:T(8,128)(2,1)S(1)}, bf16[256,512]{1,0:T(8,128)(2,1)S(1)}, u32[]{:S(2)}, u32[]{:S(2)}) %collective-permute-start.5) | collective-permute-done | bytes 262176 | tf_op jit(solution)/shard_map/ppermute | solution.py:142
  63.7 1.1 pad_maximum_fusion.2
  64.8 9.4 %eliminate.7 = f32[2,512,512]{2,1,0:T(8,128)S(1)} custom-call(f32[2,512,512]{2,1,0:T(8,128)S(1)} %eliminate.6.in_ref, s32[2,512]{1,0:T(2,128)S(1)} %copy-done.2), custom_call_target="tpu_custom_call" | custom-call | flops 5000000000 | bytes 4194304 | tf_op jit(solution)/shard_map/eliminate/pallas_call | solution.py:115
  74.8 0.9 copy-done.12
  75.9 9.4 %product.5 = bf16[8,256,512]{2,1,0:T(8,128)(2,1)} custom-call(s32[8]{0:T(128)} %broadcast_xor_fusion.1.order_ref, s32[8]{0:T(128)} %stack.158.place_ref, bf16[16,256,2048]{2,1,0:T(8,128)(2,1)} %bitcast.87, bf16[16,256,2048]{2,1,0:T(8,128)(2,1)} %bitcast.88, bf16[2,256,512]{2,1,0:T(8,128)(2,1)} %copy-done.4, bf16[2,256,512]{2,1,0:T(8,128)(2,1)} %copy-done.12, ...), custom_call_target="tpu_custom_call" | custom-call | flops 4294967296 | bytes 10485760 | tf_op jit(solution)/shard_map/product/pallas_call | solution.py:182
  86.8 2.4 collective-permute-start.16
  89.3 9.9 %product.4 = f32[8,256,512]{2,1,0:T(8,128)} custom-call(s32[8]{0:T(128)} %copy-done.16, s32[8]{0:T(128)} %stack.158.place_ref, bf16[16,256,2048]{2,1,0:T(8,128)(2,1)} %bitcast.89, bf16[16,256,2048]{2,1,0:T(8,128)(2,1)} %bitcast.90, bf16[2,256,512]{2,1,0:T(8,128)(2,1)} %copy-done.4, bf16[2,256,512]{2,1,0:T(8,128)(2,1)} %copy-done.12, ...), custom_call_target="tpu_custom_call" | custom-call | flops 4294967296 | bytes 10485760 | tf_op jit(solution)/shard_map/product/pallas_call | solution.py:182
  99.2 5.8 %fusion.31 = (bf16[8,256,512]{2,1,0:T(8,128)(2,1)S(1)}, f32[8,256,512]{2,1,0:T(8,128)}) fusion(f32[8,256,512]{2,1,0:T(8,128)} %product.4, bf16[8,256,512]{2,1,0:T(8,128)(2,1)} %collective-permute-done.11), kind=kLoop, calls=%fused_computation.65 | loop fusion | flops 3145728 | bytes 12582912 | tf_op jit(solution)/shard_map/convert.7
  105.0 1.2 fusion.33
  106.8 2.7 collective-permute-done.17.refs_3_
  109.5 2.6 collective-permute-done.16.refs_2_
  112.0 9.5 %product.7 = bf16[8,256,512]{2,1,0:T(8,128)(2,1)} custom-call(s32[8]{0:T(128)} %broadcast_xor_fusion.order_ref, s32[8]{0:T(128)} %stack.168.place_ref, bf16[16,256,2048]{2,1,0:T(8,128)(2,1)} %bitcast.91, bf16[16,256,2048]{2,1,0:T(8,128)(2,1)} %bitcast.92, bf16[4,256,512]{2,1,0:T(8,128)(2,1)} %collective-permute-done.16.refs_2_, bf16[4,256,512]{2,1,0:T(8,128)(2,1)} %copy-done.9), custom_call_target="tpu_custom_call" | custom-call | flops 4294967296 | bytes 10485760 | tf_op jit(solution)/shard_map/product/pallas_call | solution.py:182
  121.5 3.0 %collective-permute-start.18 = (bf16[8,256,512]{2,1,0:T(8,128)(2,1)}, bf16[8,256,512]{2,1,0:T(8,128)(2,1)}, u32[]{:S(2)}, u32[]{:S(2)}) collective-permute-start(bf16[8,256,512]{2,1,0:T(8,128)(2,1)} %product.7), channel_id=1, source_target_pairs={{0,1},{1,0},{2,3},{3,2},{4,5},{5,4},{6,7},{7,6},{8,9},{9,8},{10,11... | collective-permute-start | bytes 6291464 | tf_op jit(solution)/shard_map/ppermute | solution.py:142
  124.5 2.0 collective-permute-start.14
  127.2 1.7 convolution_convert_fusion.1
  128.8 9.9 %product.6 = f32[8,256,512]{2,1,0:T(8,128)} custom-call(s32[8]{0:T(128)} %copy-done.16, s32[8]{0:T(128)} %stack.168.place_ref, bf16[16,256,2048]{2,1,0:T(8,128)(2,1)} %bitcast.93, bf16[16,256,2048]{2,1,0:T(8,128)(2,1)} %bitcast.94, bf16[4,256,512]{2,1,0:T(8,128)(2,1)} %collective-permute-done.16.refs_2_, bf16[4,256,512]{2,1,0:T(8,128)(2,1)} %copy-done.9), custom_call_target="tpu_custom_call" | custom-call | flops 4294967296 | bytes 10485760 | tf_op jit(solution)/shard_map/product/pallas_call | solution.py:182
  138.7 2.8 collective-permute-done.13
  141.5 11.9 %collective-permute-done.12 = bf16[2,256,512]{2,1,0:T(8,128)(2,1)} collective-permute-done((bf16[2,256,512]{2,1,0:T(8,128)(2,1)}, bf16[2,256,512]{2,1,0:T(8,128)(2,1)}, u32[]{:S(2)}, u32[]{:S(2)}) %collective-permute-start.12) | collective-permute-done | bytes 524320 | tf_op jit(solution)/shard_map/ppermute | solution.py:142
  153.5 1.8 fusion.3
  155.3 19.8 %collective-permute-start.15 = (bf16[256,512]{1,0:T(8,128)(2,1)S(1)}, bf16[256,512]{1,0:T(8,128)(2,1)S(1)}, u32[]{:S(2)}, u32[]{:S(2)}) collective-permute-start(bf16[256,512]{1,0:T(8,128)(2,1)S(1)} %fusion.21), channel_id=1, source_target_pairs={{0,8},{1,9},{2,10},{3,11},{4,12},{5,13},{6,14},{7,15},{8,0},{9,1},... | collective-permute-start | bytes 786440 | tf_op jit(solution)/shard_map/ppermute | solution.py:142
  175.1 2.6 fusion.30
  177.9 2.7 collective-permute-start.21
  181.3 1.1 fusion.9
  182.4 20.6 %collective-permute-done.19 = bf16[2,256,512]{2,1,0:T(8,128)(2,1)S(1)} collective-permute-done((bf16[2,256,512]{2,1,0:T(8,128)(2,1)S(1)}, bf16[2,256,512]{2,1,0:T(8,128)(2,1)S(1)}, u32[]{:S(2)}, u32[]{:S(2)}) %collective-permute-start.19) | collective-permute-done | bytes 524320 | tf_op jit(solution)/shard_map/ppermute | solution.py:142
  203.4 1.1 collective-permute-start.22
  205.2 1.7 collective-permute-start.23
  206.9 2.8 collective-permute-done.22
  209.7 1.1 fusion.6
  210.8 0.8 copy-done.7
  212.3 0.9 slice_select_fusion
  213.2 2.5 collective-permute-start.25
  215.6 0.9 select_add_fusion.1
  216.6 2.0 reshape.129
  218.6 6.8 %all-to-all-start = ((f32[64,4,512]{2,1,0:T(4,128)}), f32[64,4,512]{2,1,0:T(4,128)}, u32[]{:S(2)}, u32[]{:S(2)}) async-start(f32[64,4,512]{2,1,0:T(4,128)} %reshape.129), calls=%async_computation | async-start | bytes 1048576 | tf_op jit(solution)/shard_map/all_to_all | solution.py:209
  225.5 2.0 select_add_fusion
  227.5 2.0 reshape.131
  229.5 8.1 %all-to-all-done = f32[64,4,512]{2,1,0:T(4,128)} async-done(((f32[64,4,512]{2,1,0:T(4,128)}), f32[64,4,512]{2,1,0:T(4,128)}, u32[]{:S(2)}, u32[]{:S(2)}) %all-to-all-start) | async-done | bytes 524320 | tf_op jit(solution)/shard_map/all_to_all | solution.py:209
  237.6 5.5 %all-to-all-start.2 = ((f32[64,4,512]{2,1,0:T(4,128)}), f32[64,4,512]{2,1,0:T(4,128)}, u32[]{:S(2)}, u32[]{:S(2)}) async-start(f32[64,4,512]{2,1,0:T(4,128)} %reshape.131), calls=%async_computation.2 | async-start | bytes 1048576 | tf_op jit(solution)/shard_map/all_to_all | solution.py:209
  243.2 1.2 reduce_sum.18
  244.4 9.3 %all-to-all-done.2 = f32[64,4,512]{2,1,0:T(4,128)} async-done(((f32[64,4,512]{2,1,0:T(4,128)}), f32[64,4,512]{2,1,0:T(4,128)}, u32[]{:S(2)}, u32[]{:S(2)}) %all-to-all-start.2) | async-done | bytes 524320 | tf_op jit(solution)/shard_map/all_to_all | solution.py:209
  254.5 5.2 %all-to-all-start.1 = ((bf16[64,4,512]{2,1,0:T(4,128)(2,1)}), bf16[64,4,512]{2,1,0:T(4,128)(2,1)S(1)}, u32[]{:S(2)}, u32[]{:S(2)}) async-start(bf16[64,4,512]{2,1,0:T(4,128)(2,1)} %broadcast_in_dim.42), calls=%async_computation.1 | async-start | bytes 524288 | tf_op jit(solution)/shard_map/all_to_all | solution.py:211
  259.7 1.2 reduce_sum.19
  260.8 8.1 %all-to-all-done.1 = bf16[64,4,512]{2,1,0:T(4,128)(2,1)S(1)} async-done(((bf16[64,4,512]{2,1,0:T(4,128)(2,1)}), bf16[64,4,512]{2,1,0:T(4,128)(2,1)S(1)}, u32[]{:S(2)}, u32[]{:S(2)}) %all-to-all-start.1) | async-done | bytes 262176 | tf_op jit(solution)/shard_map/all_to_all | solution.py:211
  269.7 5.5 %all-to-all-start.3 = ((bf16[64,4,512]{2,1,0:T(4,128)(2,1)}), bf16[64,4,512]{2,1,0:T(4,128)(2,1)}, u32[]{:S(2)}, u32[]{:S(2)}) async-start(bf16[64,4,512]{2,1,0:T(4,128)(2,1)} %broadcast_in_dim.43), calls=%async_computation.3 | async-start | bytes 524288 | tf_op jit(solution)/shard_map/all_to_all | solution.py:211
  276.0 3.9 %collective-permute-start.24 = (bf16[256,512]{1,0:T(8,128)(2,1)}, bf16[256,512]{1,0:T(8,128)(2,1)}, u32[]{:S(2)}, u32[]{:S(2)}) collective-permute-start(bf16[256,512]{1,0:T(8,128)(2,1)} %reshape.130), channel_id=1, source_target_pairs={{0,1},{1,0},{2,3},{3,2},{4,5},{5,4},{6,7},{7,6},{8,9},{9,8},{10,11... | collective-permute-start | bytes 786440 | tf_op jit(solution)/shard_map/ppermute | solution.py:142
  279.8 4.5 %all-to-all-done.3 = bf16[64,4,512]{2,1,0:T(4,128)(2,1)} async-done(((bf16[64,4,512]{2,1,0:T(4,128)(2,1)}), bf16[64,4,512]{2,1,0:T(4,128)(2,1)}, u32[]{:S(2)}, u32[]{:S(2)}) %all-to-all-start.3) | async-done | bytes 262176 | tf_op jit(solution)/shard_map/all_to_all | solution.py:211
  284.3 1.7 reshape.132
  286.0 5.0 %collective-permute-start.26 = (bf16[256,512]{1,0:T(8,128)(2,1)}, bf16[256,512]{1,0:T(8,128)(2,1)S(1)}, u32[]{:S(2)}, u32[]{:S(2)}) collective-permute-start(bf16[256,512]{1,0:T(8,128)(2,1)} %reshape.132), channel_id=1, source_target_pairs={{0,1},{1,0},{2,3},{3,2},{4,5},{5,4},{6,7},{7,6},{8,9},{9,8},{10,11... | collective-permute-start | bytes 786440 | tf_op jit(solution)/shard_map/ppermute | solution.py:142
  291.0 0.9 fusion.4
  291.9 1.0 select_bitcast_fusion.3
  293.3 1.5 pad_maximum_fusion
  (85 shorter events, 13.6 us)
Async XLA Ops:
  2.6 35.9 %collective-permute-start.1 = (bf16[256,512]{1,0:T(8,128)(2,1)S(1)}, bf16[256,512]{1,0:T(8,128)(2,1)}, u32[]{:S(2)}, u32[]{:S(2)}) collective-permute-start(bf16[256,512]{1,0:T(8,128)(2,1)S(1)} %get-tuple-element.41), channel_id=1, source_target_pairs={{0,64},{1,80},{2,96},{3,112},{4,0},{5,16},{6,32},{7,48},{8,65},{9,... | collective-permute-start | bytes 786440 | tf_op jit(solution)/shard_map/ppermute | solution.py:142
  8.6 29.9 %collective-permute-start = (bf16[256,512]{1,0:T(8,128)(2,1)S(1)}, bf16[256,512]{1,0:T(8,128)(2,1)}, u32[]{:S(2)}, u32[]{:S(2)}) collective-permute-start(bf16[256,512]{1,0:T(8,128)(2,1)S(1)} %get-tuple-element.41), channel_id=1, source_target_pairs={{0,0},{1,16},{2,32},{3,48},{4,64},{5,80},{6,96},{7,112},{8,1},{9,1... | collective-permute-start | bytes 786440 | tf_op jit(solution)/shard_map/ppermute | solution.py:142
  12.0 31.4 %collective-permute-start.4 = (bf16[256,512]{1,0:T(8,128)(2,1)S(1)}, bf16[256,512]{1,0:T(8,128)(2,1)}, u32[]{:S(2)}, u32[]{:S(2)}) collective-permute-start(bf16[256,512]{1,0:T(8,128)(2,1)S(1)} %get-tuple-element.40), channel_id=1, source_target_pairs={{0,48},{1,49},{2,50},{3,51},{4,52},{5,53},{6,54},{7,55},{8,56},{9,... | collective-permute-start | bytes 786440 | tf_op jit(solution)/shard_map/ppermute | solution.py:142
  15.4 28.1 %collective-permute-start.3 = (bf16[256,512]{1,0:T(8,128)(2,1)S(1)}, bf16[256,512]{1,0:T(8,128)(2,1)}, u32[]{:S(2)}, u32[]{:S(2)}) collective-permute-start(bf16[256,512]{1,0:T(8,128)(2,1)S(1)} %get-tuple-element.40), channel_id=1, source_target_pairs={{0,32},{1,33},{2,34},{3,35},{4,36},{5,37},{6,38},{7,39},{8,40},{9,... | collective-permute-start | bytes 786440 | tf_op jit(solution)/shard_map/ppermute | solution.py:142
  15.4 28.1 %collective-permute-start.2 = (bf16[256,512]{1,0:T(8,128)(2,1)S(1)}, bf16[256,512]{1,0:T(8,128)(2,1)}, u32[]{:S(2)}, u32[]{:S(2)}) collective-permute-start(bf16[256,512]{1,0:T(8,128)(2,1)S(1)} %get-tuple-element.40), channel_id=1, source_target_pairs={{0,16},{1,17},{2,18},{3,19},{4,20},{5,21},{6,22},{7,23},{8,24},{9,... | collective-permute-start | bytes 786440 | tf_op jit(solution)/shard_map/ppermute | solution.py:142
  16.1 1.6 copy-start
  17.7 0.7 copy-start.1
  18.3 9.6 %copy-start.2 = (s32[2,512]{1,0:T(2,128)S(1)}, s32[2,512]{1,0:T(2,128)}, u32[]{:S(2)}) copy-start(s32[2,512]{1,0:T(2,128)} %flag_ref.7) | copy-start | bytes 12292
  27.9 10.5 %copy-start.13 = (bf16[2,256,512]{2,1,0:T(8,128)(2,1)S(1)}, bf16[2,256,512]{2,1,0:T(8,128)(2,1)}, u32[]{:S(2)}) copy-start(bf16[2,256,512]{2,1,0:T(8,128)(2,1)} %param.7) | copy-start | bytes 1572868
  37.7 36.5 %copy-start.16 = (s32[8]{0:T(128)}, s32[8]{0:T(128)S(1)}, u32[]{:S(2)}) copy-start(s32[8]{0:T(128)S(1)} %stack.138.order_ref) | copy-start | bytes 100
  39.6 19.7 %copy-start.4 = (bf16[2,256,512]{2,1,0:T(8,128)(2,1)}, bf16[2,256,512]{2,1,0:T(8,128)(2,1)S(1)}, u32[]{:S(2)}) copy-start(bf16[2,256,512]{2,1,0:T(8,128)(2,1)S(1)} %pad_maximum_fusion.3.refs_2_) | copy-start | bytes 1572868
  39.6 35.2 %collective-permute-start.10 = (bf16[2,256,512]{2,1,0:T(8,128)(2,1)S(1)}, bf16[2,256,512]{2,1,0:T(8,128)(2,1)S(1)}, u32[]{:S(2)}, u32[]{:S(2)}) collective-permute-start(bf16[2,256,512]{2,1,0:T(8,128)(2,1)S(1)} %pad_maximum_fusion.3.refs_2_), channel_id=1, source_target_pairs={{0,48},{1,49},{2,50},{3,51},{4,52},{5,53},{6,54},{7,55},{8,56},{9,... | collective-permute-start | bytes 1572872 | tf_op jit(solution)/shard_map/ppermute | solution.py:142
  41.7 33.1 %collective-permute-start.9 = (bf16[2,256,512]{2,1,0:T(8,128)(2,1)S(1)}, bf16[2,256,512]{2,1,0:T(8,128)(2,1)S(1)}, u32[]{:S(2)}, u32[]{:S(2)}) collective-permute-start(bf16[2,256,512]{2,1,0:T(8,128)(2,1)S(1)} %pad_maximum_fusion.3.refs_2_), channel_id=1, source_target_pairs={{0,32},{1,33},{2,34},{3,35},{4,36},{5,37},{6,38},{7,39},{8,40},{9,... | collective-permute-start | bytes 1572872 | tf_op jit(solution)/shard_map/ppermute | solution.py:142
  44.8 14.5 %collective-permute-start.7 = (bf16[256,512]{1,0:T(8,128)(2,1)S(1)}, bf16[256,512]{1,0:T(8,128)(2,1)S(1)}, u32[]{:S(2)}, u32[]{:S(2)}) collective-permute-start(bf16[256,512]{1,0:T(8,128)(2,1)S(1)} %get-tuple-element.33), channel_id=1, source_target_pairs={{0,6},{1,7},{2,0},{3,1},{4,2},{5,3},{6,4},{7,5},{8,14},{9,15},{10,... | collective-permute-start | bytes 786440 | tf_op jit(solution)/shard_map/ppermute | solution.py:142
  48.9 11.1 %collective-permute-start.6 = (bf16[256,512]{1,0:T(8,128)(2,1)S(1)}, bf16[256,512]{1,0:T(8,128)(2,1)S(1)}, u32[]{:S(2)}, u32[]{:S(2)}) collective-permute-start(bf16[256,512]{1,0:T(8,128)(2,1)S(1)} %get-tuple-element.34), channel_id=1, source_target_pairs={{0,4},{1,5},{2,6},{3,7},{4,0},{5,1},{6,2},{7,3},{8,12},{9,13},{10,... | collective-permute-start | bytes 786440 | tf_op jit(solution)/shard_map/ppermute | solution.py:142
  48.9 14.8 %collective-permute-start.5 = (bf16[256,512]{1,0:T(8,128)(2,1)S(1)}, bf16[256,512]{1,0:T(8,128)(2,1)S(1)}, u32[]{:S(2)}, u32[]{:S(2)}) collective-permute-start(bf16[256,512]{1,0:T(8,128)(2,1)S(1)} %get-tuple-element.35), channel_id=1, source_target_pairs={{0,2},{1,3},{2,4},{3,5},{4,6},{5,7},{6,0},{7,1},{8,10},{9,11},{10,... | collective-permute-start | bytes 786440 | tf_op jit(solution)/shard_map/ppermute | solution.py:142
  59.3 15.5 %collective-permute-start.8 = (bf16[2,256,512]{2,1,0:T(8,128)(2,1)S(1)}, bf16[2,256,512]{2,1,0:T(8,128)(2,1)S(1)}, u32[]{:S(2)}, u32[]{:S(2)}) collective-permute-start(bf16[2,256,512]{2,1,0:T(8,128)(2,1)S(1)} %pad_maximum_fusion.3.refs_2_), channel_id=1, source_target_pairs={{0,16},{1,17},{2,18},{3,19},{4,20},{5,21},{6,22},{7,23},{8,24},{9,... | collective-permute-start | bytes 1572872 | tf_op jit(solution)/shard_map/ppermute | solution.py:142
  74.8 1.0 copy-start.10
  74.8 1.2 copy-start.11
  74.8 0.9 copy-start.12
  85.4 13.8 %collective-permute-start.11 = (bf16[8,256,512]{2,1,0:T(8,128)(2,1)}, bf16[8,256,512]{2,1,0:T(8,128)(2,1)}, u32[]{:S(2)}, u32[]{:S(2)}) collective-permute-start(bf16[8,256,512]{2,1,0:T(8,128)(2,1)} %product.5), channel_id=1, source_target_pairs={{0,1},{1,0},{2,3},{3,2},{4,5},{5,4},{6,7},{7,6},{8,9},{9,8},{10,11... | collective-permute-start | bytes 6291464 | tf_op jit(solution)/shard_map/ppermute | solution.py:142
  86.8 22.6 %collective-permute-start.17 = (bf16[4,256,512]{2,1,0:T(8,128)(2,1)}, bf16[4,256,512]{2,1,0:T(8,128)(2,1)S(1)}, u32[]{:S(2)}, u32[]{:S(2)}) collective-permute-start(bf16[4,256,512]{2,1,0:T(8,128)(2,1)} %pad_maximum_fusion.2), channel_id=1, source_target_pairs={{0,64},{1,0},{2,66},{3,2},{4,68},{5,4},{6,70},{7,6},{8,65},{9,1},{... | collective-permute-start | bytes 3145736 | tf_op jit(solution)/shard_map/ppermute | solution.py:142
  86.8 25.2 %collective-permute-start.16 = (bf16[4,256,512]{2,1,0:T(8,128)(2,1)}, bf16[4,256,512]{2,1,0:T(8,128)(2,1)}, u32[]{:S(2)}, u32[]{:S(2)}) collective-permute-start(bf16[4,256,512]{2,1,0:T(8,128)(2,1)} %pad_maximum_fusion.2), channel_id=1, source_target_pairs={{0,0},{1,64},{2,2},{3,66},{4,4},{5,68},{6,6},{7,70},{8,1},{9,65},{... | collective-permute-start | bytes 3145736 | tf_op jit(solution)/shard_map/ppermute | solution.py:142
  105.0 1.2 copy-start.17
  109.5 2.6 copy-start.9
  121.5 53.6 %collective-permute-start.18 = (bf16[8,256,512]{2,1,0:T(8,128)(2,1)}, bf16[8,256,512]{2,1,0:T(8,128)(2,1)}, u32[]{:S(2)}, u32[]{:S(2)}) collective-permute-start(bf16[8,256,512]{2,1,0:T(8,128)(2,1)} %product.7), channel_id=1, source_target_pairs={{0,1},{1,0},{2,3},{3,2},{4,5},{5,4},{6,7},{7,6},{8,9},{9,8},{10,11... | collective-permute-start | bytes 6291464 | tf_op jit(solution)/shard_map/ppermute | solution.py:142
  124.5 14.2 %collective-permute-start.14 = (bf16[2,256,512]{2,1,0:T(8,128)(2,1)}, bf16[2,256,512]{2,1,0:T(8,128)(2,1)S(1)}, u32[]{:S(2)}, u32[]{:S(2)}) collective-permute-start(bf16[2,256,512]{2,1,0:T(8,128)(2,1)} %get-tuple-element.29), channel_id=1, source_target_pairs={{0,6},{1,7},{2,0},{3,1},{4,2},{5,3},{6,4},{7,5},{8,14},{9,15},{10,... | collective-permute-start | bytes 1572872 | tf_op jit(solution)/shard_map/ppermute | solution.py:142
  126.6 15.0 %collective-permute-start.13 = (bf16[2,256,512]{2,1,0:T(8,128)(2,1)}, bf16[2,256,512]{2,1,0:T(8,128)(2,1)S(1)}, u32[]{:S(2)}, u32[]{:S(2)}) collective-permute-start(bf16[2,256,512]{2,1,0:T(8,128)(2,1)} %get-tuple-element.30), channel_id=1, source_target_pairs={{0,4},{1,5},{2,6},{3,7},{4,0},{5,1},{6,2},{7,3},{8,12},{9,13},{10,... | collective-permute-start | bytes 1572872 | tf_op jit(solution)/shard_map/ppermute | solution.py:142
  126.9 26.5 %collective-permute-start.12 = (bf16[2,256,512]{2,1,0:T(8,128)(2,1)}, bf16[2,256,512]{2,1,0:T(8,128)(2,1)}, u32[]{:S(2)}, u32[]{:S(2)}) collective-permute-start(bf16[2,256,512]{2,1,0:T(8,128)(2,1)} %get-tuple-element.31), channel_id=1, source_target_pairs={{0,2},{1,3},{2,4},{3,5},{4,6},{5,7},{6,0},{7,1},{8,10},{9,11},{10,... | collective-permute-start | bytes 1572872 | tf_op jit(solution)/shard_map/ppermute | solution.py:142
  153.5 21.6 %copy-start.3 = (f32[8,256,512]{2,1,0:T(8,128)S(1)}, f32[8,256,512]{2,1,0:T(8,128)}, u32[]{:S(2)}) copy-start(f32[8,256,512]{2,1,0:T(8,128)} %product.6) | copy-start | bytes 12582916
  155.3 26.0 %collective-permute-start.15 = (bf16[256,512]{1,0:T(8,128)(2,1)S(1)}, bf16[256,512]{1,0:T(8,128)(2,1)S(1)}, u32[]{:S(2)}, u32[]{:S(2)}) collective-permute-start(bf16[256,512]{1,0:T(8,128)(2,1)S(1)} %fusion.21), channel_id=1, source_target_pairs={{0,8},{1,9},{2,10},{3,11},{4,12},{5,13},{6,14},{7,15},{8,0},{9,1},... | collective-permute-start | bytes 786440 | tf_op jit(solution)/shard_map/ppermute | solution.py:142
  177.8 25.2 %collective-permute-start.19 = (bf16[2,256,512]{2,1,0:T(8,128)(2,1)S(1)}, bf16[2,256,512]{2,1,0:T(8,128)(2,1)S(1)}, u32[]{:S(2)}, u32[]{:S(2)}) collective-permute-start(bf16[2,256,512]{2,1,0:T(8,128)(2,1)S(1)} %get-tuple-element.26), channel_id=1, source_target_pairs={{0,2},{1,3},{2,4},{3,5},{4,6},{5,7},{6,0},{7,1},{8,10},{9,11},{10,... | collective-permute-start | bytes 1572872 | tf_op jit(solution)/shard_map/ppermute | solution.py:142
  177.9 25.1 %collective-permute-start.21 = (bf16[2,256,512]{2,1,0:T(8,128)(2,1)S(1)}, bf16[2,256,512]{2,1,0:T(8,128)(2,1)S(1)}, u32[]{:S(2)}, u32[]{:S(2)}) collective-permute-start(bf16[2,256,512]{2,1,0:T(8,128)(2,1)S(1)} %get-tuple-element.27), channel_id=1, source_target_pairs={{0,6},{1,7},{2,0},{3,1},{4,2},{5,3},{6,4},{7,5},{8,14},{9,15},{10,... | collective-permute-start | bytes 1572872 | tf_op jit(solution)/shard_map/ppermute | solution.py:142
  180.6 22.5 %collective-permute-start.20 = (bf16[2,256,512]{2,1,0:T(8,128)(2,1)S(1)}, bf16[2,256,512]{2,1,0:T(8,128)(2,1)S(1)}, u32[]{:S(2)}, u32[]{:S(2)}) collective-permute-start(bf16[2,256,512]{2,1,0:T(8,128)(2,1)S(1)} %get-tuple-element.28), channel_id=1, source_target_pairs={{0,4},{1,5},{2,6},{3,7},{4,0},{5,1},{6,2},{7,3},{8,12},{9,13},{10,... | collective-permute-start | bytes 1572872 | tf_op jit(solution)/shard_map/ppermute | solution.py:142
  182.4 22.1 %copy-start.5 = (f32[256,512]{1,0:T(8,128)}, f32[256,512]{1,0:T(8,128)S(1)}, u32[]{:S(2)}) copy-start(f32[256,512]{1,0:T(8,128)S(1)} %fusion.9) | copy-start | bytes 1572868
  203.4 6.3 %collective-permute-start.22 = (bf16[256,512]{1,0:T(8,128)(2,1)S(1)}, bf16[256,512]{1,0:T(8,128)(2,1)S(1)}, u32[]{:S(2)}, u32[]{:S(2)}) collective-permute-start(bf16[256,512]{1,0:T(8,128)(2,1)S(1)} %fusion.22), channel_id=1, source_target_pairs={{0,8},{1,9},{2,10},{3,11},{4,12},{5,13},{6,14},{7,15},{8,0},{9,1},... | collective-permute-start | bytes 786440 | tf_op jit(solution)/shard_map/ppermute | solution.py:142
  205.2 10.4 %collective-permute-start.23 = (f32[256,512]{1,0:T(8,128)S(1)}, f32[256,512]{1,0:T(8,128)S(1)}, u32[]{:S(2)}, u32[]{:S(2)}) collective-permute-start(f32[256,512]{1,0:T(8,128)S(1)} %slice_select_fusion.1), channel_id=1, source_target_pairs={{0,1},{1,0},{2,3},{3,2},{4,5},{5,4},{6,7},{7,6},{8,9},{9,8},{10,11... | collective-permute-start | bytes 1572872 | tf_op jit(solution)/shard_map/ppermute | solution.py:142
  210.8 0.8 copy-start.7
  213.2 12.3 %collective-permute-start.25 = (f32[256,512]{1,0:T(8,128)}, f32[256,512]{1,0:T(8,128)}, u32[]{:S(2)}, u32[]{:S(2)}) collective-permute-start(f32[256,512]{1,0:T(8,128)} %slice_select_fusion), channel_id=1, source_target_pairs={{0,1},{1,0},{2,3},{3,2},{4,5},{5,4},{6,7},{7,6},{8,9},{9,8},{10,11... | collective-permute-start | bytes 1572872 | tf_op jit(solution)/shard_map/ppermute | solution.py:142
  218.6 19.0 %all-to-all-start = ((f32[64,4,512]{2,1,0:T(4,128)}), f32[64,4,512]{2,1,0:T(4,128)}, u32[]{:S(2)}, u32[]{:S(2)}) async-start(f32[64,4,512]{2,1,0:T(4,128)} %reshape.129), calls=%async_computation | async-start | bytes 1048576 | tf_op jit(solution)/shard_map/all_to_all | solution.py:209
  237.6 16.1 %all-to-all-start.2 = ((f32[64,4,512]{2,1,0:T(4,128)}), f32[64,4,512]{2,1,0:T(4,128)}, u32[]{:S(2)}, u32[]{:S(2)}) async-start(f32[64,4,512]{2,1,0:T(4,128)} %reshape.131), calls=%async_computation.2 | async-start | bytes 1048576 | tf_op jit(solution)/shard_map/all_to_all | solution.py:209
  243.1 47.8 %copy-start.6 = (f32[256,512]{1,0:T(8,128)S(1)}, f32[256,512]{1,0:T(8,128)}, u32[]{:S(2)}) copy-start(f32[256,512]{1,0:T(8,128)} %copy-done.5) | copy-start | bytes 1572868
  243.1 47.8 %copy-start.8 = (f32[256,512]{1,0:T(8,128)S(1)}, f32[256,512]{1,0:T(8,128)}, u32[]{:S(2)}) copy-start(f32[256,512]{1,0:T(8,128)} %copy-done.7) | copy-start | bytes 1572868
  254.5 14.5 %all-to-all-start.1 = ((bf16[64,4,512]{2,1,0:T(4,128)(2,1)}), bf16[64,4,512]{2,1,0:T(4,128)(2,1)S(1)}, u32[]{:S(2)}, u32[]{:S(2)}) async-start(bf16[64,4,512]{2,1,0:T(4,128)(2,1)} %broadcast_in_dim.42), calls=%async_computation.1 | async-start | bytes 524288 | tf_op jit(solution)/shard_map/all_to_all | solution.py:211
  269.7 14.6 %all-to-all-start.3 = ((bf16[64,4,512]{2,1,0:T(4,128)(2,1)}), bf16[64,4,512]{2,1,0:T(4,128)(2,1)}, u32[]{:S(2)}, u32[]{:S(2)}) async-start(bf16[64,4,512]{2,1,0:T(4,128)(2,1)} %broadcast_in_dim.43), calls=%async_computation.3 | async-start | bytes 524288 | tf_op jit(solution)/shard_map/all_to_all | solution.py:211
  276.0 15.9 %copy-start.14 = (bf16[256,512]{1,0:T(8,128)(2,1)S(1)}, bf16[256,512]{1,0:T(8,128)(2,1)}, u32[]{:S(2)}) copy-start(bf16[256,512]{1,0:T(8,128)(2,1)} %reshape.130) | copy-start | bytes 786436
  276.0 15.9 %collective-permute-start.24 = (bf16[256,512]{1,0:T(8,128)(2,1)}, bf16[256,512]{1,0:T(8,128)(2,1)}, u32[]{:S(2)}, u32[]{:S(2)}) collective-permute-start(bf16[256,512]{1,0:T(8,128)(2,1)} %reshape.130), channel_id=1, source_target_pairs={{0,1},{1,0},{2,3},{3,2},{4,5},{5,4},{6,7},{7,6},{8,9},{9,8},{10,11... | collective-permute-start | bytes 786440 | tf_op jit(solution)/shard_map/ppermute | solution.py:142
  286.0 6.9 %copy-start.15 = (bf16[256,512]{1,0:T(8,128)(2,1)S(1)}, bf16[256,512]{1,0:T(8,128)(2,1)}, u32[]{:S(2)}) copy-start(bf16[256,512]{1,0:T(8,128)(2,1)} %reshape.132) | copy-start | bytes 786436
  286.0 6.9 %collective-permute-start.26 = (bf16[256,512]{1,0:T(8,128)(2,1)}, bf16[256,512]{1,0:T(8,128)(2,1)S(1)}, u32[]{:S(2)}, u32[]{:S(2)}) collective-permute-start(bf16[256,512]{1,0:T(8,128)(2,1)} %reshape.132), channel_id=1, source_target_pairs={{0,1},{1,0},{2,3},{3,2},{4,5},{5,4},{6,7},{7,6},{8,9},{9,8},{10,11... | collective-permute-start | bytes 786440 | tf_op jit(solution)/shard_map/ppermute | solution.py:142

commit v2 on v1

--- a/solution.py
+++ b/solution.py
@@ -151,8 +151,7 @@
     )
 
 
-def product_kernel(order_ref, place_ref, *refs):
-    tiles, (*pieces, out_ref, columns_ref) = refs[:GROUP], refs[GROUP:]
+def fill_columns(place_ref, pieces, columns_ref):
     rows = pieces[0].shape[1]
 
     @pl.when(pl.program_id(0) == 0)
@@ -164,12 +163,31 @@
                 columns_ref[pl.ds(start, rows), :] = piece[part]
                 slot += 1
 
+
+def tile_product(tiles, columns_ref):
     tile = jnp.concatenate([ref[0] for ref in tiles], axis=0)
     out = jnp.dot(tile, columns_ref[...], preferred_element_type=jnp.float32)
-    out_ref[...] = out.astype(out_ref.dtype).reshape(out_ref.shape)
-
-
-def product(tile, pieces, order, place, dtype):
+    return out.reshape(GROUP, -1, out.shape[1])
+
+
+def given_kernel(order_ref, place_ref, *refs):
+    tiles, (*pieces, out_ref, columns_ref) = refs[:GROUP], refs[GROUP:]
+    fill_columns(place_ref, pieces, columns_ref)
+    out_ref[...] = tile_product(tiles, columns_ref).astype(out_ref.dtype)
+
+
+def mine_kernel(order_ref, place_ref, *refs):
+    tiles, (*pieces, other_ref, o0, o1, o2, o3, columns_ref) = refs[:GROUP], refs[GROUP:]
+    fill_columns(place_ref, pieces, columns_ref)
+    both = tile_product(tiles, columns_ref) + other_ref[...].astype(jnp.float32)
+    for d, out_ref in enumerate((o0, o1, o2, o3)):
+
+        @pl.when(pl.program_id(0) == d)
+        def _(out_ref=out_ref):
+            out_ref[...] = both.astype(out_ref.dtype)
+
+
+def product(tile, pieces, order, place, other=None):
     blocks = order.shape[0]
     _, rows, depth = tile.shape
     width = pieces[0].shape[2]
@@ -179,25 +197,40 @@
             (1, rows, depth), lambda i, order, place: (order[GROUP * i + member], 0, 0)
         )
 
+    whole = lambda i, order, place: (0, 0, 0)
+    step = pl.BlockSpec((GROUP, rows, width), lambda i, order, place: (i, 0, 0))
+    in_specs = [tile_spec(member) for member in range(GROUP)]
+    in_specs += [pl.BlockSpec(p.shape, whole) for p in pieces]
+    operands = [tile] * GROUP + list(pieces)
+    if other is None:
+        kernel, out_specs = given_kernel, step
+        out_shape = jax.ShapeDtypeStruct((blocks, rows, width), jnp.bfloat16)
+    else:
+        kernel, out_specs = mine_kernel, [pl.BlockSpec((GROUP, rows, width), whole)] * 4
+        out_shape = [
+            jax.ShapeDtypeStruct((GROUP, rows, width), dtype)
+            for dtype in (jnp.float32, jnp.bfloat16, jnp.bfloat16, jnp.bfloat16)
+        ]
+        in_specs.append(step)
+        operands.append(other)
     return pl.pallas_call(
-        product_kernel,
-        out_shape=jax.ShapeDtypeStruct((blocks, rows, width), dtype),
+        kernel,
+        out_shape=out_shape,
         grid_spec=pltpu.PrefetchScalarGridSpec(
             num_scalar_prefetch=2,
             grid=(blocks // GROUP,),
-            in_specs=[tile_spec(member) for member in range(GROUP)]
-            + [pl.BlockSpec(p.shape, lambda i, order, place: (0, 0, 0)) for p in pieces],
-            out_specs=pl.BlockSpec((GROUP, rows, width), lambda i, order, place: (i, 0, 0)),
+            in_specs=in_specs,
+            out_specs=out_specs,
             scratch_shapes=[pltpu.VMEM((depth, width), jnp.bfloat16)],
         ),
-        compiler_params=pltpu.CompilerParams(vmem_limit_bytes=60 * 2**20),
+        compiler_params=pltpu.CompilerParams(vmem_limit_bytes=50 * 2**20),
         cost_estimate=pl.CostEstimate(
             flops=2 * blocks * rows * depth * width,
             bytes_accessed=2 * blocks * rows * depth + 2 * depth * width,
             transcendentals=0,
         ),
         name="product",
-    )(order, place, *[tile] * GROUP, *pieces)
+    )(order, place, *operands)
 
 
 def total(term):
@@ -206,8 +239,9 @@
     chips = 64
     low, high = term[:half], term[half:]
     part = jnp.where(core == 0, low, high) + shift(jnp.where(core == 0, high, low), core=1)
-    slices = lax.all_to_all(part.reshape(chips, half // chips, -1), CHIPS, 0, 0)
-    summed = jnp.sum(slices, axis=0, keepdims=True).astype(jnp.bfloat16)
+    slices = part.astype(jnp.bfloat16).reshape(chips, half // chips, -1)
+    slices = lax.all_to_all(slices, CHIPS, 0, 0)
+    summed = jnp.sum(slices.astype(jnp.float32), axis=0, keepdims=True).astype(jnp.bfloat16)
     spread = lax.all_to_all(jnp.broadcast_to(summed, slices.shape), CHIPS, 0, 0)
     own = spread.reshape(half, -1)
     other = shift(own, core=1)
@@ -225,51 +259,68 @@
     steps = [(d, e) for d in range(4) for e in range(2)]
     kept = jnp.stack([(z_lo ^ e) * 8 + (y + d) % 4 * 2 + core for d, e in steps]).astype(jnp.int32)
 
-    seeds = [seed(masked[0], flip) for flip in range(2)]
-    along = [masked[1]] + [shift(masked[1], x=d) for d in (1, 2, 3)]
+    seeds = []
+    for flip in range(2):
+        seeds.append(seed(masked[0], flip))
+    crossed = send(
+        masked[1], lambda z_hi, x, z_lo, y, core: dict(z_hi=z_lo, z_lo=z_hi)
+    )
+    along = [crossed]
+    for d in (1, 2, 3):
+        along.append(shift(crossed, x=d))
 
     state = eliminate(0, diag_blocks, pivot_flags)
-    state = eliminate(1, state, pivot_flags)
 
     pair = after(jnp.stack(seeds), state)
-    first = [pair] + [shift(pair, x=d) for d in (1, 2, 3)]
+    first = [pair]
+    for d in (1, 2, 3):
+        first.append(shift(pair, x=d))
     first_place = jnp.stack([(z_hi ^ e) * 4 + (x - d) % 4 for d, e in steps]).astype(jnp.int32)
 
-    stacked = after(jnp.stack(along), state)
+    stacked = after(jnp.stack(along), pair)
     turned = []
     for d in range(4):
         part = lax.dynamic_index_in_dim(stacked, (x - y - d) % 4, 0, keepdims=False)
         turned.append(shift(part, y=d) if d else part)
 
-    state = eliminate(2, after(state, pair, stacked), pivot_flags)
+    state = eliminate(1, after(state, pair, stacked), pivot_flags)
     quad = after(jnp.stack(turned), state)
     second = []
     for flip in range(2):
         second.append(
-            send(quad, lambda z_hi, x, z_lo, y, core: dict(z_hi=core ^ flip, z_lo=z_hi, core=z_lo))
+            send(
+                quad,
+                lambda z_hi, x, z_lo, y, core: dict(z_hi=core ^ flip, core=z_hi),
+            )
         )
     second_place = jnp.stack(
         [(y - d) % 4 * 2 + (z_hi ^ flip) for flip in range(2) for d in range(4)]
     ).astype(jnp.int32)
-    inverses = eliminate(3, after(state, quad), pivot_flags)
 
     pieces = [first, second]
     places = [first_place, second_place]
-    order = after(kept, inverses)
-    applied, terms = [], []
+    swapped = []
+    order = after(kept, quad)
     for k in range(nodes):
-        given = product(tile, pieces[k], order ^ 1, places[k], jnp.bfloat16)
-        other = shift(given, core=1)
-        mine = product(tile, pieces[k], order, places[k], jnp.float32)
-        both = mine + other.astype(jnp.float32)
-        leaving = [both[2 * d : 2 * d + 2].astype(jnp.bfloat16) for d in (1, 2, 3)]
+        given = product(tile, pieces[k], order ^ 1, places[k])
+        swapped.append(shift(given, core=1))
+        order = after(kept, given)
+    sums = []
+    for k in range(nodes):
+        staying, *leaving = product(tile, pieces[k], order, places[k], swapped[k])
         order = after(kept, *leaving)
-        summed = both[0:2]
+        summed = staying
         for d, part in zip((1, 2, 3), leaving):
             arrived = shift(part, y=d)
             summed = summed + arrived.astype(jnp.float32)
-        summed = summed[0] + shift(summed[1].astype(jnp.bfloat16), z_lo=1).astype(jnp.float32)
-        applied.append(jnp.dot(summed, inverses[k], precision=HIGHEST))
+        arrived = shift(summed[1].astype(jnp.bfloat16), z_lo=1)
+        sums.append(summed[0] + arrived.astype(jnp.float32))
+
+    state = eliminate(2, after(state, *leaving), pivot_flags)
+    inverses = eliminate(3, state, pivot_flags)
+    applied, terms = [], []
+    for k in range(nodes):
+        applied.append(jnp.dot(sums[k], inverses[k], precision=HIGHEST))
         normed = jnp.dot(masked[k].astype(jnp.float32), inverses[k], precision=HIGHEST)
         terms.append(
             lax.dot_general(
@@ -280,11 +331,8 @@
                 preferred_element_type=jnp.float32,
             )
         )
-        last = leaving
-    totals = [total(after(terms[0], *last)), total(terms[1])]
-    inverse_diagonal = jnp.stack(
-        [inverses[k] + totals[k].astype(jnp.float32) for k in range(nodes)]
-    )
+    totals = total(jnp.concatenate(terms)).astype(jnp.float32).reshape(inverses.shape)
+    inverse_diagonal = inverses + totals
     inverse_panel = (-jnp.stack(applied)).astype(jnp.bfloat16)
     return (inverse_panel, inverse_diagonal)
 

time: 297 us -> 249 us (0.84)
  starting transfers between devices: 91.2 us -> 53.3 us
  blocking collectives: 0 us -> 35.8 us
  other arithmetic: 27.1 us -> 9.68 us
  waiting for transfers between devices: 77.6 us -> 64.9 us
  local copies, waits for them, and re-layouts: 15.2 us -> 5.68 us
  Pallas kernels: 76.6 us -> 73.5 us
    all_to_all x0 -> x2, blocking collectives: none -> 35.8 us  [the longest x1 20 us: total(): slices = lax.all_to_all(slices, CHIPS, 0, 0)]
    all_to_all x4 -> x0, waiting for transfers between devices: 30.1 us -> none  [the longest x2 17.4 us: total(): slices = lax.all_to_all(part.reshape(chips, half // chips, -1), CHIPS, 0, 0)]
    all_to_all x4 -> x0, starting transfers between devices: 23 us -> none  [the longest x2 12.3 us: total(): slices = lax.all_to_all(part.reshape(chips, half // chips, -1), CHIPS, 0, 0)]
    ppermute x27 -> x26, waiting for transfers between devices: 47.5 us -> 64.9 us  [send(): return lax.ppermute(value, AXES, moves)]
    ppermute x27 -> x26, starting transfers between devices: 68.3 us -> 53.3 us  [send(): return lax.ppermute(value, AXES, moves)]
    another operation x4 -> x1, other arithmetic: 11.1 us -> 0.13 us  [invert(): stacked = after(jnp.stack(along), pair)]
    reshape x4 -> x0, local copies, waits for them, and re-layouts: 6.5 us -> none  [the longest x2 4.02 us: total(): slices = lax.all_to_all(part.reshape(chips, half // chips, -1), CHIPS, 0, 0)]
    pallas_call x4, Pallas kernels: 38.7 us -> 35.5 us  [product(): pl.pallas_call(kernel, out_shape=out_shape, grid_spec=pltpu.PrefetchScala...]
  transfers between devices with their start and end apart: 31 -> 26, of which waited for: 13 -> 11; matrix products, arithmetic and copies ran while one was open for 13% -> 3% of each run, Pallas kernels for 20% -> 26%
where the time goes in v2:
time: 249 us
  Pallas kernels  73.5 us (30%)
  waiting for transfers between devices  64.9 us (26%)
  starting transfers between devices  53.3 us (21%)
  blocking collectives  35.8 us (14%)
  other arithmetic  9.68 us (4%)
  local copies, waits for them, and re-layouts  5.68 us (2%)
  matrix products  4.91 us (2%)
    ppermute x26, waiting for transfers between devices, send(): return lax.ppermute(value, AXES, moves)  64.9 us
    ppermute x26, starting transfers between devices, send(): return lax.ppermute(value, AXES, moves)  53.3 us
    pallas_call x4, Pallas kernels, eliminate(): pl.pallas_call(functools.partial(inverse_kernel, block), out_shape=jax.Sh...  37.9 us
    pallas_call x4, Pallas kernels, product(): pl.pallas_call(kernel, out_shape=out_shape, grid_spec=pltpu.PrefetchScala...  35.5 us
    all_to_all x1, blocking collectives, total(): slices = lax.all_to_all(slices, CHIPS, 0, 0)  20 us
    all_to_all x1, blocking collectives, total(): spread = lax.all_to_all(jnp.broadcast_to(summed, slices.shape), CHIPS, 0, 0)  15.8 us
    unnamed x26, local copies, waits for them, and re-layouts  5.23 us
  transfers between devices with their start and end apart: 26, of which 11 were waited for; matrix products, arithmetic and copies ran while one was open for 3% of the time, Pallas kernels for 26%

profile of v2, /device:TPU:1, one launch (start us, length us, event | category | flops | bytes accessed | tf_op | source)
XLA Modules:
  0.0 248.8 jit_solution(17046722040770675639)
XLA Ops:
  0.6 0.8 compare_reduce_fusion.1
  1.4 1.2 bitcast_select_fusion.1
  2.6 0.7 collective-permute-start
  3.3 7.3 %collective-permute-start.5 = (bf16[256,512]{1,0:T(8,128)(2,1)S(1)}, bf16[256,512]{1,0:T(8,128)(2,1)S(1)}, u32[]{:S(2)}, u32[]{:S(2)}) collective-permute-start(bf16[256,512]{1,0:T(8,128)(2,1)S(1)} %get-tuple-element.45), channel_id=1, source_target_pairs={{0,64},{1,80},{2,96},{3,112},{4,0},{5,16},{6,32},{7,48},{8,65},{9,... | collective-permute-start | bytes 786440 | tf_op jit(solution)/shard_map/ppermute | solution.py:142
  10.6 3.4 %collective-permute-start.4 = (bf16[256,512]{1,0:T(8,128)(2,1)S(1)}, bf16[256,512]{1,0:T(8,128)(2,1)S(1)}, u32[]{:S(2)}, u32[]{:S(2)}) collective-permute-start(bf16[256,512]{1,0:T(8,128)(2,1)S(1)} %get-tuple-element.45), channel_id=1, source_target_pairs={{0,0},{1,16},{2,32},{3,48},{4,64},{5,80},{6,96},{7,112},{8,1},{9,1... | collective-permute-start | bytes 786440 | tf_op jit(solution)/shard_map/ppermute | solution.py:142
  14.0 3.4 %collective-permute-start.3 = (bf16[256,512]{1,0:T(8,128)(2,1)S(1)}, bf16[256,512]{1,0:T(8,128)(2,1)S(1)}, u32[]{:S(2)}, u32[]{:S(2)}) collective-permute-start(bf16[256,512]{1,0:T(8,128)(2,1)S(1)} %collective-permute-done), channel_id=1, source_target_pairs={{0,48},{1,49},{2,50},{3,51},{4,52},{5,53},{6,54},{7,55},{8,56},{9,... | collective-permute-start | bytes 786440 | tf_op jit(solution)/shard_map/ppermute | solution.py:142
  17.4 0.7 collective-permute-start.1
  18.1 1.6 copy-done.5
  19.7 0.7 copy-done.6
  20.4 9.6 %eliminate.4.in_ref = f32[2,512,512]{2,1,0:T(8,128)S(1)} custom-call(f32[2,512,512]{2,1,0:T(8,128)S(1)} %copy-done.5, s32[2,512]{1,0:T(2,128)S(1)} %copy-done.6), custom_call_target="tpu_custom_call" | custom-call | flops 5000000000 | bytes 4194304 | tf_op jit(solution)/shard_map/eliminate/pallas_call | solution.py:115
  30.0 1.3 copy-done.8
  31.3 2.4 collective-permute-done.1
  33.8 0.1 pad_maximum_fusion
  33.9 0.1 constant_dynamic-slice_fusion
  34.0 2.4 collective-permute-start.8
  36.6 3.1 %collective-permute-start.11 = (bf16[2,256,512]{2,1,0:T(8,128)(2,1)S(1)}, bf16[2,256,512]{2,1,0:T(8,128)(2,1)S(1)}, u32[]{:S(2)}, u32[]{:S(2)}) collective-permute-start(bf16[2,256,512]{2,1,0:T(8,128)(2,1)S(1)} %pad_maximum_fusion.3.refs_2_), channel_id=1, source_target_pairs={{0,48},{1,49},{2,50},{3,51},{4,52},{5,53},{6,54},{7,55},{8,56},{9,... | collective-permute-start | bytes 1572872 | tf_op jit(solution)/shard_map/ppermute | solution.py:142
  39.8 0.8 collective-permute-start.10
  40.6 1.5 collective-permute-start.7
  42.1 1.8 collective-permute-start.6
  43.9 1.6 copy-done.9
  45.5 9.5 %eliminate.5.in_ref = f32[2,512,512]{2,1,0:T(8,128)S(1)} custom-call(f32[2,512,512]{2,1,0:T(8,128)S(1)} %copy-done.9, s32[2,512]{1,0:T(2,128)S(1)} %copy-done.7), custom_call_target="tpu_custom_call" | custom-call | flops 5000000000 | bytes 4194304 | tf_op jit(solution)/shard_map/eliminate/pallas_call | solution.py:115
  55.0 1.3 pad_maximum_fusion.1
  56.3 6.0 %collective-permute-done.11.refs_5_ = bf16[2,256,512]{2,1,0:T(8,128)(2,1)S(1)} collective-permute-done((bf16[2,256,512]{2,1,0:T(8,128)(2,1)S(1)}, bf16[2,256,512]{2,1,0:T(8,128)(2,1)S(1)}, u32[]{:S(2)}, u32[]{:S(2)}) %collective-permute-start.11) | collective-permute-done | bytes 524320 | tf_op jit(solution)/shard_map/ppermute | solution.py:142
  62.4 4.0 %collective-permute-done.9.refs_3_ = bf16[2,256,512]{2,1,0:T(8,128)(2,1)S(1)} collective-permute-done((bf16[2,256,512]{2,1,0:T(8,128)(2,1)S(1)}, bf16[2,256,512]{2,1,0:T(8,128)(2,1)S(1)}, u32[]{:S(2)}, u32[]{:S(2)}) %collective-permute-start.9) | collective-permute-done | bytes 524320 | tf_op jit(solution)/shard_map/ppermute | solution.py:142
  66.3 8.7 %product.4 = bf16[8,256,512]{2,1,0:T(8,128)(2,1)} custom-call(s32[8]{0:T(128)S(1)} %broadcast_xor_fusion.1.order_ref, s32[8]{0:T(128)S(1)} %stack.156.place_ref, bf16[16,256,2048]{2,1,0:T(8,128)(2,1)} %bitcast.85, bf16[16,256,2048]{2,1,0:T(8,128)(2,1)} %bitcast.86, bf16[2,256,512]{2,1,0:T(8,128)(2,1)S(1)} %pad_maximum_fusion.3.refs_2_, ...), custom_call_target="tpu_custom_call" | custom-call | flops 4294967296 | bytes 10485760 | tf_op jit(solution)/shard_map/product/pallas_call | solution.py:216
  75.1 0.6 collective-permute-start.14
  75.6 0.1 collective-permute-start.13
  75.7 9.5 %collective-permute-start.12 = (bf16[4,256,512]{2,1,0:T(8,128)(2,1)}, bf16[4,256,512]{2,1,0:T(8,128)(2,1)S(1)}, u32[]{:S(2)}, u32[]{:S(2)}) collective-permute-start(bf16[4,256,512]{2,1,0:T(8,128)(2,1)} %pad_maximum_fusion.1), channel_id=1, source_target_pairs={{0,0},{1,64},{2,2},{3,66},{4,4},{5,68},{6,6},{7,70},{8,8},{9,72},{... | collective-permute-start | bytes 3145736 | tf_op jit(solution)/shard_map/ppermute | solution.py:142
  85.4 18.6 %collective-permute-done.13.refs_3_ = bf16[4,256,512]{2,1,0:T(8,128)(2,1)S(1)} collective-permute-done((bf16[4,256,512]{2,1,0:T(8,128)(2,1)}, bf16[4,256,512]{2,1,0:T(8,128)(2,1)S(1)}, u32[]{:S(2)}, u32[]{:S(2)}) %collective-permute-start.13) | collective-permute-done | bytes 1048608 | tf_op jit(solution)/shard_map/ppermute | solution.py:142
  104.0 2.8 %collective-permute-done.12.refs_2_ = bf16[4,256,512]{2,1,0:T(8,128)(2,1)S(1)} collective-permute-done((bf16[4,256,512]{2,1,0:T(8,128)(2,1)}, bf16[4,256,512]{2,1,0:T(8,128)(2,1)S(1)}, u32[]{:S(2)}, u32[]{:S(2)}) %collective-permute-start.12) | collective-permute-done | bytes 1048608 | tf_op jit(solution)/shard_map/ppermute | solution.py:142
  106.8 8.7 %product.5 = bf16[8,256,512]{2,1,0:T(8,128)(2,1)} custom-call(s32[8]{0:T(128)S(1)} %broadcast_xor_fusion.order_ref, s32[8]{0:T(128)S(1)} %stack.165.place_ref, bf16[16,256,2048]{2,1,0:T(8,128)(2,1)} %bitcast.87, bf16[16,256,2048]{2,1,0:T(8,128)(2,1)} %bitcast.88, bf16[4,256,512]{2,1,0:T(8,128)(2,1)S(1)} %collective-permute-done.12.refs_2_, ...), custom_call_target="tpu_custom_call" | custom-call | flops 4294967296 | bytes 10485760 | tf_op jit(solution)/shard_map/product/pallas_call | solution.py:216
  115.6 9.3 %product.6 = (f32[2,256,512]{2,1,0:T(8,128)}, bf16[2,256,512]{2,1,0:T(8,128)(2,1)}, bf16[2,256,512]{2,1,0:T(8,128)(2,1)S(1)}, bf16[2,256,512]{2,1,0:T(8,128)(2,1)S(1)}) custom-call(s32[8]{0:T(128)S(1)} %stack.135.order_ref, s32[8]{0:T(128)S(1)} %stack.156.place_ref, bf16[16,256,2048]{2,1,0:T(8,128)(2,1)} %bitcast.89, bf16[16,256,2048]{2,1,0:T(8,128)(2,1)} %bitcast.90, ...), custom_call_target="tpu_custom_call" | custom-call | flops 4294967296 | bytes 10485760 | tf_op jit(solution)/shard_map/product/pallas_call | solution.py:216
  124.8 0.9 collective-permute-start.15
  125.7 3.2 %collective-permute-start.16 = (bf16[2,256,512]{2,1,0:T(8,128)(2,1)S(1)}, bf16[2,256,512]{2,1,0:T(8,128)(2,1)S(1)}, u32[]{:S(2)}, u32[]{:S(2)}) collective-permute-start(bf16[2,256,512]{2,1,0:T(8,128)(2,1)S(1)} %get-tuple-element.28), channel_id=1, source_target_pairs={{0,4},{1,5},{2,6},{3,7},{4,0},{5,1},{6,2},{7,3},{8,12},{9,13},{10,... | collective-permute-start | bytes 1572872 | tf_op jit(solution)/shard_map/ppermute | solution.py:142
  128.9 0.8 collective-permute-start.17
  129.7 10.0 %collective-permute-done.15 = bf16[2,256,512]{2,1,0:T(8,128)(2,1)S(1)} collective-permute-done((bf16[2,256,512]{2,1,0:T(8,128)(2,1)}, bf16[2,256,512]{2,1,0:T(8,128)(2,1)S(1)}, u32[]{:S(2)}, u32[]{:S(2)}) %collective-permute-start.15) | collective-permute-done | bytes 524320 | tf_op jit(solution)/shard_map/ppermute | solution.py:142
  139.7 12.2 %collective-permute-done.16 = bf16[2,256,512]{2,1,0:T(8,128)(2,1)S(1)} collective-permute-done((bf16[2,256,512]{2,1,0:T(8,128)(2,1)S(1)}, bf16[2,256,512]{2,1,0:T(8,128)(2,1)S(1)}, u32[]{:S(2)}, u32[]{:S(2)}) %collective-permute-start.16) | collective-permute-done | bytes 524320 | tf_op jit(solution)/shard_map/ppermute | solution.py:142
  151.9 1.7 convert_add_fusion.2
  153.6 2.0 collective-permute-start.18
  155.6 8.8 %product.7 = (f32[2,256,512]{2,1,0:T(8,128)S(1)}, bf16[2,256,512]{2,1,0:T(8,128)(2,1)S(1)}, bf16[2,256,512]{2,1,0:T(8,128)(2,1)S(1)}, bf16[2,256,512]{2,1,0:T(8,128)(2,1)S(1)}) custom-call(s32[8]{0:T(128)S(1)} %stack.135.order_ref, s32[8]{0:T(128)S(1)} %stack.165.place_ref, bf16[16,256,2048]{2,1,0:T(8,128)(2,1)} %bitcast.91, ...), custom_call_target="tpu_custom_call" | custom-call | flops 4294967296 | bytes 10485760 | tf_op jit(solution)/shard_map/product/pallas_call | solution.py:216
  164.4 1.3 collective-permute-start.20
  165.7 3.1 %collective-permute-start.21 = (bf16[2,256,512]{2,1,0:T(8,128)(2,1)S(1)}, bf16[2,256,512]{2,1,0:T(8,128)(2,1)S(1)}, u32[]{:S(2)}, u32[]{:S(2)}) collective-permute-start(bf16[2,256,512]{2,1,0:T(8,128)(2,1)S(1)} %get-tuple-element.32), channel_id=1, source_target_pairs={{0,4},{1,5},{2,6},{3,7},{4,0},{5,1},{6,2},{7,3},{8,12},{9,13},{10,... | collective-permute-start | bytes 1572872 | tf_op jit(solution)/shard_map/ppermute | solution.py:142
  168.8 9.5 %eliminate.6.in_ref = f32[2,512,512]{2,1,0:T(8,128)S(1)} custom-call(f32[2,512,512]{2,1,0:T(8,128)S(1)} %copy-done.11, s32[2,512]{1,0:T(2,128)S(1)} %copy-done.7), custom_call_target="tpu_custom_call" | custom-call | flops 5000000000 | bytes 4194304 | tf_op jit(solution)/shard_map/eliminate/pallas_call | solution.py:115
  178.3 9.5 %eliminate.7 = f32[2,512,512]{2,1,0:T(8,128)S(1)} custom-call(f32[2,512,512]{2,1,0:T(8,128)S(1)} %eliminate.6.in_ref, s32[2,512]{1,0:T(2,128)S(1)} %copy-done.7), custom_call_target="tpu_custom_call" | custom-call | flops 5000000000 | bytes 4194304 | tf_op jit(solution)/shard_map/eliminate/pallas_call | solution.py:115
  187.8 1.1 fusion.1
  188.9 0.7 convolution_convert_fusion.1
  189.6 0.7 fusion.24
  190.3 0.9 collective-permute-done.21
  191.2 0.3 convert_add_fusion.1
  191.5 0.6 collective-permute-start.23
  192.1 0.7 convolution_convert_fusion
  192.8 5.1 %collective-permute-done.23 = bf16[256,512]{1,0:T(8,128)(2,1)S(1)} collective-permute-done((bf16[256,512]{1,0:T(8,128)(2,1)S(1)}, bf16[256,512]{1,0:T(8,128)(2,1)S(1)}, u32[]{:S(2)}, u32[]{:S(2)}) %collective-permute-start.23) | collective-permute-done | bytes 262176 | tf_op jit(solution)/shard_map/ppermute | solution.py:142
  197.9 1.1 fusion.2
  199.0 0.7 broadcast_select_fusion.2
  199.6 2.7 %collective-permute-start.24 = (f32[512,512]{1,0:T(8,128)S(1)}, f32[512,512]{1,0:T(8,128)S(1)}, u32[]{:S(2)}, u32[]{:S(2)}) collective-permute-start(f32[512,512]{1,0:T(8,128)S(1)} %get-tuple-element.46), channel_id=1, source_target_pairs={{0,1},{1,0},{2,3},{3,2},{4,5},{5,4},{6,7},{7,6},{8,9},{9,8},{10,11... | collective-permute-start | bytes 3145736 | tf_op jit(solution)/shard_map/ppermute | solution.py:142
  202.3 2.3 collective-permute-done.24
  204.6 0.4 fusion.3
  205.0 20.0 %all_to_all.10 = bf16[64,8,512]{2,1,0:T(8,128)(2,1)} all-to-all(bf16[64,8,512]{2,1,0:T(8,128)(2,1)S(1)} %fusion.3), channel_id=1, replica_groups=mesh['z_hi'=2,'x'=4,'z_lo'=2,'y'=4,'core'=2] {'z_hi','x','z_lo','y'}, dimensions={0} | all-to-all | bytes 1048576 | tf_op jit(solution)/shard_map/all_to_all | solution.py:243
  225.0 1.1 reduce_sum.12
  226.2 15.8 %all_to_all.11 = bf16[64,8,512]{2,1,0:T(8,128)(2,1)S(1)} all-to-all(bf16[64,8,512]{2,1,0:T(8,128)(2,1)S(1)} %broadcast_in_dim.36), channel_id=1, replica_groups=mesh['z_hi'=2,'x'=4,'z_lo'=2,'y'=4,'core'=2] {'z_hi','x','z_lo','y'}, dimensions={0} | all-to-all | bytes 1048576 | tf_op jit(solution)/shard_map/all_to_all | solution.py:245
  242.0 3.3 %collective-permute-start.25 = (bf16[512,512]{1,0:T(8,128)(2,1)S(1)}, bf16[512,512]{1,0:T(8,128)(2,1)S(1)}, u32[]{:S(2)}, u32[]{:S(2)}) collective-permute-start(bf16[512,512]{1,0:T(8,128)(2,1)S(1)} %bitcast.96), channel_id=1, source_target_pairs={{0,1},{1,0},{2,3},{3,2},{4,5},{5,4},{6,7},{7,6},{8,9},{9,8},{10,11... | collective-permute-start | bytes 1572872 | tf_op jit(solution)/shard_map/ppermute | solution.py:142
  245.3 0.9 fusion
  246.3 0.6 collective-permute-done.25
  247.0 1.7 convert_add_fusion
  (52 shorter events, 0.7 us)
Async XLA Ops:
  2.6 11.5 %collective-permute-start = (bf16[256,512]{1,0:T(8,128)(2,1)S(1)}, bf16[256,512]{1,0:T(8,128)(2,1)S(1)}, u32[]{:S(2)}, u32[]{:S(2)}) collective-permute-start(bf16[256,512]{1,0:T(8,128)(2,1)S(1)} %get-tuple-element.44), channel_id=1, source_target_pairs={{0,0},{1,1},{2,2},{3,3},{4,4},{5,5},{6,6},{7,7},{8,64},{9,65},{10,... | collective-permute-start | bytes 786440 | tf_op jit(solution)/shard_map/ppermute | solution.py:142
  3.3 28.0 %collective-permute-start.5 = (bf16[256,512]{1,0:T(8,128)(2,1)S(1)}, bf16[256,512]{1,0:T(8,128)(2,1)S(1)}, u32[]{:S(2)}, u32[]{:S(2)}) collective-permute-start(bf16[256,512]{1,0:T(8,128)(2,1)S(1)} %get-tuple-element.45), channel_id=1, source_target_pairs={{0,64},{1,80},{2,96},{3,112},{4,0},{5,16},{6,32},{7,48},{8,65},{9,... | collective-permute-start | bytes 786440 | tf_op jit(solution)/shard_map/ppermute | solution.py:142
  10.6 20.7 %collective-permute-start.4 = (bf16[256,512]{1,0:T(8,128)(2,1)S(1)}, bf16[256,512]{1,0:T(8,128)(2,1)S(1)}, u32[]{:S(2)}, u32[]{:S(2)}) collective-permute-start(bf16[256,512]{1,0:T(8,128)(2,1)S(1)} %get-tuple-element.45), channel_id=1, source_target_pairs={{0,0},{1,16},{2,32},{3,48},{4,64},{5,80},{6,96},{7,112},{8,1},{9,1... | collective-permute-start | bytes 786440 | tf_op jit(solution)/shard_map/ppermute | solution.py:142
  14.0 17.3 %collective-permute-start.3 = (bf16[256,512]{1,0:T(8,128)(2,1)S(1)}, bf16[256,512]{1,0:T(8,128)(2,1)S(1)}, u32[]{:S(2)}, u32[]{:S(2)}) collective-permute-start(bf16[256,512]{1,0:T(8,128)(2,1)S(1)} %collective-permute-done), channel_id=1, source_target_pairs={{0,48},{1,49},{2,50},{3,51},{4,52},{5,53},{6,54},{7,55},{8,56},{9,... | collective-permute-start | bytes 786440 | tf_op jit(solution)/shard_map/ppermute | solution.py:142
  17.4 13.9 %collective-permute-start.2 = (bf16[256,512]{1,0:T(8,128)(2,1)S(1)}, bf16[256,512]{1,0:T(8,128)(2,1)S(1)}, u32[]{:S(2)}, u32[]{:S(2)}) collective-permute-start(bf16[256,512]{1,0:T(8,128)(2,1)S(1)} %collective-permute-done), channel_id=1, source_target_pairs={{0,32},{1,33},{2,34},{3,35},{4,36},{5,37},{6,38},{7,39},{8,40},{9,... | collective-permute-start | bytes 786440 | tf_op jit(solution)/shard_map/ppermute | solution.py:142
  17.4 16.4 %collective-permute-start.1 = (bf16[256,512]{1,0:T(8,128)(2,1)S(1)}, bf16[256,512]{1,0:T(8,128)(2,1)S(1)}, u32[]{:S(2)}, u32[]{:S(2)}) collective-permute-start(bf16[256,512]{1,0:T(8,128)(2,1)S(1)} %collective-permute-done), channel_id=1, source_target_pairs={{0,16},{1,17},{2,18},{3,19},{4,20},{5,21},{6,22},{7,23},{8,24},{9,... | collective-permute-start | bytes 786440 | tf_op jit(solution)/shard_map/ppermute | solution.py:142
  18.1 1.6 copy-start.5
  19.7 0.7 copy-start.6
  29.9 1.3 copy-start.8
  33.8 10.1 %copy-start.7 = (s32[2,512]{1,0:T(2,128)S(1)}, s32[2,512]{1,0:T(2,128)}, u32[]{:S(2)}) copy-start(s32[2,512]{1,0:T(2,128)} %flag_ref.7) | copy-start | bytes 12292
  34.0 8.1 %collective-permute-start.8 = (bf16[256,512]{1,0:T(8,128)(2,1)S(1)}, bf16[256,512]{1,0:T(8,128)(2,1)S(1)}, u32[]{:S(2)}, u32[]{:S(2)}) collective-permute-start(bf16[256,512]{1,0:T(8,128)(2,1)S(1)} %get-tuple-element.41), channel_id=1, source_target_pairs={{0,6},{1,7},{2,0},{3,1},{4,2},{5,3},{6,4},{7,5},{8,14},{9,15},{10,... | collective-permute-start | bytes 786440 | tf_op jit(solution)/shard_map/ppermute | solution.py:142
  36.6 25.7 %collective-permute-start.11 = (bf16[2,256,512]{2,1,0:T(8,128)(2,1)S(1)}, bf16[2,256,512]{2,1,0:T(8,128)(2,1)S(1)}, u32[]{:S(2)}, u32[]{:S(2)}) collective-permute-start(bf16[2,256,512]{2,1,0:T(8,128)(2,1)S(1)} %pad_maximum_fusion.3.refs_2_), channel_id=1, source_target_pairs={{0,48},{1,49},{2,50},{3,51},{4,52},{5,53},{6,54},{7,55},{8,56},{9,... | collective-permute-start | bytes 1572872 | tf_op jit(solution)/shard_map/ppermute | solution.py:142
  39.8 22.6 %collective-permute-start.10 = (bf16[2,256,512]{2,1,0:T(8,128)(2,1)S(1)}, bf16[2,256,512]{2,1,0:T(8,128)(2,1)S(1)}, u32[]{:S(2)}, u32[]{:S(2)}) collective-permute-start(bf16[2,256,512]{2,1,0:T(8,128)(2,1)S(1)} %pad_maximum_fusion.3.refs_2_), channel_id=1, source_target_pairs={{0,32},{1,33},{2,34},{3,35},{4,36},{5,37},{6,38},{7,39},{8,40},{9,... | collective-permute-start | bytes 1572872 | tf_op jit(solution)/shard_map/ppermute | solution.py:142
  40.6 25.8 %collective-permute-start.9 = (bf16[2,256,512]{2,1,0:T(8,128)(2,1)S(1)}, bf16[2,256,512]{2,1,0:T(8,128)(2,1)S(1)}, u32[]{:S(2)}, u32[]{:S(2)}) collective-permute-start(bf16[2,256,512]{2,1,0:T(8,128)(2,1)S(1)} %pad_maximum_fusion.3.refs_2_), channel_id=1, source_target_pairs={{0,16},{1,17},{2,18},{3,19},{4,20},{5,21},{6,22},{7,23},{8,24},{9,... | collective-permute-start | bytes 1572872 | tf_op jit(solution)/shard_map/ppermute | solution.py:142
  40.6 14.4 %collective-permute-start.7 = (bf16[256,512]{1,0:T(8,128)(2,1)S(1)}, bf16[256,512]{1,0:T(8,128)(2,1)S(1)}, u32[]{:S(2)}, u32[]{:S(2)}) collective-permute-start(bf16[256,512]{1,0:T(8,128)(2,1)S(1)} %get-tuple-element.42), channel_id=1, source_target_pairs={{0,4},{1,5},{2,6},{3,7},{4,0},{5,1},{6,2},{7,3},{8,12},{9,13},{10,... | collective-permute-start | bytes 786440 | tf_op jit(solution)/shard_map/ppermute | solution.py:142
  42.1 12.9 %collective-permute-start.6 = (bf16[256,512]{1,0:T(8,128)(2,1)S(1)}, bf16[256,512]{1,0:T(8,128)(2,1)S(1)}, u32[]{:S(2)}, u32[]{:S(2)}) collective-permute-start(bf16[256,512]{1,0:T(8,128)(2,1)S(1)} %get-tuple-element.43), channel_id=1, source_target_pairs={{0,2},{1,3},{2,4},{3,5},{4,6},{5,7},{6,0},{7,1},{8,10},{9,11},{10,... | collective-permute-start | bytes 786440 | tf_op jit(solution)/shard_map/ppermute | solution.py:142
  43.9 1.6 copy-start.9
  55.0 20.1 %copy-start.10 = (f32[2,512,512]{2,1,0:T(8,128)}, f32[2,512,512]{2,1,0:T(8,128)S(1)}, u32[]{:S(2)}) copy-start(f32[2,512,512]{2,1,0:T(8,128)S(1)} %eliminate.5.in_ref) | copy-start | bytes 6291460
  62.4 12.7 %copy-start.1 = (bf16[2,256,512]{2,1,0:T(8,128)(2,1)}, bf16[2,256,512]{2,1,0:T(8,128)(2,1)S(1)}, u32[]{:S(2)}) copy-start(bf16[2,256,512]{2,1,0:T(8,128)(2,1)S(1)} %collective-permute-done.10.refs_4_) | copy-start | bytes 1572868
  66.3 8.7 %copy-start.3 = (bf16[2,256,512]{2,1,0:T(8,128)(2,1)}, bf16[2,256,512]{2,1,0:T(8,128)(2,1)S(1)}, u32[]{:S(2)}) copy-start(bf16[2,256,512]{2,1,0:T(8,128)(2,1)S(1)} %collective-permute-done.9.refs_3_) | copy-start | bytes 1572868
  75.1 40.5 %collective-permute-start.14 = (bf16[8,256,512]{2,1,0:T(8,128)(2,1)}, bf16[8,256,512]{2,1,0:T(8,128)(2,1)}, u32[]{:S(2)}, u32[]{:S(2)}) collective-permute-start(bf16[8,256,512]{2,1,0:T(8,128)(2,1)} %product.4), channel_id=1, source_target_pairs={{0,1},{1,0},{2,3},{3,2},{4,5},{5,4},{6,7},{7,6},{8,9},{9,8},{10,11... | collective-permute-start | bytes 6291464 | tf_op jit(solution)/shard_map/ppermute | solution.py:142
  75.6 28.4 %collective-permute-start.13 = (bf16[4,256,512]{2,1,0:T(8,128)(2,1)}, bf16[4,256,512]{2,1,0:T(8,128)(2,1)S(1)}, u32[]{:S(2)}, u32[]{:S(2)}) collective-permute-start(bf16[4,256,512]{2,1,0:T(8,128)(2,1)} %pad_maximum_fusion.1), channel_id=1, source_target_pairs={{0,64},{1,0},{2,66},{3,2},{4,68},{5,4},{6,70},{7,6},{8,72},{9,8},{... | collective-permute-start | bytes 3145736 | tf_op jit(solution)/shard_map/ppermute | solution.py:142
  75.7 31.1 %collective-permute-start.12 = (bf16[4,256,512]{2,1,0:T(8,128)(2,1)}, bf16[4,256,512]{2,1,0:T(8,128)(2,1)S(1)}, u32[]{:S(2)}, u32[]{:S(2)}) collective-permute-start(bf16[4,256,512]{2,1,0:T(8,128)(2,1)} %pad_maximum_fusion.1), channel_id=1, source_target_pairs={{0,0},{1,64},{2,2},{3,66},{4,4},{5,68},{6,6},{7,70},{8,8},{9,72},{... | collective-permute-start | bytes 3145736 | tf_op jit(solution)/shard_map/ppermute | solution.py:142
  85.4 30.1 %copy-start.2 = (bf16[2,256,512]{2,1,0:T(8,128)(2,1)S(1)}, bf16[2,256,512]{2,1,0:T(8,128)(2,1)}, u32[]{:S(2)}) copy-start(bf16[2,256,512]{2,1,0:T(8,128)(2,1)} %copy-done.1) | copy-start | bytes 1572868
  85.4 30.1 %copy-start.4 = (bf16[2,256,512]{2,1,0:T(8,128)(2,1)S(1)}, bf16[2,256,512]{2,1,0:T(8,128)(2,1)}, u32[]{:S(2)}) copy-start(bf16[2,256,512]{2,1,0:T(8,128)(2,1)} %copy-done.3) | copy-start | bytes 1572868
  104.0 11.5 %copy-start = (bf16[4,256,512]{2,1,0:T(8,128)(2,1)}, bf16[4,256,512]{2,1,0:T(8,128)(2,1)S(1)}, u32[]{:S(2)}) copy-start(bf16[4,256,512]{2,1,0:T(8,128)(2,1)S(1)} %collective-permute-done.13.refs_3_) | copy-start | bytes 3145732
  115.5 40.1 %collective-permute-start.19 = (bf16[8,256,512]{2,1,0:T(8,128)(2,1)}, bf16[8,256,512]{2,1,0:T(8,128)(2,1)}, u32[]{:S(2)}, u32[]{:S(2)}) collective-permute-start(bf16[8,256,512]{2,1,0:T(8,128)(2,1)} %product.5), channel_id=1, source_target_pairs={{0,1},{1,0},{2,3},{3,2},{4,5},{5,4},{6,7},{7,6},{8,9},{9,8},{10,11... | collective-permute-start | bytes 6291464 | tf_op jit(solution)/shard_map/ppermute | solution.py:142
  124.8 14.8 %collective-permute-start.15 = (bf16[2,256,512]{2,1,0:T(8,128)(2,1)}, bf16[2,256,512]{2,1,0:T(8,128)(2,1)S(1)}, u32[]{:S(2)}, u32[]{:S(2)}) collective-permute-start(bf16[2,256,512]{2,1,0:T(8,128)(2,1)} %get-tuple-element.27), channel_id=1, source_target_pairs={{0,2},{1,3},{2,4},{3,5},{4,6},{5,7},{6,0},{7,1},{8,10},{9,11},{10,... | collective-permute-start | bytes 1572872 | tf_op jit(solution)/shard_map/ppermute | solution.py:142
  125.7 26.2 %collective-permute-start.16 = (bf16[2,256,512]{2,1,0:T(8,128)(2,1)S(1)}, bf16[2,256,512]{2,1,0:T(8,128)(2,1)S(1)}, u32[]{:S(2)}, u32[]{:S(2)}) collective-permute-start(bf16[2,256,512]{2,1,0:T(8,128)(2,1)S(1)} %get-tuple-element.28), channel_id=1, source_target_pairs={{0,4},{1,5},{2,6},{3,7},{4,0},{5,1},{6,2},{7,3},{8,12},{9,13},{10,... | collective-permute-start | bytes 1572872 | tf_op jit(solution)/shard_map/ppermute | solution.py:142
  128.9 23.0 %collective-permute-start.17 = (bf16[2,256,512]{2,1,0:T(8,128)(2,1)S(1)}, bf16[2,256,512]{2,1,0:T(8,128)(2,1)}, u32[]{:S(2)}, u32[]{:S(2)}) collective-permute-start(bf16[2,256,512]{2,1,0:T(8,128)(2,1)S(1)} %get-tuple-element.29), channel_id=1, source_target_pairs={{0,6},{1,7},{2,0},{3,1},{4,2},{5,3},{6,4},{7,5},{8,14},{9,15},{10,... | collective-permute-start | bytes 1572872 | tf_op jit(solution)/shard_map/ppermute | solution.py:142
  153.6 15.3 %copy-start.11 = (f32[2,512,512]{2,1,0:T(8,128)S(1)}, f32[2,512,512]{2,1,0:T(8,128)}, u32[]{:S(2)}) copy-start(f32[2,512,512]{2,1,0:T(8,128)} %copy-done.10) | copy-start | bytes 6291460
  153.6 34.2 %collective-permute-start.18 = (bf16[256,512]{1,0:T(8,128)(2,1)S(1)}, bf16[256,512]{1,0:T(8,128)(2,1)S(1)}, u32[]{:S(2)}, u32[]{:S(2)}) collective-permute-start(bf16[256,512]{1,0:T(8,128)(2,1)S(1)} %fusion.10), channel_id=1, source_target_pairs={{0,8},{1,9},{2,10},{3,11},{4,12},{5,13},{6,14},{7,15},{8,0},{9,1},... | collective-permute-start | bytes 786440 | tf_op jit(solution)/shard_map/ppermute | solution.py:142
  164.4 25.8 %collective-permute-start.20 = (bf16[2,256,512]{2,1,0:T(8,128)(2,1)S(1)}, bf16[2,256,512]{2,1,0:T(8,128)(2,1)S(1)}, u32[]{:S(2)}, u32[]{:S(2)}) collective-permute-start(bf16[2,256,512]{2,1,0:T(8,128)(2,1)S(1)} %get-tuple-element.31), channel_id=1, source_target_pairs={{0,2},{1,3},{2,4},{3,5},{4,6},{5,7},{6,0},{7,1},{8,10},{9,11},{10,... | collective-permute-start | bytes 1572872 | tf_op jit(solution)/shard_map/ppermute | solution.py:142
  165.7 25.5 %collective-permute-start.21 = (bf16[2,256,512]{2,1,0:T(8,128)(2,1)S(1)}, bf16[2,256,512]{2,1,0:T(8,128)(2,1)S(1)}, u32[]{:S(2)}, u32[]{:S(2)}) collective-permute-start(bf16[2,256,512]{2,1,0:T(8,128)(2,1)S(1)} %get-tuple-element.32), channel_id=1, source_target_pairs={{0,4},{1,5},{2,6},{3,7},{4,0},{5,1},{6,2},{7,3},{8,12},{9,13},{10,... | collective-permute-start | bytes 1572872 | tf_op jit(solution)/shard_map/ppermute | solution.py:142
  168.8 22.3 %collective-permute-start.22 = (bf16[2,256,512]{2,1,0:T(8,128)(2,1)S(1)}, bf16[2,256,512]{2,1,0:T(8,128)(2,1)S(1)}, u32[]{:S(2)}, u32[]{:S(2)}) collective-permute-start(bf16[2,256,512]{2,1,0:T(8,128)(2,1)S(1)} %get-tuple-element.33), channel_id=1, source_target_pairs={{0,6},{1,7},{2,0},{3,1},{4,2},{5,3},{6,4},{7,5},{8,14},{9,15},{10,... | collective-permute-start | bytes 1572872 | tf_op jit(solution)/shard_map/ppermute | solution.py:142
  187.8 1.1 copy-start.12
  191.5 6.4 %collective-permute-start.23 = (bf16[256,512]{1,0:T(8,128)(2,1)S(1)}, bf16[256,512]{1,0:T(8,128)(2,1)S(1)}, u32[]{:S(2)}, u32[]{:S(2)}) collective-permute-start(bf16[256,512]{1,0:T(8,128)(2,1)S(1)} %fusion.11), channel_id=1, source_target_pairs={{0,8},{1,9},{2,10},{3,11},{4,12},{5,13},{6,14},{7,15},{8,0},{9,1},... | collective-permute-start | bytes 786440 | tf_op jit(solution)/shard_map/ppermute | solution.py:142
  199.6 5.0 %collective-permute-start.24 = (f32[512,512]{1,0:T(8,128)S(1)}, f32[512,512]{1,0:T(8,128)S(1)}, u32[]{:S(2)}, u32[]{:S(2)}) collective-permute-start(f32[512,512]{1,0:T(8,128)S(1)} %get-tuple-element.46), channel_id=1, source_target_pairs={{0,1},{1,0},{2,3},{3,2},{4,5},{5,4},{6,7},{7,6},{8,9},{9,8},{10,11... | collective-permute-start | bytes 3145736 | tf_op jit(solution)/shard_map/ppermute | solution.py:142
  242.0 4.9 %collective-permute-start.25 = (bf16[512,512]{1,0:T(8,128)(2,1)S(1)}, bf16[512,512]{1,0:T(8,128)(2,1)S(1)}, u32[]{:S(2)}, u32[]{:S(2)}) collective-permute-start(bf16[512,512]{1,0:T(8,128)(2,1)S(1)} %bitcast.96), channel_id=1, source_target_pairs={{0,1},{1,0},{2,3},{3,2},{4,5},{5,4},{6,7},{7,6},{8,9},{9,8},{10,11... | collective-permute-start | bytes 1572872 | tf_op jit(solution)/shard_map/ppermute | solution.py:142

commit v3 on v2

--- a/solution.py
+++ b/solution.py
@@ -223,7 +223,7 @@
             out_specs=out_specs,
             scratch_shapes=[pltpu.VMEM((depth, width), jnp.bfloat16)],
         ),
-        compiler_params=pltpu.CompilerParams(vmem_limit_bytes=50 * 2**20),
+        compiler_params=pltpu.CompilerParams(vmem_limit_bytes=40 * 2**20),
         cost_estimate=pl.CostEstimate(
             flops=2 * blocks * rows * depth * width,
             bytes_accessed=2 * blocks * rows * depth + 2 * depth * width,
@@ -277,13 +277,14 @@
         first.append(shift(pair, x=d))
     first_place = jnp.stack([(z_hi ^ e) * 4 + (x - d) % 4 for d, e in steps]).astype(jnp.int32)
 
-    stacked = after(jnp.stack(along), pair)
+    state = eliminate(1, after(state, pair), pivot_flags)
+    stacked = after(jnp.stack(along), state)
     turned = []
     for d in range(4):
         part = lax.dynamic_index_in_dim(stacked, (x - y - d) % 4, 0, keepdims=False)
         turned.append(shift(part, y=d) if d else part)
 
-    state = eliminate(1, after(state, pair, stacked), pivot_flags)
+    state = eliminate(2, after(state, stacked), pivot_flags)
     quad = after(jnp.stack(turned), state)
     second = []
     for flip in range(2):
@@ -299,15 +300,12 @@
 
     pieces = [first, second]
     places = [first_place, second_place]
-    swapped = []
+    sums = []
     order = after(kept, quad)
     for k in range(nodes):
         given = product(tile, pieces[k], order ^ 1, places[k])
-        swapped.append(shift(given, core=1))
-        order = after(kept, given)
-    sums = []
-    for k in range(nodes):
-        staying, *leaving = product(tile, pieces[k], order, places[k], swapped[k])
+        other = shift(given, core=1)
+        staying, *leaving = product(tile, pieces[k], order, places[k], other)
         order = after(kept, *leaving)
         summed = staying
         for d, part in zip((1, 2, 3), leaving):
@@ -316,8 +314,7 @@
         arrived = shift(summed[1].astype(jnp.bfloat16), z_lo=1)
         sums.append(summed[0] + arrived.astype(jnp.float32))
 
-    state = eliminate(2, after(state, *leaving), pivot_flags)
-    inverses = eliminate(3, state, pivot_flags)
+    inverses = eliminate(3, after(state, *leaving), pivot_flags)
     applied, terms = [], []
     for k in range(nodes):
         applied.append(jnp.dot(sums[k], inverses[k], precision=HIGHEST))

time: 249 us -> 247 us (level)
  starting transfers between devices: 53.3 us -> 47.5 us
  local copies, waits for them, and re-layouts: 5.68 us -> 8.56 us
    ppermute x26, starting transfers between devices: 53.3 us -> 47.5 us  [send(): return lax.ppermute(value, AXES, moves)]
  transfers between devices with their start and end apart: 26 -> 26, of which waited for: 11 -> 11; matrix products, arithmetic and copies ran while one was open for 3% -> 3% of each run, Pallas kernels for 26% -> 22%
where the time goes in v3:
time: 247 us; the launch traced here: 246 us
  Pallas kernels  72.7 us (29%)
  waiting for transfers between devices  65.2 us (26%)
  starting transfers between devices  47.5 us (19%)
  blocking collectives  35.7 us (14%)
  other arithmetic  10.7 us (4%)
  local copies, waits for them, and re-layouts  8.56 us (3%)
  matrix products  4.9 us (2%)
    ppermute x26, waiting for transfers between devices, send(): return lax.ppermute(value, AXES, moves)  65.2 us
    ppermute x26, starting transfers between devices, send(): return lax.ppermute(value, AXES, moves)  47.5 us
    pallas_call x4, Pallas kernels, eliminate(): pl.pallas_call(functools.partial(inverse_kernel, block), out_shape=jax.Sh...  37.9 us
    pallas_call x4, Pallas kernels, product(): pl.pallas_call(kernel, out_shape=out_shape, grid_spec=pltpu.PrefetchScala...  34.8 us
    all_to_all x1, blocking collectives, total(): slices = lax.all_to_all(slices, CHIPS, 0, 0)  19.9 us
    all_to_all x1, blocking collectives, total(): spread = lax.all_to_all(jnp.broadcast_to(summed, slices.shape), CHIPS, 0, 0)  15.8 us
    unnamed x26, local copies, waits for them, and re-layouts  7.29 us
  transfers between devices with their start and end apart: 26, of which 11 were waited for; matrix products, arithmetic and copies ran while one was open for 3% of the time, Pallas kernels for 22%

profile of v3, /device:TPU:1, one launch (start us, length us, event | category | flops | bytes accessed | tf_op | source)
XLA Modules:
  0.0 246.2 jit_solution(15181465448868932997)
XLA Ops:
  0.6 0.8 compare_reduce_fusion.1
  1.4 1.2 bitcast_select_fusion.1
  2.6 4.5 %collective-permute-start.4 = (bf16[256,512]{1,0:T(8,128)(2,1)S(1)}, bf16[256,512]{1,0:T(8,128)(2,1)S(1)}, u32[]{:S(2)}, u32[]{:S(2)}) collective-permute-start(bf16[256,512]{1,0:T(8,128)(2,1)S(1)} %get-tuple-element.43), channel_id=1, source_target_pairs={{0,0},{1,16},{2,32},{3,48},{4,64},{5,80},{6,96},{7,112},{8,1},{9,1... | collective-permute-start | bytes 786440 | tf_op jit(solution)/shard_map/ppermute | solution.py:142
  7.1 4.5 %collective-permute-start.5 = (bf16[256,512]{1,0:T(8,128)(2,1)S(1)}, bf16[256,512]{1,0:T(8,128)(2,1)S(1)}, u32[]{:S(2)}, u32[]{:S(2)}) collective-permute-start(bf16[256,512]{1,0:T(8,128)(2,1)S(1)} %get-tuple-element.43), channel_id=1, source_target_pairs={{0,64},{1,80},{2,96},{3,112},{4,0},{5,16},{6,32},{7,48},{8,65},{9,... | collective-permute-start | bytes 786440 | tf_op jit(solution)/shard_map/ppermute | solution.py:142
  11.6 0.7 collective-permute-start
  12.3 1.6 copy-done.5
  13.8 0.7 copy-done.6
  14.5 9.5 %eliminate.4.in_ref = f32[2,512,512]{2,1,0:T(8,128)S(1)} custom-call(f32[2,512,512]{2,1,0:T(8,128)S(1)} %copy-done.5, s32[2,512]{1,0:T(2,128)S(1)} %copy-done.6), custom_call_target="tpu_custom_call" | custom-call | flops 5000000000 | bytes 4194304 | tf_op jit(solution)/shard_map/eliminate/pallas_call | solution.py:115
  24.1 1.3 copy-done.10
  25.5 1.3 collective-permute-start.1
  26.8 6.9 %collective-permute-start.2 = (bf16[256,512]{1,0:T(8,128)(2,1)S(1)}, bf16[256,512]{1,0:T(8,128)(2,1)S(1)}, u32[]{:S(2)}, u32[]{:S(2)}) collective-permute-start(bf16[256,512]{1,0:T(8,128)(2,1)S(1)} %collective-permute-done), channel_id=1, source_target_pairs={{0,32},{1,33},{2,34},{3,35},{4,36},{5,37},{6,38},{7,39},{8,40},{9,... | collective-permute-start | bytes 786440 | tf_op jit(solution)/shard_map/ppermute | solution.py:142
  33.7 1.6 copy-done.11
  35.3 9.5 %eliminate.5.in_ref = f32[2,512,512]{2,1,0:T(8,128)S(1)} custom-call(f32[2,512,512]{2,1,0:T(8,128)S(1)} %copy-done.11, s32[2,512]{1,0:T(2,128)S(1)} %copy-done.7), custom_call_target="tpu_custom_call" | custom-call | flops 5000000000 | bytes 4194304 | tf_op jit(solution)/shard_map/eliminate/pallas_call | solution.py:115
  44.8 1.0 collective-permute-done.2
  45.7 0.1 pad_maximum_fusion
  45.9 0.9 constant_dynamic-slice_fusion
  47.0 0.5 collective-permute-start.10
  47.5 2.6 %collective-permute-start.11 = (bf16[2,256,512]{2,1,0:T(8,128)(2,1)S(1)}, bf16[2,256,512]{2,1,0:T(8,128)(2,1)S(1)}, u32[]{:S(2)}, u32[]{:S(2)}) collective-permute-start(bf16[2,256,512]{2,1,0:T(8,128)(2,1)S(1)} %pad_maximum_fusion.3.refs_2_), channel_id=1, source_target_pairs={{0,48},{1,49},{2,50},{3,51},{4,52},{5,53},{6,54},{7,55},{8,56},{9,... | collective-permute-start | bytes 1572872 | tf_op jit(solution)/shard_map/ppermute | solution.py:142
  50.1 10.9 %collective-permute-done.6 = bf16[256,512]{1,0:T(8,128)(2,1)} collective-permute-done((bf16[256,512]{1,0:T(8,128)(2,1)}, bf16[256,512]{1,0:T(8,128)(2,1)}, u32[]{:S(2)}, u32[]{:S(2)}) %collective-permute-start.6) | collective-permute-done | bytes 262176 | tf_op jit(solution)/shard_map/ppermute | solution.py:142
  61.0 9.5 %eliminate.6.in_ref = f32[2,512,512]{2,1,0:T(8,128)S(1)} custom-call(f32[2,512,512]{2,1,0:T(8,128)S(1)} %eliminate.5.in_ref, s32[2,512]{1,0:T(2,128)S(1)} %copy-done.7), custom_call_target="tpu_custom_call" | custom-call | flops 5000000000 | bytes 4194304 | tf_op jit(solution)/shard_map/eliminate/pallas_call | solution.py:115
  70.5 2.3 pad_maximum_fusion.1
  72.8 0.8 collective-permute-done.9.refs_3_
  73.6 8.7 %product.4 = bf16[8,256,512]{2,1,0:T(8,128)(2,1)} custom-call(s32[8]{0:T(128)S(1)} %broadcast_xor_fusion.1.order_ref, s32[8]{0:T(128)S(1)} %stack.156.place_ref, bf16[16,256,2048]{2,1,0:T(8,128)(2,1)} %bitcast.85, bf16[16,256,2048]{2,1,0:T(8,128)(2,1)} %bitcast.86, bf16[2,256,512]{2,1,0:T(8,128)(2,1)S(1)} %pad_maximum_fusion.3.refs_2_, ...), custom_call_target="tpu_custom_call" | custom-call | flops 4294967296 | bytes 10485760 | tf_op jit(solution)/shard_map/product/pallas_call | solution.py:216
  82.3 1.0 collective-permute-start.12
  83.3 6.2 %collective-permute-start.17 = (bf16[4,256,512]{2,1,0:T(8,128)(2,1)}, bf16[4,256,512]{2,1,0:T(8,128)(2,1)S(1)}, u32[]{:S(2)}, u32[]{:S(2)}) collective-permute-start(bf16[4,256,512]{2,1,0:T(8,128)(2,1)} %pad_maximum_fusion.1), channel_id=1, source_target_pairs={{0,0},{1,64},{2,2},{3,66},{4,4},{5,68},{6,6},{7,70},{8,8},{9,72},{... | collective-permute-start | bytes 3145736 | tf_op jit(solution)/shard_map/ppermute | solution.py:142
  89.5 0.3 collective-permute-start.18
  89.9 1.0 copy-done.1
  91.0 1.0 copy-done.3
  92.0 9.3 %product.5 = (f32[2,256,512]{2,1,0:T(8,128)S(1)}, bf16[2,256,512]{2,1,0:T(8,128)(2,1)}, bf16[2,256,512]{2,1,0:T(8,128)(2,1)}, bf16[2,256,512]{2,1,0:T(8,128)(2,1)}) custom-call(s32[8]{0:T(128)S(1)} %stack.135.order_ref, s32[8]{0:T(128)S(1)} %stack.156.place_ref, bf16[16,256,2048]{2,1,0:T(8,128)(2,1)} %bitcast.87, bf16[16,256,2048]{2,1,0:T(8,128)(2,1)} %bitcast.88, ...), custom_call_target="tpu_custom_call" | custom-call | flops 4294967296 | bytes 10485760 | tf_op jit(solution)/shard_map/product/pallas_call | solution.py:216
  101.3 10.6 %collective-permute-done.17.refs_2_ = bf16[4,256,512]{2,1,0:T(8,128)(2,1)S(1)} collective-permute-done((bf16[4,256,512]{2,1,0:T(8,128)(2,1)}, bf16[4,256,512]{2,1,0:T(8,128)(2,1)S(1)}, u32[]{:S(2)}, u32[]{:S(2)}) %collective-permute-start.17) | collective-permute-done | bytes 1048608 | tf_op jit(solution)/shard_map/ppermute | solution.py:142
  111.9 1.5 collective-permute-done.18.refs_3_
  113.4 8.7 %product.6 = bf16[8,256,512]{2,1,0:T(8,128)(2,1)} custom-call(s32[8]{0:T(128)S(1)} %broadcast_xor_fusion.order_ref, s32[8]{0:T(128)S(1)} %stack.165.place_ref, bf16[16,256,2048]{2,1,0:T(8,128)(2,1)} %bitcast.89, bf16[16,256,2048]{2,1,0:T(8,128)(2,1)} %bitcast.90, bf16[4,256,512]{2,1,0:T(8,128)(2,1)S(1)} %collective-permute-done.17.refs_2_, ...), custom_call_target="tpu_custom_call" | custom-call | flops 4294967296 | bytes 10485760 | tf_op jit(solution)/shard_map/product/pallas_call | solution.py:216
  122.1 1.8 collective-permute-start.13
  123.9 1.8 collective-permute-start.14
  125.7 1.0 collective-permute-start.15
  126.7 9.9 %collective-permute-done.13 = bf16[2,256,512]{2,1,0:T(8,128)(2,1)S(1)} collective-permute-done((bf16[2,256,512]{2,1,0:T(8,128)(2,1)}, bf16[2,256,512]{2,1,0:T(8,128)(2,1)S(1)}, u32[]{:S(2)}, u32[]{:S(2)}) %collective-permute-start.13) | collective-permute-done | bytes 524320 | tf_op jit(solution)/shard_map/ppermute | solution.py:142
  136.6 12.1 %collective-permute-done.14 = bf16[2,256,512]{2,1,0:T(8,128)(2,1)S(1)} collective-permute-done((bf16[2,256,512]{2,1,0:T(8,128)(2,1)}, bf16[2,256,512]{2,1,0:T(8,128)(2,1)S(1)}, u32[]{:S(2)}, u32[]{:S(2)}) %collective-permute-start.14) | collective-permute-done | bytes 524320 | tf_op jit(solution)/shard_map/ppermute | solution.py:142
  148.8 1.7 convert_add_fusion.2
  150.5 3.5 %collective-permute-start.16 = (bf16[256,512]{1,0:T(8,128)(2,1)S(1)}, bf16[256,512]{1,0:T(8,128)(2,1)S(1)}, u32[]{:S(2)}, u32[]{:S(2)}) collective-permute-start(bf16[256,512]{1,0:T(8,128)(2,1)S(1)} %fusion.10), channel_id=1, source_target_pairs={{0,8},{1,9},{2,10},{3,11},{4,12},{5,13},{6,14},{7,15},{8,0},{9,1},... | collective-permute-start | bytes 786440 | tf_op jit(solution)/shard_map/ppermute | solution.py:142
  153.9 8.2 %product.7 = (f32[2,256,512]{2,1,0:T(8,128)S(1)}, bf16[2,256,512]{2,1,0:T(8,128)(2,1)S(1)}, bf16[2,256,512]{2,1,0:T(8,128)(2,1)S(1)}, bf16[2,256,512]{2,1,0:T(8,128)(2,1)S(1)}) custom-call(s32[8]{0:T(128)S(1)} %stack.135.order_ref, s32[8]{0:T(128)S(1)} %stack.165.place_ref, bf16[16,256,2048]{2,1,0:T(8,128)(2,1)} %bitcast.91, ...), custom_call_target="tpu_custom_call" | custom-call | flops 4294967296 | bytes 10485760 | tf_op jit(solution)/shard_map/product/pallas_call | solution.py:216
  162.1 2.0 collective-permute-start.20
  164.1 2.2 collective-permute-start.21
  166.3 0.3 collective-permute-start.22
  166.6 9.4 %eliminate.7 = f32[2,512,512]{2,1,0:T(8,128)S(1)} custom-call(f32[2,512,512]{2,1,0:T(8,128)S(1)} %copy-done.9, s32[2,512]{1,0:T(2,128)S(1)} %copy-done.7), custom_call_target="tpu_custom_call" | custom-call | flops 5000000000 | bytes 4194304 | tf_op jit(solution)/shard_map/eliminate/pallas_call | solution.py:115
  176.1 1.1 fusion.1
  177.2 0.7 convolution_convert_fusion.1
  177.9 0.7 fusion.24
  178.6 10.2 %collective-permute-done.21 = bf16[2,256,512]{2,1,0:T(8,128)(2,1)S(1)} collective-permute-done((bf16[2,256,512]{2,1,0:T(8,128)(2,1)S(1)}, bf16[2,256,512]{2,1,0:T(8,128)(2,1)S(1)}, u32[]{:S(2)}, u32[]{:S(2)}) %collective-permute-start.21) | collective-permute-done | bytes 524320 | tf_op jit(solution)/shard_map/ppermute | solution.py:142
  188.8 0.3 convert_add_fusion.1
  189.1 0.6 collective-permute-start.23
  189.7 0.7 convolution_convert_fusion
  190.4 5.2 %collective-permute-done.23 = bf16[256,512]{1,0:T(8,128)(2,1)S(1)} collective-permute-done((bf16[256,512]{1,0:T(8,128)(2,1)S(1)}, bf16[256,512]{1,0:T(8,128)(2,1)S(1)}, u32[]{:S(2)}, u32[]{:S(2)}) %collective-permute-start.23) | collective-permute-done | bytes 262176 | tf_op jit(solution)/shard_map/ppermute | solution.py:142
  195.6 1.1 fusion.2
  196.7 0.7 broadcast_select_fusion.2
  197.4 2.6 %collective-permute-start.24 = (f32[512,512]{1,0:T(8,128)S(1)}, f32[512,512]{1,0:T(8,128)S(1)}, u32[]{:S(2)}, u32[]{:S(2)}) collective-permute-start(f32[512,512]{1,0:T(8,128)S(1)} %get-tuple-element.44), channel_id=1, source_target_pairs={{0,1},{1,0},{2,3},{3,2},{4,5},{5,4},{6,7},{7,6},{8,9},{9,8},{10,11... | collective-permute-start | bytes 3145736 | tf_op jit(solution)/shard_map/ppermute | solution.py:142
  199.9 2.3 collective-permute-done.24
  202.2 0.4 fusion.3
  202.6 19.9 %all_to_all.10 = bf16[64,8,512]{2,1,0:T(8,128)(2,1)} all-to-all(bf16[64,8,512]{2,1,0:T(8,128)(2,1)S(1)} %fusion.3), channel_id=1, replica_groups=mesh['z_hi'=2,'x'=4,'z_lo'=2,'y'=4,'core'=2] {'z_hi','x','z_lo','y'}, dimensions={0} | all-to-all | bytes 1048576 | tf_op jit(solution)/shard_map/all_to_all | solution.py:243
  222.5 1.1 reduce_sum.12
  223.7 15.8 %all_to_all.11 = bf16[64,8,512]{2,1,0:T(8,128)(2,1)S(1)} all-to-all(bf16[64,8,512]{2,1,0:T(8,128)(2,1)S(1)} %broadcast_in_dim.36), channel_id=1, replica_groups=mesh['z_hi'=2,'x'=4,'z_lo'=2,'y'=4,'core'=2] {'z_hi','x','z_lo','y'}, dimensions={0} | all-to-all | bytes 1048576 | tf_op jit(solution)/shard_map/all_to_all | solution.py:245
  239.5 3.3 %collective-permute-start.25 = (bf16[512,512]{1,0:T(8,128)(2,1)S(1)}, bf16[512,512]{1,0:T(8,128)(2,1)S(1)}, u32[]{:S(2)}, u32[]{:S(2)}) collective-permute-start(bf16[512,512]{1,0:T(8,128)(2,1)S(1)} %bitcast.96), channel_id=1, source_target_pairs={{0,1},{1,0},{2,3},{3,2},{4,5},{5,4},{6,7},{7,6},{8,9},{9,8},{10,11... | collective-permute-start | bytes 1572872 | tf_op jit(solution)/shard_map/ppermute | solution.py:142
  242.8 0.9 fusion
  243.7 0.6 collective-permute-done.25
  244.5 1.7 convert_add_fusion
  (52 shorter events, 0.7 us)
Async XLA Ops:
  2.6 22.8 %collective-permute-start.4 = (bf16[256,512]{1,0:T(8,128)(2,1)S(1)}, bf16[256,512]{1,0:T(8,128)(2,1)S(1)}, u32[]{:S(2)}, u32[]{:S(2)}) collective-permute-start(bf16[256,512]{1,0:T(8,128)(2,1)S(1)} %get-tuple-element.43), channel_id=1, source_target_pairs={{0,0},{1,16},{2,32},{3,48},{4,64},{5,80},{6,96},{7,112},{8,1},{9,1... | collective-permute-start | bytes 786440 | tf_op jit(solution)/shard_map/ppermute | solution.py:142
  7.1 18.3 %collective-permute-start.5 = (bf16[256,512]{1,0:T(8,128)(2,1)S(1)}, bf16[256,512]{1,0:T(8,128)(2,1)S(1)}, u32[]{:S(2)}, u32[]{:S(2)}) collective-permute-start(bf16[256,512]{1,0:T(8,128)(2,1)S(1)} %get-tuple-element.43), channel_id=1, source_target_pairs={{0,64},{1,80},{2,96},{3,112},{4,0},{5,16},{6,32},{7,48},{8,65},{9,... | collective-permute-start | bytes 786440 | tf_op jit(solution)/shard_map/ppermute | solution.py:142
  11.6 13.9 %collective-permute-start = (bf16[256,512]{1,0:T(8,128)(2,1)S(1)}, bf16[256,512]{1,0:T(8,128)(2,1)S(1)}, u32[]{:S(2)}, u32[]{:S(2)}) collective-permute-start(bf16[256,512]{1,0:T(8,128)(2,1)S(1)} %get-tuple-element.42), channel_id=1, source_target_pairs={{0,0},{1,1},{2,2},{3,3},{4,4},{5,5},{6,6},{7,7},{8,64},{9,65},{10,... | collective-permute-start | bytes 786440 | tf_op jit(solution)/shard_map/ppermute | solution.py:142
  12.2 1.6 copy-start.5
  13.8 0.7 copy-start.6
  14.5 19.2 %copy-start.7 = (s32[2,512]{1,0:T(2,128)S(1)}, s32[2,512]{1,0:T(2,128)}, u32[]{:S(2)}) copy-start(s32[2,512]{1,0:T(2,128)} %flag_ref.7) | copy-start | bytes 12292
  24.1 1.3 copy-start.10
  25.5 19.3 %collective-permute-start.1 = (bf16[256,512]{1,0:T(8,128)(2,1)S(1)}, bf16[256,512]{1,0:T(8,128)(2,1)S(1)}, u32[]{:S(2)}, u32[]{:S(2)}) collective-permute-start(bf16[256,512]{1,0:T(8,128)(2,1)S(1)} %collective-permute-done), channel_id=1, source_target_pairs={{0,16},{1,17},{2,18},{3,19},{4,20},{5,21},{6,22},{7,23},{8,24},{9,... | collective-permute-start | bytes 786440 | tf_op jit(solution)/shard_map/ppermute | solution.py:142
  26.8 18.9 %collective-permute-start.2 = (bf16[256,512]{1,0:T(8,128)(2,1)S(1)}, bf16[256,512]{1,0:T(8,128)(2,1)S(1)}, u32[]{:S(2)}, u32[]{:S(2)}) collective-permute-start(bf16[256,512]{1,0:T(8,128)(2,1)S(1)} %collective-permute-done), channel_id=1, source_target_pairs={{0,32},{1,33},{2,34},{3,35},{4,36},{5,37},{6,38},{7,39},{8,40},{9,... | collective-permute-start | bytes 786440 | tf_op jit(solution)/shard_map/ppermute | solution.py:142
  33.7 12.0 %collective-permute-start.3 = (bf16[256,512]{1,0:T(8,128)(2,1)S(1)}, bf16[256,512]{1,0:T(8,128)(2,1)S(1)}, u32[]{:S(2)}, u32[]{:S(2)}) collective-permute-start(bf16[256,512]{1,0:T(8,128)(2,1)S(1)} %collective-permute-done), channel_id=1, source_target_pairs={{0,48},{1,49},{2,50},{3,51},{4,52},{5,53},{6,54},{7,55},{8,56},{9,... | collective-permute-start | bytes 786440 | tf_op jit(solution)/shard_map/ppermute | solution.py:142
  33.7 1.6 copy-start.11
  46.8 14.2 %collective-permute-start.6 = (bf16[256,512]{1,0:T(8,128)(2,1)}, bf16[256,512]{1,0:T(8,128)(2,1)}, u32[]{:S(2)}, u32[]{:S(2)}) collective-permute-start(bf16[256,512]{1,0:T(8,128)(2,1)} %get-tuple-element.41), channel_id=1, source_target_pairs={{0,2},{1,3},{2,4},{3,5},{4,6},{5,7},{6,0},{7,1},{8,10},{9,11},{10,... | collective-permute-start | bytes 786440 | tf_op jit(solution)/shard_map/ppermute | solution.py:142
  47.0 25.8 %collective-permute-start.10 = (bf16[2,256,512]{2,1,0:T(8,128)(2,1)S(1)}, bf16[2,256,512]{2,1,0:T(8,128)(2,1)S(1)}, u32[]{:S(2)}, u32[]{:S(2)}) collective-permute-start(bf16[2,256,512]{2,1,0:T(8,128)(2,1)S(1)} %pad_maximum_fusion.3.refs_2_), channel_id=1, source_target_pairs={{0,32},{1,33},{2,34},{3,35},{4,36},{5,37},{6,38},{7,39},{8,40},{9,... | collective-permute-start | bytes 1572872 | tf_op jit(solution)/shard_map/ppermute | solution.py:142
  47.5 25.3 %collective-permute-start.11 = (bf16[2,256,512]{2,1,0:T(8,128)(2,1)S(1)}, bf16[2,256,512]{2,1,0:T(8,128)(2,1)S(1)}, u32[]{:S(2)}, u32[]{:S(2)}) collective-permute-start(bf16[2,256,512]{2,1,0:T(8,128)(2,1)S(1)} %pad_maximum_fusion.3.refs_2_), channel_id=1, source_target_pairs={{0,48},{1,49},{2,50},{3,51},{4,52},{5,53},{6,54},{7,55},{8,56},{9,... | collective-permute-start | bytes 1572872 | tf_op jit(solution)/shard_map/ppermute | solution.py:142
  50.1 23.5 %collective-permute-start.9 = (bf16[2,256,512]{2,1,0:T(8,128)(2,1)S(1)}, bf16[2,256,512]{2,1,0:T(8,128)(2,1)S(1)}, u32[]{:S(2)}, u32[]{:S(2)}) collective-permute-start(bf16[2,256,512]{2,1,0:T(8,128)(2,1)S(1)} %pad_maximum_fusion.3.refs_2_), channel_id=1, source_target_pairs={{0,16},{1,17},{2,18},{3,19},{4,20},{5,21},{6,22},{7,23},{8,24},{9,... | collective-permute-start | bytes 1572872 | tf_op jit(solution)/shard_map/ppermute | solution.py:142
  50.1 20.4 %collective-permute-start.7 = (bf16[256,512]{1,0:T(8,128)(2,1)}, bf16[256,512]{1,0:T(8,128)(2,1)S(1)}, u32[]{:S(2)}, u32[]{:S(2)}) collective-permute-start(bf16[256,512]{1,0:T(8,128)(2,1)} %get-tuple-element.40), channel_id=1, source_target_pairs={{0,4},{1,5},{2,6},{3,7},{4,0},{5,1},{6,2},{7,3},{8,12},{9,13},{10,... | collective-permute-start | bytes 786440 | tf_op jit(solution)/shard_map/ppermute | solution.py:142
  61.0 9.5 %collective-permute-start.8 = (bf16[256,512]{1,0:T(8,128)(2,1)}, bf16[256,512]{1,0:T(8,128)(2,1)S(1)}, u32[]{:S(2)}, u32[]{:S(2)}) collective-permute-start(bf16[256,512]{1,0:T(8,128)(2,1)} %get-tuple-element.39), channel_id=1, source_target_pairs={{0,6},{1,7},{2,0},{3,1},{4,2},{5,3},{6,4},{7,5},{8,14},{9,15},{10,... | collective-permute-start | bytes 786440 | tf_op jit(solution)/shard_map/ppermute | solution.py:142
  70.4 3.1 %copy-start.8 = (f32[2,512,512]{2,1,0:T(8,128)}, f32[2,512,512]{2,1,0:T(8,128)S(1)}, u32[]{:S(2)}) copy-start(f32[2,512,512]{2,1,0:T(8,128)S(1)} %eliminate.6.in_ref) | copy-start | bytes 6291460
  72.8 9.5 %copy-start = (bf16[2,256,512]{2,1,0:T(8,128)(2,1)}, bf16[2,256,512]{2,1,0:T(8,128)(2,1)S(1)}, u32[]{:S(2)}) copy-start(bf16[2,256,512]{2,1,0:T(8,128)(2,1)S(1)} %collective-permute-done.11.refs_5_) | copy-start | bytes 1572868
  73.6 8.7 %copy-start.2 = (bf16[2,256,512]{2,1,0:T(8,128)(2,1)}, bf16[2,256,512]{2,1,0:T(8,128)(2,1)S(1)}, u32[]{:S(2)}) copy-start(bf16[2,256,512]{2,1,0:T(8,128)(2,1)S(1)} %collective-permute-done.9.refs_3_) | copy-start | bytes 1572868
  82.3 7.7 %collective-permute-start.12 = (bf16[8,256,512]{2,1,0:T(8,128)(2,1)}, bf16[8,256,512]{2,1,0:T(8,128)(2,1)}, u32[]{:S(2)}, u32[]{:S(2)}) collective-permute-start(bf16[8,256,512]{2,1,0:T(8,128)(2,1)} %product.4), channel_id=1, source_target_pairs={{0,1},{1,0},{2,3},{3,2},{4,5},{5,4},{6,7},{7,6},{8,9},{9,8},{10,11... | collective-permute-start | bytes 6291464 | tf_op jit(solution)/shard_map/ppermute | solution.py:142
  83.3 28.6 %collective-permute-start.17 = (bf16[4,256,512]{2,1,0:T(8,128)(2,1)}, bf16[4,256,512]{2,1,0:T(8,128)(2,1)S(1)}, u32[]{:S(2)}, u32[]{:S(2)}) collective-permute-start(bf16[4,256,512]{2,1,0:T(8,128)(2,1)} %pad_maximum_fusion.1), channel_id=1, source_target_pairs={{0,0},{1,64},{2,2},{3,66},{4,4},{5,68},{6,6},{7,70},{8,8},{9,72},{... | collective-permute-start | bytes 3145736 | tf_op jit(solution)/shard_map/ppermute | solution.py:142
  89.5 23.9 %collective-permute-start.18 = (bf16[4,256,512]{2,1,0:T(8,128)(2,1)}, bf16[4,256,512]{2,1,0:T(8,128)(2,1)S(1)}, u32[]{:S(2)}, u32[]{:S(2)}) collective-permute-start(bf16[4,256,512]{2,1,0:T(8,128)(2,1)} %pad_maximum_fusion.1), channel_id=1, source_target_pairs={{0,64},{1,0},{2,66},{3,2},{4,68},{5,4},{6,70},{7,6},{8,72},{9,8},{... | collective-permute-start | bytes 3145736 | tf_op jit(solution)/shard_map/ppermute | solution.py:142
  89.9 1.0 copy-start.1
  91.0 1.0 copy-start.3
  101.3 20.8 %copy-start.4 = (f32[2,256,512]{2,1,0:T(8,128)}, f32[2,256,512]{2,1,0:T(8,128)S(1)}, u32[]{:S(2)}) copy-start(f32[2,256,512]{2,1,0:T(8,128)S(1)} %get-tuple-element.24) | copy-start | bytes 3145732
  122.1 31.8 %collective-permute-start.19 = (bf16[8,256,512]{2,1,0:T(8,128)(2,1)}, bf16[8,256,512]{2,1,0:T(8,128)(2,1)}, u32[]{:S(2)}, u32[]{:S(2)}) collective-permute-start(bf16[8,256,512]{2,1,0:T(8,128)(2,1)} %product.6), channel_id=1, source_target_pairs={{0,1},{1,0},{2,3},{3,2},{4,5},{5,4},{6,7},{7,6},{8,9},{9,8},{10,11... | collective-permute-start | bytes 6291464 | tf_op jit(solution)/shard_map/ppermute | solution.py:142
  122.1 14.5 %collective-permute-start.13 = (bf16[2,256,512]{2,1,0:T(8,128)(2,1)}, bf16[2,256,512]{2,1,0:T(8,128)(2,1)S(1)}, u32[]{:S(2)}, u32[]{:S(2)}) collective-permute-start(bf16[2,256,512]{2,1,0:T(8,128)(2,1)} %get-tuple-element.25), channel_id=1, source_target_pairs={{0,2},{1,3},{2,4},{3,5},{4,6},{5,7},{6,0},{7,1},{8,10},{9,11},{10,... | collective-permute-start | bytes 1572872 | tf_op jit(solution)/shard_map/ppermute | solution.py:142
  123.9 24.8 %collective-permute-start.14 = (bf16[2,256,512]{2,1,0:T(8,128)(2,1)}, bf16[2,256,512]{2,1,0:T(8,128)(2,1)S(1)}, u32[]{:S(2)}, u32[]{:S(2)}) collective-permute-start(bf16[2,256,512]{2,1,0:T(8,128)(2,1)} %get-tuple-element.26), channel_id=1, source_target_pairs={{0,4},{1,5},{2,6},{3,7},{4,0},{5,1},{6,2},{7,3},{8,12},{9,13},{10,... | collective-permute-start | bytes 1572872 | tf_op jit(solution)/shard_map/ppermute | solution.py:142
  125.7 23.0 %collective-permute-start.15 = (bf16[2,256,512]{2,1,0:T(8,128)(2,1)}, bf16[2,256,512]{2,1,0:T(8,128)(2,1)}, u32[]{:S(2)}, u32[]{:S(2)}) collective-permute-start(bf16[2,256,512]{2,1,0:T(8,128)(2,1)} %get-tuple-element.27), channel_id=1, source_target_pairs={{0,6},{1,7},{2,0},{3,1},{4,2},{5,3},{6,4},{7,5},{8,14},{9,15},{10,... | collective-permute-start | bytes 1572872 | tf_op jit(solution)/shard_map/ppermute | solution.py:142
  150.5 16.1 %copy-start.9 = (f32[2,512,512]{2,1,0:T(8,128)S(1)}, f32[2,512,512]{2,1,0:T(8,128)}, u32[]{:S(2)}) copy-start(f32[2,512,512]{2,1,0:T(8,128)} %copy-done.8) | copy-start | bytes 6291460
  150.5 25.6 %collective-permute-start.16 = (bf16[256,512]{1,0:T(8,128)(2,1)S(1)}, bf16[256,512]{1,0:T(8,128)(2,1)S(1)}, u32[]{:S(2)}, u32[]{:S(2)}) collective-permute-start(bf16[256,512]{1,0:T(8,128)(2,1)S(1)} %fusion.10), channel_id=1, source_target_pairs={{0,8},{1,9},{2,10},{3,11},{4,12},{5,13},{6,14},{7,15},{8,0},{9,1},... | collective-permute-start | bytes 786440 | tf_op jit(solution)/shard_map/ppermute | solution.py:142
  162.1 16.4 %collective-permute-start.20 = (bf16[2,256,512]{2,1,0:T(8,128)(2,1)S(1)}, bf16[2,256,512]{2,1,0:T(8,128)(2,1)S(1)}, u32[]{:S(2)}, u32[]{:S(2)}) collective-permute-start(bf16[2,256,512]{2,1,0:T(8,128)(2,1)S(1)} %get-tuple-element.29), channel_id=1, source_target_pairs={{0,2},{1,3},{2,4},{3,5},{4,6},{5,7},{6,0},{7,1},{8,10},{9,11},{10,... | collective-permute-start | bytes 1572872 | tf_op jit(solution)/shard_map/ppermute | solution.py:142
  164.1 24.7 %collective-permute-start.21 = (bf16[2,256,512]{2,1,0:T(8,128)(2,1)S(1)}, bf16[2,256,512]{2,1,0:T(8,128)(2,1)S(1)}, u32[]{:S(2)}, u32[]{:S(2)}) collective-permute-start(bf16[2,256,512]{2,1,0:T(8,128)(2,1)S(1)} %get-tuple-element.30), channel_id=1, source_target_pairs={{0,4},{1,5},{2,6},{3,7},{4,0},{5,1},{6,2},{7,3},{8,12},{9,13},{10,... | collective-permute-start | bytes 1572872 | tf_op jit(solution)/shard_map/ppermute | solution.py:142
  166.3 22.5 %collective-permute-start.22 = (bf16[2,256,512]{2,1,0:T(8,128)(2,1)S(1)}, bf16[2,256,512]{2,1,0:T(8,128)(2,1)S(1)}, u32[]{:S(2)}, u32[]{:S(2)}) collective-permute-start(bf16[2,256,512]{2,1,0:T(8,128)(2,1)S(1)} %get-tuple-element.31), channel_id=1, source_target_pairs={{0,6},{1,7},{2,0},{3,1},{4,2},{5,3},{6,4},{7,5},{8,14},{9,15},{10,... | collective-permute-start | bytes 1572872 | tf_op jit(solution)/shard_map/ppermute | solution.py:142
  176.0 1.1 copy-start.12
  189.1 6.5 %collective-permute-start.23 = (bf16[256,512]{1,0:T(8,128)(2,1)S(1)}, bf16[256,512]{1,0:T(8,128)(2,1)S(1)}, u32[]{:S(2)}, u32[]{:S(2)}) collective-permute-start(bf16[256,512]{1,0:T(8,128)(2,1)S(1)} %fusion.11), channel_id=1, source_target_pairs={{0,8},{1,9},{2,10},{3,11},{4,12},{5,13},{6,14},{7,15},{8,0},{9,1},... | collective-permute-start | bytes 786440 | tf_op jit(solution)/shard_map/ppermute | solution.py:142
  197.4 4.9 %collective-permute-start.24 = (f32[512,512]{1,0:T(8,128)S(1)}, f32[512,512]{1,0:T(8,128)S(1)}, u32[]{:S(2)}, u32[]{:S(2)}) collective-permute-start(f32[512,512]{1,0:T(8,128)S(1)} %get-tuple-element.44), channel_id=1, source_target_pairs={{0,1},{1,0},{2,3},{3,2},{4,5},{5,4},{6,7},{7,6},{8,9},{9,8},{10,11... | collective-permute-start | bytes 3145736 | tf_op jit(solution)/shard_map/ppermute | solution.py:142
  239.5 4.9 %collective-permute-start.25 = (bf16[512,512]{1,0:T(8,128)(2,1)S(1)}, bf16[512,512]{1,0:T(8,128)(2,1)S(1)}, u32[]{:S(2)}, u32[]{:S(2)}) collective-permute-start(bf16[512,512]{1,0:T(8,128)(2,1)S(1)} %bitcast.96), channel_id=1, source_target_pairs={{0,1},{1,0},{2,3},{3,2},{4,5},{5,4},{6,7},{7,6},{8,9},{9,8},{10,11... | collective-permute-start | bytes 1572872 | tf_op jit(solution)/shard_map/ppermute | solution.py:142

commit v4 on v3

--- a/solution.py
+++ b/solution.py
@@ -77,6 +77,14 @@
     lax.fori_loop(0, n // STRIP, step, 0)
 
 
+def split_dot(a, b):
+    a_head, b_head = a.astype(jnp.bfloat16), b.astype(jnp.bfloat16)
+    a_rest = (a - a_head.astype(jnp.float32)).astype(jnp.bfloat16)
+    b_rest = (b - b_head.astype(jnp.float32)).astype(jnp.bfloat16)
+    dot = functools.partial(jnp.dot, preferred_element_type=jnp.float32)
+    return dot(a_head, b_head) + (dot(a_head, b_rest) + dot(a_rest, b_head))
+
+
 def inverse_kernel(block, in_ref, flag_ref, out_ref, block_ref, panel_ref):
     count, width, _ = in_ref.shape
     n = block_ref.shape[1]
@@ -95,15 +103,11 @@
 
     def update(k, carry):
         inner = block_ref[k]
-        panel_ref[...] = jnp.dot(
-            inner, out_ref[k, here, :], precision=HIGHEST, preferred_element_type=jnp.float32
-        )
+        panel_ref[...] = split_dot(inner, out_ref[k, here, :])
         panel_ref[:, here] = inner
         left = out_ref[k, :, here]
         out_ref[k, :, here] = jnp.zeros((width, n), jnp.float32)
-        out_ref[k] = out_ref[k] - jnp.dot(
-            left, panel_ref[...], precision=HIGHEST, preferred_element_type=jnp.float32
-        )
+        out_ref[k] = out_ref[k] - split_dot(left, panel_ref[...])
         out_ref[k, here, :] = panel_ref[...]
         return carry
 
@@ -277,15 +281,13 @@
         first.append(shift(pair, x=d))
     first_place = jnp.stack([(z_hi ^ e) * 4 + (x - d) % 4 for d, e in steps]).astype(jnp.int32)
 
-    state = eliminate(1, after(state, pair), pivot_flags)
-    stacked = after(jnp.stack(along), state)
+    stacked = after(jnp.stack(along), pair)
     turned = []
     for d in range(4):
         part = lax.dynamic_index_in_dim(stacked, (x - y - d) % 4, 0, keepdims=False)
         turned.append(shift(part, y=d) if d else part)
 
-    state = eliminate(2, after(state, stacked), pivot_flags)
-    quad = after(jnp.stack(turned), state)
+    quad = jnp.stack(turned)
     second = []
     for flip in range(2):
         second.append(
@@ -305,6 +307,8 @@
     for k in range(nodes):
         given = product(tile, pieces[k], order ^ 1, places[k])
         other = shift(given, core=1)
+        if k == 0:
+            state = eliminate(1, after(state, given), pivot_flags)
         staying, *leaving = product(tile, pieces[k], order, places[k], other)
         order = after(kept, *leaving)
         summed = staying
@@ -314,7 +318,8 @@
         arrived = shift(summed[1].astype(jnp.bfloat16), z_lo=1)
         sums.append(summed[0] + arrived.astype(jnp.float32))
 
-    inverses = eliminate(3, after(state, *leaving), pivot_flags)
+    state = eliminate(2, after(state, *leaving), pivot_flags)
+    inverses = eliminate(3, state, pivot_flags)
     applied, terms = [], []
     for k in range(nodes):
         applied.append(jnp.dot(sums[k], inverses[k], precision=HIGHEST))

time: 247 us -> 241 us (0.976)
  waiting for transfers between devices: 65.2 us -> 57.2 us
  starting transfers between devices: 47.5 us -> 53.8 us
  Pallas kernels: 72.7 us -> 68.5 us
    ppermute x26, waiting for transfers between devices: 65.2 us -> 57.2 us  [send(): return lax.ppermute(value, AXES, moves)]
    ppermute x26, starting transfers between devices: 47.5 us -> 53.8 us  [send(): return lax.ppermute(value, AXES, moves)]
    pallas_call x4, Pallas kernels: 37.9 us -> 33.7 us  [eliminate(): pl.pallas_call(functools.partial(inverse_kernel, block), out_shape=jax.Sh...]
    unnamed x26 -> x24, local copies, waits for them, and re-layouts: 7.29 us -> 7.29 us
  transfers between devices with their start and end apart: 26 -> 26, of which waited for: 11 -> 13; matrix products, arithmetic and copies ran while one was open for 3% -> 3% of each run, Pallas kernels for 22% -> 21%
where the time goes in v4:
time: 241 us; the launch traced here: 240 us
  Pallas kernels  68.5 us (28%)
  waiting for transfers between devices  57.2 us (24%)
  starting transfers between devices  53.8 us (22%)
  blocking collectives  36.6 us (15%)
  other arithmetic  10.3 us (4%)
  local copies, waits for them, and re-layouts  7.73 us (3%)
  matrix products  4.87 us (2%)
    ppermute x26, waiting for transfers between devices, send(): return lax.ppermute(value, AXES, moves)  57.2 us
    ppermute x26, starting transfers between devices, send(): return lax.ppermute(value, AXES, moves)  53.8 us
    pallas_call x4, Pallas kernels, product(): pl.pallas_call(kernel, out_shape=out_shape, grid_spec=pltpu.PrefetchScala...  34.8 us
    pallas_call x4, Pallas kernels, eliminate(): pl.pallas_call(functools.partial(inverse_kernel, block), out_shape=jax.Sh...  33.7 us
    all_to_all x1, blocking collectives, total(): slices = lax.all_to_all(slices, CHIPS, 0, 0)  20.8 us
    all_to_all x1, blocking collectives, total(): spread = lax.all_to_all(jnp.broadcast_to(summed, slices.shape), CHIPS, 0, 0)  15.8 us
    unnamed x24, local copies, waits for them, and re-layouts  7.29 us
  transfers between devices with their start and end apart: 26, of which 13 were waited for; matrix products, arithmetic and copies ran while one was open for 3% of the time, Pallas kernels for 21%

profile of v4, /device:TPU:1, one launch (start us, length us, event | category | flops | bytes accessed | tf_op | source)
XLA Modules:
  0.0 240.0 jit_solution(17349957432389738122)
XLA Ops:
  0.6 0.8 compare_reduce_fusion
  1.4 1.2 bitcast_select_fusion
  2.6 0.7 collective-permute-start
  3.3 7.3 %collective-permute-start.5 = (bf16[256,512]{1,0:T(8,128)(2,1)S(1)}, bf16[256,512]{1,0:T(8,128)(2,1)S(1)}, u32[]{:S(2)}, u32[]{:S(2)}) collective-permute-start(bf16[256,512]{1,0:T(8,128)(2,1)S(1)} %get-tuple-element.38), channel_id=1, source_target_pairs={{0,64},{1,80},{2,96},{3,112},{4,0},{5,16},{6,32},{7,48},{8,65},{9,... | collective-permute-start | bytes 786440 | tf_op jit(solution)/shard_map/ppermute | solution.py:146
  10.6 3.4 %collective-permute-start.4 = (bf16[256,512]{1,0:T(8,128)(2,1)S(1)}, bf16[256,512]{1,0:T(8,128)(2,1)S(1)}, u32[]{:S(2)}, u32[]{:S(2)}) collective-permute-start(bf16[256,512]{1,0:T(8,128)(2,1)S(1)} %get-tuple-element.38), channel_id=1, source_target_pairs={{0,0},{1,16},{2,32},{3,48},{4,64},{5,80},{6,96},{7,112},{8,1},{9,1... | collective-permute-start | bytes 786440 | tf_op jit(solution)/shard_map/ppermute | solution.py:146
  14.0 3.4 %collective-permute-start.3 = (bf16[256,512]{1,0:T(8,128)(2,1)S(1)}, bf16[256,512]{1,0:T(8,128)(2,1)S(1)}, u32[]{:S(2)}, u32[]{:S(2)}) collective-permute-start(bf16[256,512]{1,0:T(8,128)(2,1)S(1)} %collective-permute-done), channel_id=1, source_target_pairs={{0,48},{1,49},{2,50},{3,51},{4,52},{5,53},{6,54},{7,55},{8,56},{9,... | collective-permute-start | bytes 786440 | tf_op jit(solution)/shard_map/ppermute | solution.py:146
  17.4 0.7 collective-permute-start.1
  18.1 1.6 copy-done.6
  19.7 0.7 copy-done.7
  20.4 8.5 %eliminate.4.in_ref = f32[2,512,512]{2,1,0:T(8,128)S(1)} custom-call(f32[2,512,512]{2,1,0:T(8,128)S(1)} %copy-done.6, s32[2,512]{1,0:T(2,128)S(1)} %copy-done.7), custom_call_target="tpu_custom_call" | custom-call | flops 5000000000 | bytes 4194304 | tf_op jit(solution)/shard_map/eliminate/pallas_call | solution.py:119
  28.9 1.3 copy-done.9
  30.3 3.5 %collective-permute-done.1 = bf16[256,512]{1,0:T(8,128)(2,1)S(1)} collective-permute-done((bf16[256,512]{1,0:T(8,128)(2,1)S(1)}, bf16[256,512]{1,0:T(8,128)(2,1)S(1)}, u32[]{:S(2)}, u32[]{:S(2)}) %collective-permute-start.1) | collective-permute-done | bytes 262176 | tf_op jit(solution)/shard_map/ppermute | solution.py:146
  34.0 2.4 %collective-permute-start.8 = (bf16[256,512]{1,0:T(8,128)(2,1)S(1)}, bf16[256,512]{1,0:T(8,128)(2,1)S(1)}, u32[]{:S(2)}, u32[]{:S(2)}) collective-permute-start(bf16[256,512]{1,0:T(8,128)(2,1)S(1)} %get-tuple-element.35), channel_id=1, source_target_pairs={{0,6},{1,7},{2,0},{3,1},{4,2},{5,3},{6,4},{7,5},{8,14},{9,15},{10,... | collective-permute-start | bytes 786440 | tf_op jit(solution)/shard_map/ppermute | solution.py:146
  36.4 1.7 collective-permute-start.7
  38.1 0.3 collective-permute-start.6
  38.4 2.8 %collective-permute-start.11 = (bf16[2,256,512]{2,1,0:T(8,128)(2,1)S(1)}, bf16[2,256,512]{2,1,0:T(8,128)(2,1)S(1)}, u32[]{:S(2)}, u32[]{:S(2)}) collective-permute-start(bf16[2,256,512]{2,1,0:T(8,128)(2,1)S(1)} %pad_maximum_fusion.3.refs_2_), channel_id=1, source_target_pairs={{0,48},{1,49},{2,50},{3,51},{4,52},{5,53},{6,54},{7,55},{8,56},{9,... | collective-permute-start | bytes 1572872 | tf_op jit(solution)/shard_map/ppermute | solution.py:146
  41.2 0.5 collective-permute-start.10
  41.7 0.7 collective-permute-done.8
  42.5 4.1 %collective-permute-start.9 = (bf16[2,256,512]{2,1,0:T(8,128)(2,1)S(1)}, bf16[2,256,512]{2,1,0:T(8,128)(2,1)S(1)}, u32[]{:S(2)}, u32[]{:S(2)}) collective-permute-start(bf16[2,256,512]{2,1,0:T(8,128)(2,1)S(1)} %pad_maximum_fusion.3.refs_2_), channel_id=1, source_target_pairs={{0,16},{1,17},{2,18},{3,19},{4,20},{5,21},{6,22},{7,23},{8,24},{9,... | collective-permute-start | bytes 1572872 | tf_op jit(solution)/shard_map/ppermute | solution.py:146
  46.7 4.0 %collective-permute-done.6 = bf16[256,512]{1,0:T(8,128)(2,1)} collective-permute-done((bf16[256,512]{1,0:T(8,128)(2,1)S(1)}, bf16[256,512]{1,0:T(8,128)(2,1)}, u32[]{:S(2)}, u32[]{:S(2)}) %collective-permute-start.6) | collective-permute-done | bytes 262176 | tf_op jit(solution)/shard_map/ppermute | solution.py:146
  50.7 2.1 pad_maximum_fusion.1
  52.8 10.8 %collective-permute-done.11.refs_5_ = bf16[2,256,512]{2,1,0:T(8,128)(2,1)S(1)} collective-permute-done((bf16[2,256,512]{2,1,0:T(8,128)(2,1)S(1)}, bf16[2,256,512]{2,1,0:T(8,128)(2,1)S(1)}, u32[]{:S(2)}, u32[]{:S(2)}) %collective-permute-start.11) | collective-permute-done | bytes 524320 | tf_op jit(solution)/shard_map/ppermute | solution.py:146
  63.6 4.2 %collective-permute-done.9.refs_3_ = bf16[2,256,512]{2,1,0:T(8,128)(2,1)S(1)} collective-permute-done((bf16[2,256,512]{2,1,0:T(8,128)(2,1)S(1)}, bf16[2,256,512]{2,1,0:T(8,128)(2,1)S(1)}, u32[]{:S(2)}, u32[]{:S(2)}) %collective-permute-start.9) | collective-permute-done | bytes 524320 | tf_op jit(solution)/shard_map/ppermute | solution.py:146
  67.8 8.7 %product.4 = bf16[8,256,512]{2,1,0:T(8,128)(2,1)} custom-call(s32[8]{0:T(128)S(1)} %broadcast_xor_fusion.1.order_ref, s32[8]{0:T(128)S(1)} %stack.156.place_ref, bf16[16,256,2048]{2,1,0:T(8,128)(2,1)} %bitcast.85, bf16[16,256,2048]{2,1,0:T(8,128)(2,1)} %bitcast.86, bf16[2,256,512]{2,1,0:T(8,128)(2,1)S(1)} %pad_maximum_fusion.3.refs_2_, ...), custom_call_target="tpu_custom_call" | custom-call | flops 4294967296 | bytes 10485760 | tf_op jit(solution)/shard_map/product/pallas_call | solution.py:220
  76.5 0.6 collective-permute-start.12
  77.2 10.2 %collective-permute-start.17 = (bf16[4,256,512]{2,1,0:T(8,128)(2,1)}, bf16[4,256,512]{2,1,0:T(8,128)(2,1)S(1)}, u32[]{:S(2)}, u32[]{:S(2)}) collective-permute-start(bf16[4,256,512]{2,1,0:T(8,128)(2,1)} %pad_maximum_fusion.1), channel_id=1, source_target_pairs={{0,0},{1,64},{2,2},{3,66},{4,4},{5,68},{6,6},{7,70},{8,8},{9,72},{... | collective-permute-start | bytes 3145736 | tf_op jit(solution)/shard_map/ppermute | solution.py:146
  87.6 1.0 copy-done.1
  88.6 1.0 copy-done.3
  89.7 9.3 %product.5 = (f32[2,256,512]{2,1,0:T(8,128)S(1)}, bf16[2,256,512]{2,1,0:T(8,128)(2,1)}, bf16[2,256,512]{2,1,0:T(8,128)(2,1)}, bf16[2,256,512]{2,1,0:T(8,128)(2,1)}) custom-call(s32[8]{0:T(128)S(1)} %stack.135.order_ref, s32[8]{0:T(128)S(1)} %stack.156.place_ref, bf16[16,256,2048]{2,1,0:T(8,128)(2,1)} %bitcast.87, bf16[16,256,2048]{2,1,0:T(8,128)(2,1)} %bitcast.88, ...), custom_call_target="tpu_custom_call" | custom-call | flops 4294967296 | bytes 10485760 | tf_op jit(solution)/shard_map/product/pallas_call | solution.py:220
  98.9 7.2 %collective-permute-done.18.refs_3_ = bf16[4,256,512]{2,1,0:T(8,128)(2,1)S(1)} collective-permute-done((bf16[4,256,512]{2,1,0:T(8,128)(2,1)}, bf16[4,256,512]{2,1,0:T(8,128)(2,1)S(1)}, u32[]{:S(2)}, u32[]{:S(2)}) %collective-permute-start.18) | collective-permute-done | bytes 1048608 | tf_op jit(solution)/shard_map/ppermute | solution.py:146
  106.2 2.8 %collective-permute-done.17.refs_2_ = bf16[4,256,512]{2,1,0:T(8,128)(2,1)S(1)} collective-permute-done((bf16[4,256,512]{2,1,0:T(8,128)(2,1)}, bf16[4,256,512]{2,1,0:T(8,128)(2,1)S(1)}, u32[]{:S(2)}, u32[]{:S(2)}) %collective-permute-start.17) | collective-permute-done | bytes 1048608 | tf_op jit(solution)/shard_map/ppermute | solution.py:146
  109.0 8.7 %product.6 = bf16[8,256,512]{2,1,0:T(8,128)(2,1)} custom-call(s32[8]{0:T(128)S(1)} %broadcast_xor_fusion.order_ref, s32[8]{0:T(128)S(1)} %stack.165.place_ref, bf16[16,256,2048]{2,1,0:T(8,128)(2,1)} %bitcast.89, bf16[16,256,2048]{2,1,0:T(8,128)(2,1)} %bitcast.90, bf16[4,256,512]{2,1,0:T(8,128)(2,1)S(1)} %collective-permute-done.17.refs_2_, ...), custom_call_target="tpu_custom_call" | custom-call | flops 4294967296 | bytes 10485760 | tf_op jit(solution)/shard_map/product/pallas_call | solution.py:220
  117.7 3.2 %collective-permute-start.14 = (bf16[2,256,512]{2,1,0:T(8,128)(2,1)}, bf16[2,256,512]{2,1,0:T(8,128)(2,1)}, u32[]{:S(2)}, u32[]{:S(2)}) collective-permute-start(bf16[2,256,512]{2,1,0:T(8,128)(2,1)} %get-tuple-element.21), channel_id=1, source_target_pairs={{0,4},{1,5},{2,6},{3,7},{4,0},{5,1},{6,2},{7,3},{8,12},{9,13},{10,... | collective-permute-start | bytes 1572872 | tf_op jit(solution)/shard_map/ppermute | solution.py:146
  121.1 1.6 copy-done.10
  122.7 8.4 %eliminate.5.in_ref = f32[2,512,512]{2,1,0:T(8,128)S(1)} custom-call(f32[2,512,512]{2,1,0:T(8,128)S(1)} %copy-done.10, s32[2,512]{1,0:T(2,128)S(1)} %copy-done.8), custom_call_target="tpu_custom_call" | custom-call | flops 5000000000 | bytes 4194304 | tf_op jit(solution)/shard_map/eliminate/pallas_call | solution.py:119
  131.1 1.1 collective-permute-done.13
  132.2 11.9 %collective-permute-done.14 = bf16[2,256,512]{2,1,0:T(8,128)(2,1)} collective-permute-done((bf16[2,256,512]{2,1,0:T(8,128)(2,1)}, bf16[2,256,512]{2,1,0:T(8,128)(2,1)}, u32[]{:S(2)}, u32[]{:S(2)}) %collective-permute-start.14) | collective-permute-done | bytes 524320 | tf_op jit(solution)/shard_map/ppermute | solution.py:146
  144.1 1.5 convert_add_fusion.2
  145.6 1.1 collective-permute-start.16
  146.7 8.2 %product.7 = (f32[2,256,512]{2,1,0:T(8,128)S(1)}, bf16[2,256,512]{2,1,0:T(8,128)(2,1)S(1)}, bf16[2,256,512]{2,1,0:T(8,128)(2,1)S(1)}, bf16[2,256,512]{2,1,0:T(8,128)(2,1)S(1)}) custom-call(s32[8]{0:T(128)S(1)} %stack.135.order_ref, s32[8]{0:T(128)S(1)} %stack.165.place_ref, bf16[16,256,2048]{2,1,0:T(8,128)(2,1)} %bitcast.91, ...), custom_call_target="tpu_custom_call" | custom-call | flops 4294967296 | bytes 10485760 | tf_op jit(solution)/shard_map/product/pallas_call | solution.py:220
  154.8 2.3 collective-permute-start.20
  157.1 2.3 collective-permute-start.21
  159.6 8.4 %eliminate.6.in_ref = f32[2,512,512]{2,1,0:T(8,128)S(1)} custom-call(f32[2,512,512]{2,1,0:T(8,128)S(1)} %eliminate.5.in_ref, s32[2,512]{1,0:T(2,128)S(1)} %copy-done.8), custom_call_target="tpu_custom_call" | custom-call | flops 5000000000 | bytes 4194304 | tf_op jit(solution)/shard_map/eliminate/pallas_call | solution.py:119
  168.0 8.4 %eliminate.7 = f32[2,512,512]{2,1,0:T(8,128)S(1)} custom-call(f32[2,512,512]{2,1,0:T(8,128)S(1)} %eliminate.6.in_ref, s32[2,512]{1,0:T(2,128)S(1)} %copy-done.8), custom_call_target="tpu_custom_call" | custom-call | flops 5000000000 | bytes 4194304 | tf_op jit(solution)/shard_map/eliminate/pallas_call | solution.py:119
  176.5 1.1 fusion.1
  177.6 0.7 convolution_convert_fusion.1
  178.3 0.7 fusion.24
  178.9 3.0 %collective-permute-done.21 = bf16[2,256,512]{2,1,0:T(8,128)(2,1)S(1)} collective-permute-done((bf16[2,256,512]{2,1,0:T(8,128)(2,1)S(1)}, bf16[2,256,512]{2,1,0:T(8,128)(2,1)S(1)}, u32[]{:S(2)}, u32[]{:S(2)}) %collective-permute-start.21) | collective-permute-done | bytes 524320 | tf_op jit(solution)/shard_map/ppermute | solution.py:146
  181.9 0.3 convert_add_fusion.1
  182.2 0.5 collective-permute-start.23
  182.7 0.7 convolution_convert_fusion
  183.4 5.1 %collective-permute-done.23 = bf16[256,512]{1,0:T(8,128)(2,1)S(1)} collective-permute-done((bf16[256,512]{1,0:T(8,128)(2,1)S(1)}, bf16[256,512]{1,0:T(8,128)(2,1)S(1)}, u32[]{:S(2)}, u32[]{:S(2)}) %collective-permute-start.23) | collective-permute-done | bytes 262176 | tf_op jit(solution)/shard_map/ppermute | solution.py:146
  188.5 1.1 fusion.2
  189.6 0.7 broadcast_select_fusion.2
  190.3 2.6 %collective-permute-start.24 = (f32[512,512]{1,0:T(8,128)S(1)}, f32[512,512]{1,0:T(8,128)S(1)}, u32[]{:S(2)}, u32[]{:S(2)}) collective-permute-start(f32[512,512]{1,0:T(8,128)S(1)} %get-tuple-element.40), channel_id=1, source_target_pairs={{0,1},{1,0},{2,3},{3,2},{4,5},{5,4},{6,7},{7,6},{8,9},{9,8},{10,11... | collective-permute-start | bytes 3145736 | tf_op jit(solution)/shard_map/ppermute | solution.py:146
  192.8 2.3 collective-permute-done.24
  195.1 0.4 fusion.3
  195.5 20.8 %all_to_all.10 = bf16[64,8,512]{2,1,0:T(8,128)(2,1)} all-to-all(bf16[64,8,512]{2,1,0:T(8,128)(2,1)S(1)} %fusion.3), channel_id=1, replica_groups=mesh['z_hi'=2,'x'=4,'z_lo'=2,'y'=4,'core'=2] {'z_hi','x','z_lo','y'}, dimensions={0} | all-to-all | bytes 1048576 | tf_op jit(solution)/shard_map/all_to_all | solution.py:247
  216.3 1.1 reduce_sum.12
  217.5 15.8 %all_to_all.11 = bf16[64,8,512]{2,1,0:T(8,128)(2,1)S(1)} all-to-all(bf16[64,8,512]{2,1,0:T(8,128)(2,1)S(1)} %broadcast_in_dim.36), channel_id=1, replica_groups=mesh['z_hi'=2,'x'=4,'z_lo'=2,'y'=4,'core'=2] {'z_hi','x','z_lo','y'}, dimensions={0} | all-to-all | bytes 1048576 | tf_op jit(solution)/shard_map/all_to_all | solution.py:249
  233.3 3.3 %collective-permute-start.25 = (bf16[512,512]{1,0:T(8,128)(2,1)S(1)}, bf16[512,512]{1,0:T(8,128)(2,1)S(1)}, u32[]{:S(2)}, u32[]{:S(2)}) collective-permute-start(bf16[512,512]{1,0:T(8,128)(2,1)S(1)} %bitcast.96), channel_id=1, source_target_pairs={{0,1},{1,0},{2,3},{3,2},{4,5},{5,4},{6,7},{7,6},{8,9},{9,8},{10,11... | collective-permute-start | bytes 1572872 | tf_op jit(solution)/shard_map/ppermute | solution.py:146
  236.6 0.9 fusion
  237.5 0.6 collective-permute-done.25
  238.3 1.7 convert_add_fusion
  (50 shorter events, 1.4 us)
Async XLA Ops:
  2.6 11.5 %collective-permute-start = (bf16[256,512]{1,0:T(8,128)(2,1)S(1)}, bf16[256,512]{1,0:T(8,128)(2,1)S(1)}, u32[]{:S(2)}, u32[]{:S(2)}) collective-permute-start(bf16[256,512]{1,0:T(8,128)(2,1)S(1)} %get-tuple-element.39), channel_id=1, source_target_pairs={{0,0},{1,1},{2,2},{3,3},{4,4},{5,5},{6,6},{7,7},{8,64},{9,65},{10,... | collective-permute-start | bytes 786440 | tf_op jit(solution)/shard_map/ppermute | solution.py:146
  3.3 26.9 %collective-permute-start.5 = (bf16[256,512]{1,0:T(8,128)(2,1)S(1)}, bf16[256,512]{1,0:T(8,128)(2,1)S(1)}, u32[]{:S(2)}, u32[]{:S(2)}) collective-permute-start(bf16[256,512]{1,0:T(8,128)(2,1)S(1)} %get-tuple-element.38), channel_id=1, source_target_pairs={{0,64},{1,80},{2,96},{3,112},{4,0},{5,16},{6,32},{7,48},{8,65},{9,... | collective-permute-start | bytes 786440 | tf_op jit(solution)/shard_map/ppermute | solution.py:146
  10.6 19.6 %collective-permute-start.4 = (bf16[256,512]{1,0:T(8,128)(2,1)S(1)}, bf16[256,512]{1,0:T(8,128)(2,1)S(1)}, u32[]{:S(2)}, u32[]{:S(2)}) collective-permute-start(bf16[256,512]{1,0:T(8,128)(2,1)S(1)} %get-tuple-element.38), channel_id=1, source_target_pairs={{0,0},{1,16},{2,32},{3,48},{4,64},{5,80},{6,96},{7,112},{8,1},{9,1... | collective-permute-start | bytes 786440 | tf_op jit(solution)/shard_map/ppermute | solution.py:146
  14.0 16.2 %collective-permute-start.3 = (bf16[256,512]{1,0:T(8,128)(2,1)S(1)}, bf16[256,512]{1,0:T(8,128)(2,1)S(1)}, u32[]{:S(2)}, u32[]{:S(2)}) collective-permute-start(bf16[256,512]{1,0:T(8,128)(2,1)S(1)} %collective-permute-done), channel_id=1, source_target_pairs={{0,48},{1,49},{2,50},{3,51},{4,52},{5,53},{6,54},{7,55},{8,56},{9,... | collective-permute-start | bytes 786440 | tf_op jit(solution)/shard_map/ppermute | solution.py:146
  17.4 12.8 %collective-permute-start.2 = (bf16[256,512]{1,0:T(8,128)(2,1)S(1)}, bf16[256,512]{1,0:T(8,128)(2,1)S(1)}, u32[]{:S(2)}, u32[]{:S(2)}) collective-permute-start(bf16[256,512]{1,0:T(8,128)(2,1)S(1)} %collective-permute-done), channel_id=1, source_target_pairs={{0,32},{1,33},{2,34},{3,35},{4,36},{5,37},{6,38},{7,39},{8,40},{9,... | collective-permute-start | bytes 786440 | tf_op jit(solution)/shard_map/ppermute | solution.py:146
  17.4 16.4 %collective-permute-start.1 = (bf16[256,512]{1,0:T(8,128)(2,1)S(1)}, bf16[256,512]{1,0:T(8,128)(2,1)S(1)}, u32[]{:S(2)}, u32[]{:S(2)}) collective-permute-start(bf16[256,512]{1,0:T(8,128)(2,1)S(1)} %collective-permute-done), channel_id=1, source_target_pairs={{0,16},{1,17},{2,18},{3,19},{4,20},{5,21},{6,22},{7,23},{8,24},{9,... | collective-permute-start | bytes 786440 | tf_op jit(solution)/shard_map/ppermute | solution.py:146
  18.1 1.6 copy-start.6
  19.7 0.7 copy-start.7
  28.9 1.3 copy-start.9
  34.0 8.4 %collective-permute-start.8 = (bf16[256,512]{1,0:T(8,128)(2,1)S(1)}, bf16[256,512]{1,0:T(8,128)(2,1)S(1)}, u32[]{:S(2)}, u32[]{:S(2)}) collective-permute-start(bf16[256,512]{1,0:T(8,128)(2,1)S(1)} %get-tuple-element.35), channel_id=1, source_target_pairs={{0,6},{1,7},{2,0},{3,1},{4,2},{5,3},{6,4},{7,5},{8,14},{9,15},{10,... | collective-permute-start | bytes 786440 | tf_op jit(solution)/shard_map/ppermute | solution.py:146
  36.4 10.3 %collective-permute-start.7 = (bf16[256,512]{1,0:T(8,128)(2,1)S(1)}, bf16[256,512]{1,0:T(8,128)(2,1)S(1)}, u32[]{:S(2)}, u32[]{:S(2)}) collective-permute-start(bf16[256,512]{1,0:T(8,128)(2,1)S(1)} %get-tuple-element.36), channel_id=1, source_target_pairs={{0,4},{1,5},{2,6},{3,7},{4,0},{5,1},{6,2},{7,3},{8,12},{9,13},{10,... | collective-permute-start | bytes 786440 | tf_op jit(solution)/shard_map/ppermute | solution.py:146
  38.1 12.6 %collective-permute-start.6 = (bf16[256,512]{1,0:T(8,128)(2,1)S(1)}, bf16[256,512]{1,0:T(8,128)(2,1)}, u32[]{:S(2)}, u32[]{:S(2)}) collective-permute-start(bf16[256,512]{1,0:T(8,128)(2,1)S(1)} %get-tuple-element.37), channel_id=1, source_target_pairs={{0,2},{1,3},{2,4},{3,5},{4,6},{5,7},{6,0},{7,1},{8,10},{9,11},{10,... | collective-permute-start | bytes 786440 | tf_op jit(solution)/shard_map/ppermute | solution.py:146
  38.4 25.2 %collective-permute-start.11 = (bf16[2,256,512]{2,1,0:T(8,128)(2,1)S(1)}, bf16[2,256,512]{2,1,0:T(8,128)(2,1)S(1)}, u32[]{:S(2)}, u32[]{:S(2)}) collective-permute-start(bf16[2,256,512]{2,1,0:T(8,128)(2,1)S(1)} %pad_maximum_fusion.3.refs_2_), channel_id=1, source_target_pairs={{0,48},{1,49},{2,50},{3,51},{4,52},{5,53},{6,54},{7,55},{8,56},{9,... | collective-permute-start | bytes 1572872 | tf_op jit(solution)/shard_map/ppermute | solution.py:146
  41.2 22.4 %collective-permute-start.10 = (bf16[2,256,512]{2,1,0:T(8,128)(2,1)S(1)}, bf16[2,256,512]{2,1,0:T(8,128)(2,1)S(1)}, u32[]{:S(2)}, u32[]{:S(2)}) collective-permute-start(bf16[2,256,512]{2,1,0:T(8,128)(2,1)S(1)} %pad_maximum_fusion.3.refs_2_), channel_id=1, source_target_pairs={{0,32},{1,33},{2,34},{3,35},{4,36},{5,37},{6,38},{7,39},{8,40},{9,... | collective-permute-start | bytes 1572872 | tf_op jit(solution)/shard_map/ppermute | solution.py:146
  42.5 25.4 %collective-permute-start.9 = (bf16[2,256,512]{2,1,0:T(8,128)(2,1)S(1)}, bf16[2,256,512]{2,1,0:T(8,128)(2,1)S(1)}, u32[]{:S(2)}, u32[]{:S(2)}) collective-permute-start(bf16[2,256,512]{2,1,0:T(8,128)(2,1)S(1)} %pad_maximum_fusion.3.refs_2_), channel_id=1, source_target_pairs={{0,16},{1,17},{2,18},{3,19},{4,20},{5,21},{6,22},{7,23},{8,24},{9,... | collective-permute-start | bytes 1572872 | tf_op jit(solution)/shard_map/ppermute | solution.py:146
  63.6 12.9 %copy-start = (bf16[2,256,512]{2,1,0:T(8,128)(2,1)}, bf16[2,256,512]{2,1,0:T(8,128)(2,1)S(1)}, u32[]{:S(2)}) copy-start(bf16[2,256,512]{2,1,0:T(8,128)(2,1)S(1)} %collective-permute-done.10.refs_4_) | copy-start | bytes 1572868
  67.8 8.7 %copy-start.2 = (bf16[2,256,512]{2,1,0:T(8,128)(2,1)}, bf16[2,256,512]{2,1,0:T(8,128)(2,1)S(1)}, u32[]{:S(2)}) copy-start(bf16[2,256,512]{2,1,0:T(8,128)(2,1)S(1)} %collective-permute-done.9.refs_3_) | copy-start | bytes 1572868
  76.5 11.1 %collective-permute-start.12 = (bf16[8,256,512]{2,1,0:T(8,128)(2,1)}, bf16[8,256,512]{2,1,0:T(8,128)(2,1)}, u32[]{:S(2)}, u32[]{:S(2)}) collective-permute-start(bf16[8,256,512]{2,1,0:T(8,128)(2,1)} %product.4), channel_id=1, source_target_pairs={{0,1},{1,0},{2,3},{3,2},{4,5},{5,4},{6,7},{7,6},{8,9},{9,8},{10,11... | collective-permute-start | bytes 6291464 | tf_op jit(solution)/shard_map/ppermute | solution.py:146
  77.1 29.1 %collective-permute-start.18 = (bf16[4,256,512]{2,1,0:T(8,128)(2,1)}, bf16[4,256,512]{2,1,0:T(8,128)(2,1)S(1)}, u32[]{:S(2)}, u32[]{:S(2)}) collective-permute-start(bf16[4,256,512]{2,1,0:T(8,128)(2,1)} %pad_maximum_fusion.1), channel_id=1, source_target_pairs={{0,64},{1,0},{2,66},{3,2},{4,68},{5,4},{6,70},{7,6},{8,72},{9,8},{... | collective-permute-start | bytes 3145736 | tf_op jit(solution)/shard_map/ppermute | solution.py:146
  77.2 31.8 %collective-permute-start.17 = (bf16[4,256,512]{2,1,0:T(8,128)(2,1)}, bf16[4,256,512]{2,1,0:T(8,128)(2,1)S(1)}, u32[]{:S(2)}, u32[]{:S(2)}) collective-permute-start(bf16[4,256,512]{2,1,0:T(8,128)(2,1)} %pad_maximum_fusion.1), channel_id=1, source_target_pairs={{0,0},{1,64},{2,2},{3,66},{4,4},{5,68},{6,6},{7,70},{8,8},{9,72},{... | collective-permute-start | bytes 3145736 | tf_op jit(solution)/shard_map/ppermute | solution.py:146
  87.6 1.0 copy-start.1
  88.6 1.0 copy-start.3
  98.9 18.7 %copy-start.4 = (f32[2,256,512]{2,1,0:T(8,128)}, f32[2,256,512]{2,1,0:T(8,128)S(1)}, u32[]{:S(2)}) copy-start(f32[2,256,512]{2,1,0:T(8,128)S(1)} %get-tuple-element.19) | copy-start | bytes 3145732
  98.9 22.2 %copy-start.8 = (s32[2,512]{1,0:T(2,128)S(1)}, s32[2,512]{1,0:T(2,128)}, u32[]{:S(2)}) copy-start(s32[2,512]{1,0:T(2,128)} %flag_ref.7) | copy-start | bytes 12292
  117.7 29.0 %collective-permute-start.19 = (bf16[8,256,512]{2,1,0:T(8,128)(2,1)}, bf16[8,256,512]{2,1,0:T(8,128)(2,1)}, u32[]{:S(2)}, u32[]{:S(2)}) collective-permute-start(bf16[8,256,512]{2,1,0:T(8,128)(2,1)} %product.6), channel_id=1, source_target_pairs={{0,1},{1,0},{2,3},{3,2},{4,5},{5,4},{6,7},{7,6},{8,9},{9,8},{10,11... | collective-permute-start | bytes 6291464 | tf_op jit(solution)/shard_map/ppermute | solution.py:146
  117.7 14.5 %collective-permute-start.13 = (bf16[2,256,512]{2,1,0:T(8,128)(2,1)}, bf16[2,256,512]{2,1,0:T(8,128)(2,1)S(1)}, u32[]{:S(2)}, u32[]{:S(2)}) collective-permute-start(bf16[2,256,512]{2,1,0:T(8,128)(2,1)} %get-tuple-element.20), channel_id=1, source_target_pairs={{0,2},{1,3},{2,4},{3,5},{4,6},{5,7},{6,0},{7,1},{8,10},{9,11},{10,... | collective-permute-start | bytes 1572872 | tf_op jit(solution)/shard_map/ppermute | solution.py:146
  117.7 26.3 %collective-permute-start.14 = (bf16[2,256,512]{2,1,0:T(8,128)(2,1)}, bf16[2,256,512]{2,1,0:T(8,128)(2,1)}, u32[]{:S(2)}, u32[]{:S(2)}) collective-permute-start(bf16[2,256,512]{2,1,0:T(8,128)(2,1)} %get-tuple-element.21), channel_id=1, source_target_pairs={{0,4},{1,5},{2,6},{3,7},{4,0},{5,1},{6,2},{7,3},{8,12},{9,13},{10,... | collective-permute-start | bytes 1572872 | tf_op jit(solution)/shard_map/ppermute | solution.py:146
  120.9 23.1 %collective-permute-start.15 = (bf16[2,256,512]{2,1,0:T(8,128)(2,1)}, bf16[2,256,512]{2,1,0:T(8,128)(2,1)}, u32[]{:S(2)}, u32[]{:S(2)}) collective-permute-start(bf16[2,256,512]{2,1,0:T(8,128)(2,1)} %get-tuple-element.22), channel_id=1, source_target_pairs={{0,6},{1,7},{2,0},{3,1},{4,2},{5,3},{6,4},{7,5},{8,14},{9,15},{10,... | collective-permute-start | bytes 1572872 | tf_op jit(solution)/shard_map/ppermute | solution.py:146
  121.1 1.6 copy-start.10
  122.7 21.4 %copy-start.5 = (f32[2,256,512]{2,1,0:T(8,128)S(1)}, f32[2,256,512]{2,1,0:T(8,128)}, u32[]{:S(2)}) copy-start(f32[2,256,512]{2,1,0:T(8,128)} %copy-done.4) | copy-start | bytes 3145732
  145.6 30.9 %collective-permute-start.16 = (bf16[256,512]{1,0:T(8,128)(2,1)S(1)}, bf16[256,512]{1,0:T(8,128)(2,1)S(1)}, u32[]{:S(2)}, u32[]{:S(2)}) collective-permute-start(bf16[256,512]{1,0:T(8,128)(2,1)S(1)} %fusion.10), channel_id=1, source_target_pairs={{0,8},{1,9},{2,10},{3,11},{4,12},{5,13},{6,14},{7,15},{8,0},{9,1},... | collective-permute-start | bytes 786440 | tf_op jit(solution)/shard_map/ppermute | solution.py:146
  154.8 24.1 %collective-permute-start.20 = (bf16[2,256,512]{2,1,0:T(8,128)(2,1)S(1)}, bf16[2,256,512]{2,1,0:T(8,128)(2,1)S(1)}, u32[]{:S(2)}, u32[]{:S(2)}) collective-permute-start(bf16[2,256,512]{2,1,0:T(8,128)(2,1)S(1)} %get-tuple-element.25), channel_id=1, source_target_pairs={{0,2},{1,3},{2,4},{3,5},{4,6},{5,7},{6,0},{7,1},{8,10},{9,11},{10,... | collective-permute-start | bytes 1572872 | tf_op jit(solution)/shard_map/ppermute | solution.py:146
  157.1 24.8 %collective-permute-start.21 = (bf16[2,256,512]{2,1,0:T(8,128)(2,1)S(1)}, bf16[2,256,512]{2,1,0:T(8,128)(2,1)S(1)}, u32[]{:S(2)}, u32[]{:S(2)}) collective-permute-start(bf16[2,256,512]{2,1,0:T(8,128)(2,1)S(1)} %get-tuple-element.26), channel_id=1, source_target_pairs={{0,4},{1,5},{2,6},{3,7},{4,0},{5,1},{6,2},{7,3},{8,12},{9,13},{10,... | collective-permute-start | bytes 1572872 | tf_op jit(solution)/shard_map/ppermute | solution.py:146
  159.4 22.5 %collective-permute-start.22 = (bf16[2,256,512]{2,1,0:T(8,128)(2,1)S(1)}, bf16[2,256,512]{2,1,0:T(8,128)(2,1)S(1)}, u32[]{:S(2)}, u32[]{:S(2)}) collective-permute-start(bf16[2,256,512]{2,1,0:T(8,128)(2,1)S(1)} %get-tuple-element.27), channel_id=1, source_target_pairs={{0,6},{1,7},{2,0},{3,1},{4,2},{5,3},{6,4},{7,5},{8,14},{9,15},{10,... | collective-permute-start | bytes 1572872 | tf_op jit(solution)/shard_map/ppermute | solution.py:146
  176.4 1.1 copy-start.11
  182.2 6.3 %collective-permute-start.23 = (bf16[256,512]{1,0:T(8,128)(2,1)S(1)}, bf16[256,512]{1,0:T(8,128)(2,1)S(1)}, u32[]{:S(2)}, u32[]{:S(2)}) collective-permute-start(bf16[256,512]{1,0:T(8,128)(2,1)S(1)} %fusion.11), channel_id=1, source_target_pairs={{0,8},{1,9},{2,10},{3,11},{4,12},{5,13},{6,14},{7,15},{8,0},{9,1},... | collective-permute-start | bytes 786440 | tf_op jit(solution)/shard_map/ppermute | solution.py:146
  190.3 4.9 %collective-permute-start.24 = (f32[512,512]{1,0:T(8,128)S(1)}, f32[512,512]{1,0:T(8,128)S(1)}, u32[]{:S(2)}, u32[]{:S(2)}) collective-permute-start(f32[512,512]{1,0:T(8,128)S(1)} %get-tuple-element.40), channel_id=1, source_target_pairs={{0,1},{1,0},{2,3},{3,2},{4,5},{5,4},{6,7},{7,6},{8,9},{9,8},{10,11... | collective-permute-start | bytes 3145736 | tf_op jit(solution)/shard_map/ppermute | solution.py:146
  233.3 4.9 %collective-permute-start.25 = (bf16[512,512]{1,0:T(8,128)(2,1)S(1)}, bf16[512,512]{1,0:T(8,128)(2,1)S(1)}, u32[]{:S(2)}, u32[]{:S(2)}) collective-permute-start(bf16[512,512]{1,0:T(8,128)(2,1)S(1)} %bitcast.96), channel_id=1, source_target_pairs={{0,1},{1,0},{2,3},{3,2},{4,5},{5,4},{6,7},{7,6},{8,9},{9,8},{10,11... | collective-permute-start | bytes 1572872 | tf_op jit(solution)/shard_map/ppermute | solution.py:146

commit v5 on v4

--- a/solution.py
+++ b/solution.py
@@ -315,15 +315,17 @@
         for d, part in zip((1, 2, 3), leaving):
             arrived = shift(part, y=d)
             summed = summed + arrived.astype(jnp.float32)
-        arrived = shift(summed[1].astype(jnp.bfloat16), z_lo=1)
+        rising = summed[1].astype(jnp.bfloat16)
+        arrived = shift(rising, z_lo=1)
         sums.append(summed[0] + arrived.astype(jnp.float32))
 
     state = eliminate(2, after(state, *leaving), pivot_flags)
     inverses = eliminate(3, state, pivot_flags)
+    ready = after(inverses, rising)
     applied, terms = [], []
     for k in range(nodes):
-        applied.append(jnp.dot(sums[k], inverses[k], precision=HIGHEST))
-        normed = jnp.dot(masked[k].astype(jnp.float32), inverses[k], precision=HIGHEST)
+        applied.append(jnp.dot(sums[k], ready[k], precision=HIGHEST))
+        normed = jnp.dot(masked[k].astype(jnp.float32), ready[k], precision=HIGHEST)
         terms.append(
             lax.dot_general(
                 normed.astype(jnp.bfloat16).astype(jnp.float32),

time: 241 us -> 241 us (level)
  no operation moved by 1% of the time
where the time goes in v5:
time: 241 us; the launch traced here: 240 us
  Pallas kernels  68.5 us (28%)
  waiting for transfers between devices  57 us (24%)
  starting transfers between devices  53.8 us (22%)
  blocking collectives  36.6 us (15%)
  other arithmetic  10.3 us (4%)
  local copies, waits for them, and re-layouts  7.96 us (3%)
  matrix products  4.9 us (2%)
    ppermute x26, waiting for transfers between devices, send(): return lax.ppermute(value, AXES, moves)  57 us
    ppermute x26, starting transfers between devices, send(): return lax.ppermute(value, AXES, moves)  53.8 us
    pallas_call x4, Pallas kernels, product(): pl.pallas_call(kernel, out_shape=out_shape, grid_spec=pltpu.PrefetchScala...  34.8 us
    pallas_call x4, Pallas kernels, eliminate(): pl.pallas_call(functools.partial(inverse_kernel, block), out_shape=jax.Sh...  33.7 us
    all_to_all x1, blocking collectives, total(): slices = lax.all_to_all(slices, CHIPS, 0, 0)  20.8 us
    all_to_all x1, blocking collectives, total(): spread = lax.all_to_all(jnp.broadcast_to(summed, slices.shape), CHIPS, 0, 0)  15.8 us
    unnamed x24, local copies, waits for them, and re-layouts  7.52 us
  transfers between devices with their start and end apart: 26, of which 13 were waited for; matrix products, arithmetic and copies ran while one was open for 3% of the time, Pallas kernels for 21%

profile of v5, /device:TPU:1, one launch (start us, length us, event | category | flops | bytes accessed | tf_op | source)
XLA Modules:
  0.0 240.1 jit_solution(8481370760344285429)
XLA Ops:
  0.6 0.8 compare_reduce_fusion
  1.4 1.2 bitcast_select_fusion
  2.6 0.7 collective-permute-start
  3.3 7.3 %collective-permute-start.5 = (bf16[256,512]{1,0:T(8,128)(2,1)S(1)}, bf16[256,512]{1,0:T(8,128)(2,1)S(1)}, u32[]{:S(2)}, u32[]{:S(2)}) collective-permute-start(bf16[256,512]{1,0:T(8,128)(2,1)S(1)} %get-tuple-element.40), channel_id=1, source_target_pairs={{0,64},{1,80},{2,96},{3,112},{4,0},{5,16},{6,32},{7,48},{8,65},{9,... | collective-permute-start | bytes 786440 | tf_op jit(solution)/shard_map/ppermute | solution.py:146
  10.6 3.4 %collective-permute-start.4 = (bf16[256,512]{1,0:T(8,128)(2,1)S(1)}, bf16[256,512]{1,0:T(8,128)(2,1)S(1)}, u32[]{:S(2)}, u32[]{:S(2)}) collective-permute-start(bf16[256,512]{1,0:T(8,128)(2,1)S(1)} %get-tuple-element.40), channel_id=1, source_target_pairs={{0,0},{1,16},{2,32},{3,48},{4,64},{5,80},{6,96},{7,112},{8,1},{9,1... | collective-permute-start | bytes 786440 | tf_op jit(solution)/shard_map/ppermute | solution.py:146
  14.0 3.4 %collective-permute-start.3 = (bf16[256,512]{1,0:T(8,128)(2,1)S(1)}, bf16[256,512]{1,0:T(8,128)(2,1)S(1)}, u32[]{:S(2)}, u32[]{:S(2)}) collective-permute-start(bf16[256,512]{1,0:T(8,128)(2,1)S(1)} %collective-permute-done), channel_id=1, source_target_pairs={{0,48},{1,49},{2,50},{3,51},{4,52},{5,53},{6,54},{7,55},{8,56},{9,... | collective-permute-start | bytes 786440 | tf_op jit(solution)/shard_map/ppermute | solution.py:146
  17.4 0.7 collective-permute-start.1
  18.1 1.6 copy-done.6
  19.7 0.7 copy-done.7
  20.4 8.5 %eliminate.4.in_ref = f32[2,512,512]{2,1,0:T(8,128)S(1)} custom-call(f32[2,512,512]{2,1,0:T(8,128)S(1)} %copy-done.6, s32[2,512]{1,0:T(2,128)S(1)} %copy-done.7), custom_call_target="tpu_custom_call" | custom-call | flops 5000000000 | bytes 4194304 | tf_op jit(solution)/shard_map/eliminate/pallas_call | solution.py:119
  28.9 1.3 copy-done.9
  30.3 3.5 %collective-permute-done.1 = bf16[256,512]{1,0:T(8,128)(2,1)S(1)} collective-permute-done((bf16[256,512]{1,0:T(8,128)(2,1)S(1)}, bf16[256,512]{1,0:T(8,128)(2,1)S(1)}, u32[]{:S(2)}, u32[]{:S(2)}) %collective-permute-start.1) | collective-permute-done | bytes 262176 | tf_op jit(solution)/shard_map/ppermute | solution.py:146
  34.0 2.4 %collective-permute-start.8 = (bf16[256,512]{1,0:T(8,128)(2,1)S(1)}, bf16[256,512]{1,0:T(8,128)(2,1)S(1)}, u32[]{:S(2)}, u32[]{:S(2)}) collective-permute-start(bf16[256,512]{1,0:T(8,128)(2,1)S(1)} %get-tuple-element.37), channel_id=1, source_target_pairs={{0,6},{1,7},{2,0},{3,1},{4,2},{5,3},{6,4},{7,5},{8,14},{9,15},{10,... | collective-permute-start | bytes 786440 | tf_op jit(solution)/shard_map/ppermute | solution.py:146
  36.4 1.7 collective-permute-start.7
  38.1 0.3 collective-permute-start.6
  38.4 2.8 %collective-permute-start.11 = (bf16[2,256,512]{2,1,0:T(8,128)(2,1)S(1)}, bf16[2,256,512]{2,1,0:T(8,128)(2,1)S(1)}, u32[]{:S(2)}, u32[]{:S(2)}) collective-permute-start(bf16[2,256,512]{2,1,0:T(8,128)(2,1)S(1)} %pad_maximum_fusion.3.refs_2_), channel_id=1, source_target_pairs={{0,48},{1,49},{2,50},{3,51},{4,52},{5,53},{6,54},{7,55},{8,56},{9,... | collective-permute-start | bytes 1572872 | tf_op jit(solution)/shard_map/ppermute | solution.py:146
  41.2 0.5 collective-permute-start.10
  41.7 0.7 collective-permute-done.8
  42.5 4.1 %collective-permute-start.9 = (bf16[2,256,512]{2,1,0:T(8,128)(2,1)S(1)}, bf16[2,256,512]{2,1,0:T(8,128)(2,1)S(1)}, u32[]{:S(2)}, u32[]{:S(2)}) collective-permute-start(bf16[2,256,512]{2,1,0:T(8,128)(2,1)S(1)} %pad_maximum_fusion.3.refs_2_), channel_id=1, source_target_pairs={{0,16},{1,17},{2,18},{3,19},{4,20},{5,21},{6,22},{7,23},{8,24},{9,... | collective-permute-start | bytes 1572872 | tf_op jit(solution)/shard_map/ppermute | solution.py:146
  46.7 4.0 %collective-permute-done.6 = bf16[256,512]{1,0:T(8,128)(2,1)} collective-permute-done((bf16[256,512]{1,0:T(8,128)(2,1)S(1)}, bf16[256,512]{1,0:T(8,128)(2,1)}, u32[]{:S(2)}, u32[]{:S(2)}) %collective-permute-start.6) | collective-permute-done | bytes 262176 | tf_op jit(solution)/shard_map/ppermute | solution.py:146
  50.7 2.1 pad_maximum_fusion.1
  52.8 10.8 %collective-permute-done.11.refs_5_ = bf16[2,256,512]{2,1,0:T(8,128)(2,1)S(1)} collective-permute-done((bf16[2,256,512]{2,1,0:T(8,128)(2,1)S(1)}, bf16[2,256,512]{2,1,0:T(8,128)(2,1)S(1)}, u32[]{:S(2)}, u32[]{:S(2)}) %collective-permute-start.11) | collective-permute-done | bytes 524320 | tf_op jit(solution)/shard_map/ppermute | solution.py:146
  63.6 4.2 %collective-permute-done.9.refs_3_ = bf16[2,256,512]{2,1,0:T(8,128)(2,1)S(1)} collective-permute-done((bf16[2,256,512]{2,1,0:T(8,128)(2,1)S(1)}, bf16[2,256,512]{2,1,0:T(8,128)(2,1)S(1)}, u32[]{:S(2)}, u32[]{:S(2)}) %collective-permute-start.9) | collective-permute-done | bytes 524320 | tf_op jit(solution)/shard_map/ppermute | solution.py:146
  67.8 8.7 %product.4 = bf16[8,256,512]{2,1,0:T(8,128)(2,1)} custom-call(s32[8]{0:T(128)S(1)} %broadcast_xor_fusion.1.order_ref, s32[8]{0:T(128)S(1)} %stack.156.place_ref, bf16[16,256,2048]{2,1,0:T(8,128)(2,1)} %bitcast.87, bf16[16,256,2048]{2,1,0:T(8,128)(2,1)} %bitcast.88, bf16[2,256,512]{2,1,0:T(8,128)(2,1)S(1)} %pad_maximum_fusion.3.refs_2_, ...), custom_call_target="tpu_custom_call" | custom-call | flops 4294967296 | bytes 10485760 | tf_op jit(solution)/shard_map/product/pallas_call | solution.py:220
  76.5 0.6 collective-permute-start.12
  77.2 10.2 %collective-permute-start.17 = (bf16[4,256,512]{2,1,0:T(8,128)(2,1)}, bf16[4,256,512]{2,1,0:T(8,128)(2,1)S(1)}, u32[]{:S(2)}, u32[]{:S(2)}) collective-permute-start(bf16[4,256,512]{2,1,0:T(8,128)(2,1)} %pad_maximum_fusion.1), channel_id=1, source_target_pairs={{0,0},{1,64},{2,2},{3,66},{4,4},{5,68},{6,6},{7,70},{8,8},{9,72},{... | collective-permute-start | bytes 3145736 | tf_op jit(solution)/shard_map/ppermute | solution.py:146
  87.6 1.0 copy-done.1
  88.6 1.0 copy-done.3
  89.7 9.3 %product.5 = (f32[2,256,512]{2,1,0:T(8,128)S(1)}, bf16[2,256,512]{2,1,0:T(8,128)(2,1)}, bf16[2,256,512]{2,1,0:T(8,128)(2,1)}, bf16[2,256,512]{2,1,0:T(8,128)(2,1)}) custom-call(s32[8]{0:T(128)S(1)} %stack.135.order_ref, s32[8]{0:T(128)S(1)} %stack.156.place_ref, bf16[16,256,2048]{2,1,0:T(8,128)(2,1)} %bitcast.89, bf16[16,256,2048]{2,1,0:T(8,128)(2,1)} %bitcast.90, ...), custom_call_target="tpu_custom_call" | custom-call | flops 4294967296 | bytes 10485760 | tf_op jit(solution)/shard_map/product/pallas_call | solution.py:220
  98.9 7.2 %collective-permute-done.18.refs_3_ = bf16[4,256,512]{2,1,0:T(8,128)(2,1)S(1)} collective-permute-done((bf16[4,256,512]{2,1,0:T(8,128)(2,1)}, bf16[4,256,512]{2,1,0:T(8,128)(2,1)S(1)}, u32[]{:S(2)}, u32[]{:S(2)}) %collective-permute-start.18) | collective-permute-done | bytes 1048608 | tf_op jit(solution)/shard_map/ppermute | solution.py:146
  106.2 2.8 %collective-permute-done.17.refs_2_ = bf16[4,256,512]{2,1,0:T(8,128)(2,1)S(1)} collective-permute-done((bf16[4,256,512]{2,1,0:T(8,128)(2,1)}, bf16[4,256,512]{2,1,0:T(8,128)(2,1)S(1)}, u32[]{:S(2)}, u32[]{:S(2)}) %collective-permute-start.17) | collective-permute-done | bytes 1048608 | tf_op jit(solution)/shard_map/ppermute | solution.py:146
  109.0 8.7 %product.6 = bf16[8,256,512]{2,1,0:T(8,128)(2,1)} custom-call(s32[8]{0:T(128)S(1)} %broadcast_xor_fusion.order_ref, s32[8]{0:T(128)S(1)} %stack.165.place_ref, bf16[16,256,2048]{2,1,0:T(8,128)(2,1)} %bitcast.91, bf16[16,256,2048]{2,1,0:T(8,128)(2,1)} %bitcast.92, bf16[4,256,512]{2,1,0:T(8,128)(2,1)S(1)} %collective-permute-done.17.refs_2_, ...), custom_call_target="tpu_custom_call" | custom-call | flops 4294967296 | bytes 10485760 | tf_op jit(solution)/shard_map/product/pallas_call | solution.py:220
  117.7 3.2 %collective-permute-start.14 = (bf16[2,256,512]{2,1,0:T(8,128)(2,1)}, bf16[2,256,512]{2,1,0:T(8,128)(2,1)}, u32[]{:S(2)}, u32[]{:S(2)}) collective-permute-start(bf16[2,256,512]{2,1,0:T(8,128)(2,1)} %get-tuple-element.22), channel_id=1, source_target_pairs={{0,4},{1,5},{2,6},{3,7},{4,0},{5,1},{6,2},{7,3},{8,12},{9,13},{10,... | collective-permute-start | bytes 1572872 | tf_op jit(solution)/shard_map/ppermute | solution.py:146
  121.1 1.6 copy-done.10
  122.7 8.4 %eliminate.5.in_ref = f32[2,512,512]{2,1,0:T(8,128)S(1)} custom-call(f32[2,512,512]{2,1,0:T(8,128)S(1)} %copy-done.10, s32[2,512]{1,0:T(2,128)S(1)} %copy-done.8), custom_call_target="tpu_custom_call" | custom-call | flops 5000000000 | bytes 4194304 | tf_op jit(solution)/shard_map/eliminate/pallas_call | solution.py:119
  131.1 1.1 collective-permute-done.13
  132.2 11.9 %collective-permute-done.14 = bf16[2,256,512]{2,1,0:T(8,128)(2,1)} collective-permute-done((bf16[2,256,512]{2,1,0:T(8,128)(2,1)}, bf16[2,256,512]{2,1,0:T(8,128)(2,1)}, u32[]{:S(2)}, u32[]{:S(2)}) %collective-permute-start.14) | collective-permute-done | bytes 524320 | tf_op jit(solution)/shard_map/ppermute | solution.py:146
  144.1 1.5 convert_add_fusion.2
  145.6 1.1 collective-permute-start.16
  146.7 8.2 %product.7 = (f32[2,256,512]{2,1,0:T(8,128)S(1)}, bf16[2,256,512]{2,1,0:T(8,128)(2,1)S(1)}, bf16[2,256,512]{2,1,0:T(8,128)(2,1)S(1)}, bf16[2,256,512]{2,1,0:T(8,128)(2,1)S(1)}) custom-call(s32[8]{0:T(128)S(1)} %stack.135.order_ref, s32[8]{0:T(128)S(1)} %stack.165.place_ref, bf16[16,256,2048]{2,1,0:T(8,128)(2,1)} %bitcast.93, ...), custom_call_target="tpu_custom_call" | custom-call | flops 4294967296 | bytes 10485760 | tf_op jit(solution)/shard_map/product/pallas_call | solution.py:220
  154.8 2.3 collective-permute-start.20
  157.1 2.3 collective-permute-start.21
  159.6 8.4 %eliminate.6.in_ref = f32[2,512,512]{2,1,0:T(8,128)S(1)} custom-call(f32[2,512,512]{2,1,0:T(8,128)S(1)} %eliminate.5.in_ref, s32[2,512]{1,0:T(2,128)S(1)} %copy-done.8), custom_call_target="tpu_custom_call" | custom-call | flops 5000000000 | bytes 4194304 | tf_op jit(solution)/shard_map/eliminate/pallas_call | solution.py:119
  168.0 8.4 %eliminate.7 = f32[2,512,512]{2,1,0:T(8,128)S(1)} custom-call(f32[2,512,512]{2,1,0:T(8,128)S(1)} %eliminate.6.in_ref, s32[2,512]{1,0:T(2,128)S(1)} %copy-done.8), custom_call_target="tpu_custom_call" | custom-call | flops 5000000000 | bytes 4194304 | tf_op jit(solution)/shard_map/eliminate/pallas_call | solution.py:119
  176.4 5.5 %collective-permute-done.21 = bf16[2,256,512]{2,1,0:T(8,128)(2,1)S(1)} collective-permute-done((bf16[2,256,512]{2,1,0:T(8,128)(2,1)S(1)}, bf16[2,256,512]{2,1,0:T(8,128)(2,1)S(1)}, u32[]{:S(2)}, u32[]{:S(2)}) %collective-permute-start.21) | collective-permute-done | bytes 524320 | tf_op jit(solution)/shard_map/ppermute | solution.py:146
  181.9 0.3 convert_add_fusion.1
  182.2 0.5 collective-permute-start.23
  182.9 0.7 convolution_convert_fusion.1
  183.7 1.1 fusion.5
  184.8 0.7 fusion.32
  185.4 0.7 convolution_convert_fusion
  186.1 2.4 %collective-permute-done.23 = bf16[256,512]{1,0:T(8,128)(2,1)S(1)} collective-permute-done((bf16[256,512]{1,0:T(8,128)(2,1)S(1)}, bf16[256,512]{1,0:T(8,128)(2,1)S(1)}, u32[]{:S(2)}, u32[]{:S(2)}) %collective-permute-start.23) | collective-permute-done | bytes 262176 | tf_op jit(solution)/shard_map/ppermute | solution.py:146
  188.5 1.1 fusion.2
  189.6 0.7 broadcast_select_fusion.2
  190.3 2.6 %collective-permute-start.24 = (f32[512,512]{1,0:T(8,128)S(1)}, f32[512,512]{1,0:T(8,128)S(1)}, u32[]{:S(2)}, u32[]{:S(2)}) collective-permute-start(f32[512,512]{1,0:T(8,128)S(1)} %get-tuple-element.42), channel_id=1, source_target_pairs={{0,1},{1,0},{2,3},{3,2},{4,5},{5,4},{6,7},{7,6},{8,9},{9,8},{10,11... | collective-permute-start | bytes 3145736 | tf_op jit(solution)/shard_map/ppermute | solution.py:146
  192.9 2.3 collective-permute-done.24
  195.2 0.4 fusion.11
  195.6 20.8 %all_to_all.10 = bf16[64,8,512]{2,1,0:T(8,128)(2,1)} all-to-all(bf16[64,8,512]{2,1,0:T(8,128)(2,1)S(1)} %fusion.11), channel_id=1, replica_groups=mesh['z_hi'=2,'x'=4,'z_lo'=2,'y'=4,'core'=2] {'z_hi','x','z_lo','y'}, dimensions={0} | all-to-all | bytes 1048576 | tf_op jit(solution)/shard_map/all_to_all | solution.py:247
  216.3 1.1 reduce_sum.12
  217.5 15.8 %all_to_all.11 = bf16[64,8,512]{2,1,0:T(8,128)(2,1)S(1)} all-to-all(bf16[64,8,512]{2,1,0:T(8,128)(2,1)S(1)} %broadcast_in_dim.36), channel_id=1, replica_groups=mesh['z_hi'=2,'x'=4,'z_lo'=2,'y'=4,'core'=2] {'z_hi','x','z_lo','y'}, dimensions={0} | all-to-all | bytes 1048576 | tf_op jit(solution)/shard_map/all_to_all | solution.py:249
  233.3 3.3 %collective-permute-start.25 = (bf16[512,512]{1,0:T(8,128)(2,1)S(1)}, bf16[512,512]{1,0:T(8,128)(2,1)S(1)}, u32[]{:S(2)}, u32[]{:S(2)}) collective-permute-start(bf16[512,512]{1,0:T(8,128)(2,1)S(1)} %bitcast.98), channel_id=1, source_target_pairs={{0,1},{1,0},{2,3},{3,2},{4,5},{5,4},{6,7},{7,6},{8,9},{9,8},{10,11... | collective-permute-start | bytes 1572872 | tf_op jit(solution)/shard_map/ppermute | solution.py:146
  236.7 0.9 fusion
  237.6 0.6 collective-permute-done.25
  238.3 1.7 convert_add_fusion
  (50 shorter events, 1.6 us)
Async XLA Ops:
  2.6 11.5 %collective-permute-start = (bf16[256,512]{1,0:T(8,128)(2,1)S(1)}, bf16[256,512]{1,0:T(8,128)(2,1)S(1)}, u32[]{:S(2)}, u32[]{:S(2)}) collective-permute-start(bf16[256,512]{1,0:T(8,128)(2,1)S(1)} %get-tuple-element.41), channel_id=1, source_target_pairs={{0,0},{1,1},{2,2},{3,3},{4,4},{5,5},{6,6},{7,7},{8,64},{9,65},{10,... | collective-permute-start | bytes 786440 | tf_op jit(solution)/shard_map/ppermute | solution.py:146
  3.3 26.9 %collective-permute-start.5 = (bf16[256,512]{1,0:T(8,128)(2,1)S(1)}, bf16[256,512]{1,0:T(8,128)(2,1)S(1)}, u32[]{:S(2)}, u32[]{:S(2)}) collective-permute-start(bf16[256,512]{1,0:T(8,128)(2,1)S(1)} %get-tuple-element.40), channel_id=1, source_target_pairs={{0,64},{1,80},{2,96},{3,112},{4,0},{5,16},{6,32},{7,48},{8,65},{9,... | collective-permute-start | bytes 786440 | tf_op jit(solution)/shard_map/ppermute | solution.py:146
  10.6 19.6 %collective-permute-start.4 = (bf16[256,512]{1,0:T(8,128)(2,1)S(1)}, bf16[256,512]{1,0:T(8,128)(2,1)S(1)}, u32[]{:S(2)}, u32[]{:S(2)}) collective-permute-start(bf16[256,512]{1,0:T(8,128)(2,1)S(1)} %get-tuple-element.40), channel_id=1, source_target_pairs={{0,0},{1,16},{2,32},{3,48},{4,64},{5,80},{6,96},{7,112},{8,1},{9,1... | collective-permute-start | bytes 786440 | tf_op jit(solution)/shard_map/ppermute | solution.py:146
  14.0 16.2 %collective-permute-start.3 = (bf16[256,512]{1,0:T(8,128)(2,1)S(1)}, bf16[256,512]{1,0:T(8,128)(2,1)S(1)}, u32[]{:S(2)}, u32[]{:S(2)}) collective-permute-start(bf16[256,512]{1,0:T(8,128)(2,1)S(1)} %collective-permute-done), channel_id=1, source_target_pairs={{0,48},{1,49},{2,50},{3,51},{4,52},{5,53},{6,54},{7,55},{8,56},{9,... | collective-permute-start | bytes 786440 | tf_op jit(solution)/shard_map/ppermute | solution.py:146
  17.4 12.8 %collective-permute-start.2 = (bf16[256,512]{1,0:T(8,128)(2,1)S(1)}, bf16[256,512]{1,0:T(8,128)(2,1)S(1)}, u32[]{:S(2)}, u32[]{:S(2)}) collective-permute-start(bf16[256,512]{1,0:T(8,128)(2,1)S(1)} %collective-permute-done), channel_id=1, source_target_pairs={{0,32},{1,33},{2,34},{3,35},{4,36},{5,37},{6,38},{7,39},{8,40},{9,... | collective-permute-start | bytes 786440 | tf_op jit(solution)/shard_map/ppermute | solution.py:146
  17.4 16.4 %collective-permute-start.1 = (bf16[256,512]{1,0:T(8,128)(2,1)S(1)}, bf16[256,512]{1,0:T(8,128)(2,1)S(1)}, u32[]{:S(2)}, u32[]{:S(2)}) collective-permute-start(bf16[256,512]{1,0:T(8,128)(2,1)S(1)} %collective-permute-done), channel_id=1, source_target_pairs={{0,16},{1,17},{2,18},{3,19},{4,20},{5,21},{6,22},{7,23},{8,24},{9,... | collective-permute-start | bytes 786440 | tf_op jit(solution)/shard_map/ppermute | solution.py:146
  18.1 1.6 copy-start.6
  19.7 0.7 copy-start.7
  28.9 1.3 copy-start.9
  34.0 8.4 %collective-permute-start.8 = (bf16[256,512]{1,0:T(8,128)(2,1)S(1)}, bf16[256,512]{1,0:T(8,128)(2,1)S(1)}, u32[]{:S(2)}, u32[]{:S(2)}) collective-permute-start(bf16[256,512]{1,0:T(8,128)(2,1)S(1)} %get-tuple-element.37), channel_id=1, source_target_pairs={{0,6},{1,7},{2,0},{3,1},{4,2},{5,3},{6,4},{7,5},{8,14},{9,15},{10,... | collective-permute-start | bytes 786440 | tf_op jit(solution)/shard_map/ppermute | solution.py:146
  36.4 10.3 %collective-permute-start.7 = (bf16[256,512]{1,0:T(8,128)(2,1)S(1)}, bf16[256,512]{1,0:T(8,128)(2,1)S(1)}, u32[]{:S(2)}, u32[]{:S(2)}) collective-permute-start(bf16[256,512]{1,0:T(8,128)(2,1)S(1)} %get-tuple-element.38), channel_id=1, source_target_pairs={{0,4},{1,5},{2,6},{3,7},{4,0},{5,1},{6,2},{7,3},{8,12},{9,13},{10,... | collective-permute-start | bytes 786440 | tf_op jit(solution)/shard_map/ppermute | solution.py:146
  38.1 12.6 %collective-permute-start.6 = (bf16[256,512]{1,0:T(8,128)(2,1)S(1)}, bf16[256,512]{1,0:T(8,128)(2,1)}, u32[]{:S(2)}, u32[]{:S(2)}) collective-permute-start(bf16[256,512]{1,0:T(8,128)(2,1)S(1)} %get-tuple-element.39), channel_id=1, source_target_pairs={{0,2},{1,3},{2,4},{3,5},{4,6},{5,7},{6,0},{7,1},{8,10},{9,11},{10,... | collective-permute-start | bytes 786440 | tf_op jit(solution)/shard_map/ppermute | solution.py:146
  38.4 25.2 %collective-permute-start.11 = (bf16[2,256,512]{2,1,0:T(8,128)(2,1)S(1)}, bf16[2,256,512]{2,1,0:T(8,128)(2,1)S(1)}, u32[]{:S(2)}, u32[]{:S(2)}) collective-permute-start(bf16[2,256,512]{2,1,0:T(8,128)(2,1)S(1)} %pad_maximum_fusion.3.refs_2_), channel_id=1, source_target_pairs={{0,48},{1,49},{2,50},{3,51},{4,52},{5,53},{6,54},{7,55},{8,56},{9,... | collective-permute-start | bytes 1572872 | tf_op jit(solution)/shard_map/ppermute | solution.py:146
  41.2 22.4 %collective-permute-start.10 = (bf16[2,256,512]{2,1,0:T(8,128)(2,1)S(1)}, bf16[2,256,512]{2,1,0:T(8,128)(2,1)S(1)}, u32[]{:S(2)}, u32[]{:S(2)}) collective-permute-start(bf16[2,256,512]{2,1,0:T(8,128)(2,1)S(1)} %pad_maximum_fusion.3.refs_2_), channel_id=1, source_target_pairs={{0,32},{1,33},{2,34},{3,35},{4,36},{5,37},{6,38},{7,39},{8,40},{9,... | collective-permute-start | bytes 1572872 | tf_op jit(solution)/shard_map/ppermute | solution.py:146
  42.5 25.4 %collective-permute-start.9 = (bf16[2,256,512]{2,1,0:T(8,128)(2,1)S(1)}, bf16[2,256,512]{2,1,0:T(8,128)(2,1)S(1)}, u32[]{:S(2)}, u32[]{:S(2)}) collective-permute-start(bf16[2,256,512]{2,1,0:T(8,128)(2,1)S(1)} %pad_maximum_fusion.3.refs_2_), channel_id=1, source_target_pairs={{0,16},{1,17},{2,18},{3,19},{4,20},{5,21},{6,22},{7,23},{8,24},{9,... | collective-permute-start | bytes 1572872 | tf_op jit(solution)/shard_map/ppermute | solution.py:146
  63.6 12.9 %copy-start = (bf16[2,256,512]{2,1,0:T(8,128)(2,1)}, bf16[2,256,512]{2,1,0:T(8,128)(2,1)S(1)}, u32[]{:S(2)}) copy-start(bf16[2,256,512]{2,1,0:T(8,128)(2,1)S(1)} %collective-permute-done.10.refs_4_) | copy-start | bytes 1572868
  67.8 8.7 %copy-start.2 = (bf16[2,256,512]{2,1,0:T(8,128)(2,1)}, bf16[2,256,512]{2,1,0:T(8,128)(2,1)S(1)}, u32[]{:S(2)}) copy-start(bf16[2,256,512]{2,1,0:T(8,128)(2,1)S(1)} %collective-permute-done.9.refs_3_) | copy-start | bytes 1572868
  76.5 11.1 %collective-permute-start.12 = (bf16[8,256,512]{2,1,0:T(8,128)(2,1)}, bf16[8,256,512]{2,1,0:T(8,128)(2,1)}, u32[]{:S(2)}, u32[]{:S(2)}) collective-permute-start(bf16[8,256,512]{2,1,0:T(8,128)(2,1)} %product.4), channel_id=1, source_target_pairs={{0,1},{1,0},{2,3},{3,2},{4,5},{5,4},{6,7},{7,6},{8,9},{9,8},{10,11... | collective-permute-start | bytes 6291464 | tf_op jit(solution)/shard_map/ppermute | solution.py:146
  77.1 29.1 %collective-permute-start.18 = (bf16[4,256,512]{2,1,0:T(8,128)(2,1)}, bf16[4,256,512]{2,1,0:T(8,128)(2,1)S(1)}, u32[]{:S(2)}, u32[]{:S(2)}) collective-permute-start(bf16[4,256,512]{2,1,0:T(8,128)(2,1)} %pad_maximum_fusion.1), channel_id=1, source_target_pairs={{0,64},{1,0},{2,66},{3,2},{4,68},{5,4},{6,70},{7,6},{8,72},{9,8},{... | collective-permute-start | bytes 3145736 | tf_op jit(solution)/shard_map/ppermute | solution.py:146
  77.2 31.8 %collective-permute-start.17 = (bf16[4,256,512]{2,1,0:T(8,128)(2,1)}, bf16[4,256,512]{2,1,0:T(8,128)(2,1)S(1)}, u32[]{:S(2)}, u32[]{:S(2)}) collective-permute-start(bf16[4,256,512]{2,1,0:T(8,128)(2,1)} %pad_maximum_fusion.1), channel_id=1, source_target_pairs={{0,0},{1,64},{2,2},{3,66},{4,4},{5,68},{6,6},{7,70},{8,8},{9,72},{... | collective-permute-start | bytes 3145736 | tf_op jit(solution)/shard_map/ppermute | solution.py:146
  87.6 1.0 copy-start.1
  88.6 1.0 copy-start.3
  98.9 18.7 %copy-start.4 = (f32[2,256,512]{2,1,0:T(8,128)}, f32[2,256,512]{2,1,0:T(8,128)S(1)}, u32[]{:S(2)}) copy-start(f32[2,256,512]{2,1,0:T(8,128)S(1)} %get-tuple-element.20) | copy-start | bytes 3145732
  98.9 22.2 %copy-start.8 = (s32[2,512]{1,0:T(2,128)S(1)}, s32[2,512]{1,0:T(2,128)}, u32[]{:S(2)}) copy-start(s32[2,512]{1,0:T(2,128)} %flag_ref.7) | copy-start | bytes 12292
  117.7 29.0 %collective-permute-start.19 = (bf16[8,256,512]{2,1,0:T(8,128)(2,1)}, bf16[8,256,512]{2,1,0:T(8,128)(2,1)}, u32[]{:S(2)}, u32[]{:S(2)}) collective-permute-start(bf16[8,256,512]{2,1,0:T(8,128)(2,1)} %product.6), channel_id=1, source_target_pairs={{0,1},{1,0},{2,3},{3,2},{4,5},{5,4},{6,7},{7,6},{8,9},{9,8},{10,11... | collective-permute-start | bytes 6291464 | tf_op jit(solution)/shard_map/ppermute | solution.py:146
  117.7 14.5 %collective-permute-start.13 = (bf16[2,256,512]{2,1,0:T(8,128)(2,1)}, bf16[2,256,512]{2,1,0:T(8,128)(2,1)S(1)}, u32[]{:S(2)}, u32[]{:S(2)}) collective-permute-start(bf16[2,256,512]{2,1,0:T(8,128)(2,1)} %get-tuple-element.21), channel_id=1, source_target_pairs={{0,2},{1,3},{2,4},{3,5},{4,6},{5,7},{6,0},{7,1},{8,10},{9,11},{10,... | collective-permute-start | bytes 1572872 | tf_op jit(solution)/shard_map/ppermute | solution.py:146
  117.7 26.3 %collective-permute-start.14 = (bf16[2,256,512]{2,1,0:T(8,128)(2,1)}, bf16[2,256,512]{2,1,0:T(8,128)(2,1)}, u32[]{:S(2)}, u32[]{:S(2)}) collective-permute-start(bf16[2,256,512]{2,1,0:T(8,128)(2,1)} %get-tuple-element.22), channel_id=1, source_target_pairs={{0,4},{1,5},{2,6},{3,7},{4,0},{5,1},{6,2},{7,3},{8,12},{9,13},{10,... | collective-permute-start | bytes 1572872 | tf_op jit(solution)/shard_map/ppermute | solution.py:146
  120.9 23.1 %collective-permute-start.15 = (bf16[2,256,512]{2,1,0:T(8,128)(2,1)}, bf16[2,256,512]{2,1,0:T(8,128)(2,1)}, u32[]{:S(2)}, u32[]{:S(2)}) collective-permute-start(bf16[2,256,512]{2,1,0:T(8,128)(2,1)} %get-tuple-element.23), channel_id=1, source_target_pairs={{0,6},{1,7},{2,0},{3,1},{4,2},{5,3},{6,4},{7,5},{8,14},{9,15},{10,... | collective-permute-start | bytes 1572872 | tf_op jit(solution)/shard_map/ppermute | solution.py:146
  121.1 1.6 copy-start.10
  122.7 21.4 %copy-start.5 = (f32[2,256,512]{2,1,0:T(8,128)S(1)}, f32[2,256,512]{2,1,0:T(8,128)}, u32[]{:S(2)}) copy-start(f32[2,256,512]{2,1,0:T(8,128)} %copy-done.4) | copy-start | bytes 3145732
  145.6 38.1 %collective-permute-start.16 = (bf16[256,512]{1,0:T(8,128)(2,1)S(1)}, bf16[256,512]{1,0:T(8,128)(2,1)S(1)}, u32[]{:S(2)}, u32[]{:S(2)}) collective-permute-start(bf16[256,512]{1,0:T(8,128)(2,1)S(1)} %fusion.18), channel_id=1, source_target_pairs={{0,8},{1,9},{2,10},{3,11},{4,12},{5,13},{6,14},{7,15},{8,0},{9,1},... | collective-permute-start | bytes 786440 | tf_op jit(solution)/shard_map/ppermute | solution.py:146
  154.8 21.6 %collective-permute-start.20 = (bf16[2,256,512]{2,1,0:T(8,128)(2,1)S(1)}, bf16[2,256,512]{2,1,0:T(8,128)(2,1)S(1)}, u32[]{:S(2)}, u32[]{:S(2)}) collective-permute-start(bf16[2,256,512]{2,1,0:T(8,128)(2,1)S(1)} %get-tuple-element.26), channel_id=1, source_target_pairs={{0,2},{1,3},{2,4},{3,5},{4,6},{5,7},{6,0},{7,1},{8,10},{9,11},{10,... | collective-permute-start | bytes 1572872 | tf_op jit(solution)/shard_map/ppermute | solution.py:146
  157.1 24.8 %collective-permute-start.21 = (bf16[2,256,512]{2,1,0:T(8,128)(2,1)S(1)}, bf16[2,256,512]{2,1,0:T(8,128)(2,1)S(1)}, u32[]{:S(2)}, u32[]{:S(2)}) collective-permute-start(bf16[2,256,512]{2,1,0:T(8,128)(2,1)S(1)} %get-tuple-element.27), channel_id=1, source_target_pairs={{0,4},{1,5},{2,6},{3,7},{4,0},{5,1},{6,2},{7,3},{8,12},{9,13},{10,... | collective-permute-start | bytes 1572872 | tf_op jit(solution)/shard_map/ppermute | solution.py:146
  159.4 22.5 %collective-permute-start.22 = (bf16[2,256,512]{2,1,0:T(8,128)(2,1)S(1)}, bf16[2,256,512]{2,1,0:T(8,128)(2,1)S(1)}, u32[]{:S(2)}, u32[]{:S(2)}) collective-permute-start(bf16[2,256,512]{2,1,0:T(8,128)(2,1)S(1)} %get-tuple-element.28), channel_id=1, source_target_pairs={{0,6},{1,7},{2,0},{3,1},{4,2},{5,3},{6,4},{7,5},{8,14},{9,15},{10,... | collective-permute-start | bytes 1572872 | tf_op jit(solution)/shard_map/ppermute | solution.py:146
  181.9 1.0 copy-start.11
  182.2 6.3 %collective-permute-start.23 = (bf16[256,512]{1,0:T(8,128)(2,1)S(1)}, bf16[256,512]{1,0:T(8,128)(2,1)S(1)}, u32[]{:S(2)}, u32[]{:S(2)}) collective-permute-start(bf16[256,512]{1,0:T(8,128)(2,1)S(1)} %fusion.19), channel_id=1, source_target_pairs={{0,8},{1,9},{2,10},{3,11},{4,12},{5,13},{6,14},{7,15},{8,0},{9,1},... | collective-permute-start | bytes 786440 | tf_op jit(solution)/shard_map/ppermute | solution.py:146
  190.3 4.9 %collective-permute-start.24 = (f32[512,512]{1,0:T(8,128)S(1)}, f32[512,512]{1,0:T(8,128)S(1)}, u32[]{:S(2)}, u32[]{:S(2)}) collective-permute-start(f32[512,512]{1,0:T(8,128)S(1)} %get-tuple-element.42), channel_id=1, source_target_pairs={{0,1},{1,0},{2,3},{3,2},{4,5},{5,4},{6,7},{7,6},{8,9},{9,8},{10,11... | collective-permute-start | bytes 3145736 | tf_op jit(solution)/shard_map/ppermute | solution.py:146
  233.3 4.9 %collective-permute-start.25 = (bf16[512,512]{1,0:T(8,128)(2,1)S(1)}, bf16[512,512]{1,0:T(8,128)(2,1)S(1)}, u32[]{:S(2)}, u32[]{:S(2)}) collective-permute-start(bf16[512,512]{1,0:T(8,128)(2,1)S(1)} %bitcast.98), channel_id=1, source_target_pairs={{0,1},{1,0},{2,3},{3,2},{4,5},{5,4},{6,7},{7,6},{8,9},{9,8},{10,11... | collective-permute-start | bytes 1572872 | tf_op jit(solution)/shard_map/ppermute | solution.py:146
